TPU v7x, 128 devices: a whole 4x4x4 slice. The times are simulated.
128 devices in a mesh: bond: 32 (over x, z_lo, y), outer: 4 (over z_hi, core).
Axes of the slice: x: 4, y: 4, z: 4 (z_hi: 2, z_lo: 2; z = z_hi * 2 + z_lo), core: 2. Of those that a mesh axis runs over, the one named last changes fastest.
Arguments:
- upper: bfloat16 [128, 128, 128], P(None, 'bond'), may hold values from -4 to 4
- lower: bfloat16 [128, 128, 8, 128], P(None, 'bond', 'outer'), may hold values from -4 to 4
- isometry: bfloat16 [16384, 128], P(('bond', 'outer')), may hold values from -0.046875 to 0.046875
Outputs:
- coarse: float32 [128, 8, 128], P('bond', 'outer')
All inputs are finite; a program needn't handle non-finite values.
Results may differ from a plain program's by a relative error of at most 0.004.
Values may be sent and summed in bfloat16 or wider, within the bound.
No kernel may reach another device: no remote copies, remote signals or barrier semaphores. Data moves between devices by JAX's collectives and lax.ppermute only.
A program may use at most 64 MiB of HBM per device.

v0:
```python
import jax
import jax.numpy as jnp
from jax import lax
from jax.experimental import pallas as pl
from jax.experimental.pallas import tpu as pltpu
from jax.sharding import Mesh, PartitionSpec as P

SIZES = (4, 2, 4, 2, 2)
NAMES = ("x", "zl", "y", "zh", "c")
BF16 = jnp.bfloat16
F32 = jnp.float32


def swapped(value, axis):
    return lax.ppermute(value, axis, [(0, 1), (1, 0)])


def both_swapped(value):
    return lax.ppermute(value, ("zl", "zh"), [(i, 3 - i) for i in range(4)])


def mm(a, b):
    return lax.dot_general(a, b, (((1,), (0,)), ((), ())), preferred_element_type=F32)


QB = 4


def step_kernel(zh_ref, w_ref, u_ref, wr_ref, l00, l01, l10, l11, acc_ref, out_ref, wt, lower):
    for k in range(8):
        wt[k * 128 : (k + 1) * 128, :] = w_ref[k].T
    for zk, refs in enumerate(((l00, l01), (l10, l11))):
        for zd, ref in enumerate(refs):
            for j in range(4):
                for e in range(2):
                    row, col = (zk * 4 + j) * 128, (zd * 2 + e) * 128
                    lower[row : row + 128, col : col + 128] = ref[j, e]

    for at in range(0, u_ref.shape[0], QB):
        u = jnp.concatenate([u_ref[at + q] for q in range(QB)], axis=1)
        joined = mm(wt[...], u).astype(BF16)
        left = jnp.concatenate(
            [
                jnp.concatenate(
                    [
                        joined[k * 128 : (k + 1) * 128, q * 128 : (q + 1) * 128]
                        for k in range(8)
                    ],
                    axis=1,
                )
                for q in range(QB)
            ],
            axis=0,
        )
        paired = mm(left, lower[...]).astype(BF16)
        rows = jnp.concatenate(
            [
                jnp.concatenate(
                    [
                        paired[q * 128 : (q + 1) * 128, d * 128 : (d + 1) * 128]
                        for q in range(QB)
                    ],
                    axis=1,
                )
                for d in range(4)
            ],
            axis=0,
        )
        part = mm(rows, wr_ref[at : at + QB].reshape(QB * 128, 128))
        part = part.reshape(2, 2, 128, 128)
        for zd in range(2):
            to = zh_ref[0] if zd == 0 else 1 - zh_ref[0]
            if at > 0:
                out_ref[to] += part[zd]
            elif acc_ref is None:
                out_ref[to] = part[zd]
            else:
                out_ref[to] = acc_ref[to] + part[zd]


def contract(zh, w, u, wr, lowers, acc):
    vmem = pl.BlockSpec(memory_space=pltpu.VMEM)
    body = step_kernel
    args = [zh, w, u, wr, *lowers]
    if acc is None:

        def body(*refs):
            step_kernel(*refs[:8], None, *refs[8:])
    else:
        args.append(acc)

    return pl.pallas_call(
        body,
        in_specs=[pl.BlockSpec(memory_space=pltpu.SMEM)] + [vmem] * (len(args) - 1),
        out_specs=vmem,
        out_shape=jax.ShapeDtypeStruct((2, 2, 128, 128), F32),
        scratch_shapes=[pltpu.VMEM((1024, 128), BF16), pltpu.VMEM((1024, 512), BF16)],
        compiler_params=pltpu.CompilerParams(vmem_limit_bytes=40 * 1024 * 1024),
        cost_estimate=pl.CostEstimate(
            flops=4 * 10**9, bytes_accessed=4 * 2**20, transcendentals=0
        ),
        name="contract",
    )(*args)


def on_device(upper, lower, isometry):
    zl = lax.axis_index("zl")
    zh = lax.axis_index("zh")
    c = lax.axis_index("c")

    t = jnp.arange(32)
    plane = jnp.where(t < 16, zl, 1 - zl)
    xy = t % 16
    wanted = 4 * ((xy // 4) * 8 + plane * 4 + xy % 4) + 2 * zh + c
    pick = (wanted[:, None] == jnp.arange(128)[None, :]).astype(BF16)
    rights = jnp.einsum(
        "qr,mlr->qlm", pick, upper, preferred_element_type=F32
    ).astype(BF16)
    mine, theirs = rights[:16], swapped(rights[16:], "zl")

    ks = isometry.reshape(4, 2, 4, 4, 128).transpose(0, 2, 1, 3, 4)
    ks = jnp.broadcast_to(ks.reshape(16, 1, 8, 128), (16, 8, 8, 128)).reshape(128, 8, 128)
    w = lax.all_to_all(ks, ("x", "y", "zl", "zh", "c"), 0, 0, tiled=True)

    l00 = lower.transpose(1, 2, 0, 3)
    l01 = swapped(l00, "zh")
    l10 = swapped(l00, "zl")
    l11 = both_swapped(l00)
    lowers = (l00, l01, l10, l11)

    first = jnp.where(zl == 0, mine, theirs)
    second = jnp.where(zl == 0, theirs, mine)
    rights = jnp.concatenate([first, second], axis=1)
    send = jnp.concatenate([rights.reshape(128, 128), isometry], axis=0)
    send, w, *lowers = lax.optimization_barrier((send, w, *lowers))
    send = jnp.broadcast_to(send[None], (16, 256, 128))
    got = lax.all_to_all(send, ("x", "y"), 0, 0, tiled=True)
    w = w.transpose(1, 0, 2).reshape(2, 4, 128, 128)
    w = jnp.where(zl == 0, w, w[::-1]).reshape(8, 128, 128)
    u = got[:, :128].reshape(16, 16, 8, 128).transpose(1, 0, 2, 3).reshape(16, 128, 128)
    wr = got[:, 128:]
    u_other, wr_other = swapped(u, "c"), swapped(wr, "c")

    at = zh.astype(jnp.int32)[None]
    acc = contract(at, w, u, wr, lowers, None)
    acc = contract(at, w, u_other, wr_other, lowers, acc)

    parts = acc.reshape(2, 2, 32, 4, 128).transpose(2, 0, 1, 3, 4).reshape(64, 8, 128)
    parts = lax.all_to_all(parts, ("x", "zl", "y", "zh"), 0, 0, tiled=True)
    return jnp.sum(parts, axis=0).reshape(2, 4, 128).transpose(1, 0, 2)


def solution(mesh):
    return jax.shard_map(
        on_device,
        mesh=Mesh(mesh.devices.reshape(SIZES), NAMES),
        in_specs=(
            P(None, ("x", "zl", "y"), None),
            P(None, ("x", "zl", "y"), ("zh", "c"), None),
            P(NAMES, None),
        ),
        out_specs=P(("x", "zl", "y"), ("zh", "c"), None),
        check_vma=False,
    )
```

profile of v0, /device:TPU:0, one launch (start us, length us, event | category | flops | bytes accessed | tf_op | source)
XLA Modules:
  0.0 78.5 jit_solution(2460019456665678316)
XLA Ops:
  0.0 0.0 copy-start
  0.0 0.9 %copy-done = bf16[128,4,128]{2,1,0:T(4,128)(2,1)S(1)} copy-done((bf16[128,4,128]{2,1,0:T(4,128)(2,1)S(1)}, bf16[128,4,128]{2,1,0:T(4,128)(2,1)}, u32[]{:S(2)}) %copy-start) | copy-done | bytes 131096
  0.9 0.2 fusion
  1.1 0.0 copy-start.1
  1.1 2.1 %collective-permute-start = (bf16[16,4,128]{2,0,1:T(8,128)(2,1)S(1)}, bf16[16,4,128]{2,0,1:T(8,128)(2,1)S(1)}, u32[]{:S(2)}, u32[]{:S(2)}) collective-permute-start(bf16[16,4,128]{2,0,1:T(8,128)(2,1)S(1)} %slice.17), channel_id=1, source_target_pairs={{0,16},{16,0},{1,17},{17,1},{2,18},{18,2},{3,19},{19,3},{4,20},{20... | collective-permute-start | bytes 49160 | tf_op jit(solution)/shard_map/ppermute | solution.py:15
  3.2 1.0 %copy.30 = bf16[128,4,2,128]{3,0,2,1:T(8,128)(2,1)S(1)} copy(bf16[128,4,2,128]{3,2,1,0:T(2,128)(2,1)} %param.4) | data formatting | bytes 524288 | tf_op args[1]
  4.2 2.6 %collective-permute-start.3 = (bf16[4,2,128,128]{3,2,1,0:T(8,128)(2,1)S(1)}, bf16[4,2,128,128]{3,2,1,0:T(8,128)(2,1)S(1)}, u32[]{:S(2)}, u32[]{:S(2)}) collective-permute-start(bf16[4,2,128,128]{3,2,1,0:T(8,128)(2,1)S(1)} %bitcast.39), channel_id=1, source_target_pairs={{0,18},{2,16},{16,2},{18,0},{1,19},{3,17},{17,3},{19,1},{4,22},{6,... | collective-permute-start | bytes 786440 | tf_op jit(solution)/shard_map/ppermute | solution.py:19
  6.8 1.0 %collective-permute-start.2 = (bf16[4,2,128,128]{3,2,1,0:T(8,128)(2,1)S(1)}, bf16[4,2,128,128]{3,2,1,0:T(8,128)(2,1)S(1)}, u32[]{:S(2)}, u32[]{:S(2)}) collective-permute-start(bf16[4,2,128,128]{3,2,1,0:T(8,128)(2,1)S(1)} %bitcast.40), channel_id=1, source_target_pairs={{0,16},{16,0},{1,17},{17,1},{2,18},{18,2},{3,19},{19,3},{4,20},{20... | collective-permute-start | bytes 786440 | tf_op jit(solution)/shard_map/ppermute | solution.py:15
  7.8 1.2 %collective-permute-start.1 = (bf16[4,2,128,128]{3,2,1,0:T(8,128)(2,1)S(1)}, bf16[4,2,128,128]{3,2,1,0:T(8,128)(2,1)S(1)}, u32[]{:S(2)}, u32[]{:S(2)}) collective-permute-start(bf16[4,2,128,128]{3,2,1,0:T(8,128)(2,1)S(1)} %bitcast.41), channel_id=1, source_target_pairs={{0,2},{2,0},{1,3},{3,1},{4,6},{6,4},{5,7},{7,5},{8,10},{10,8},{9,1... | collective-permute-start | bytes 786440 | tf_op jit(solution)/shard_map/ppermute | solution.py:15
  9.0 0.0 copy-done.1
  9.0 0.7 broadcast_in_dim.30
  9.8 9.5 %all-to-all-start = ((bf16[128,8,128]{2,1,0:T(8,128)(2,1)}), bf16[128,8,128]{2,1,0:T(8,128)(2,1)S(1)}, u32[]{:S(2)}, u32[]{:S(2)}) async-start(bf16[128,8,128]{2,1,0:T(8,128)(2,1)} %bitcast.7), calls=%async_computation | async-start | bytes 524288 | tf_op jit(solution)/shard_map/all_to_all | solution.py:123
  19.3 0.0 collective-permute-done
  19.4 10.8 %all-to-all-done = bf16[128,8,128]{2,1,0:T(8,128)(2,1)S(1)} async-done(((bf16[128,8,128]{2,1,0:T(8,128)(2,1)}), bf16[128,8,128]{2,1,0:T(8,128)(2,1)S(1)}, u32[]{:S(2)}, u32[]{:S(2)}) %all-to-all-start) | async-done | bytes 262176 | tf_op jit(solution)/shard_map/all_to_all | solution.py:123
  30.2 0.0 collective-permute-done.3.refs_7_.l11
  30.2 0.0 collective-permute-done.2.refs_6_.l10
  30.2 0.0 collective-permute-done.1.refs_5_.l01
  30.2 1.2 %broadcast_in_dim.31 = bf16[16,256,128]{2,1,0:T(8,128)(2,1)} broadcast(bf16[256,128]{1,0:T(8,128)(2,1)S(1)} %pad_maximum_fusion), dimensions={1,2} | broadcast | bytes 1114112 | tf_op jit(solution)/shard_map/broadcast_in_dim | solution.py:136
  31.4 3.7 %all-to-all-start.1 = ((bf16[16,256,128]{2,1,0:T(8,128)(2,1)}), bf16[16,256,128]{2,1,0:T(8,128)(2,1)S(1)}, u32[]{:S(2)}, u32[]{:S(2)}) async-start(bf16[16,256,128]{2,1,0:T(8,128)(2,1)} %broadcast_in_dim.31), calls=%async_computation.1 | async-start | bytes 2097152 | tf_op jit(solution)/shard_map/all_to_all | solution.py:137
  35.1 17.5 %all-to-all-done.1 = bf16[16,256,128]{2,1,0:T(8,128)(2,1)S(1)} async-done(((bf16[16,256,128]{2,1,0:T(8,128)(2,1)}), bf16[16,256,128]{2,1,0:T(8,128)(2,1)S(1)}, u32[]{:S(2)}, u32[]{:S(2)}) %all-to-all-start.1) | async-done | bytes 1048608 | tf_op jit(solution)/shard_map/all_to_all | solution.py:137
  52.7 0.1 fusion.8
  52.7 0.1 copy.29
  52.9 0.1 collective-permute-start.4
  53.0 0.5 collective-permute-start.5
  53.5 0.1 reverse_select_fusion
  53.5 4.4 %contract.2.acc_ref = f32[2,2,128,128]{3,2,1,0:T(8,128)S(1)} custom-call(s32[1]{0:T(128)} %bitcast.refs_0_.zh_ref, bf16[8,128,128]{2,1,0:T(8,128)(2,1)S(1)} %bitcast.37, bf16[16,128,128]{2,1,0:T(8,128)(2,1)S(1)} %bitcast.36, bf16[16,128,128]{2,1,0:T(8,128)(2,1)S(1)} %get-tuple-element.17.refs_3_, bf16[4,2,128,128]{3,2,1,0:T(8,128)(2,1)S(1)} %bitcast.42, ...), custom_call_target="tpu_custom_call" | custom-call | flops 4000000000 | bytes 4194304 | tf_op jit(solution)/shard_map/contract/pallas_call | solution.py:92
  57.9 0.0 collective-permute-done.4.u_ref
  57.9 0.0 collective-permute-done.5.wr_ref
  57.9 4.2 %contract.3 = f32[2,2,128,128]{3,2,1,0:T(8,128)S(1)} custom-call(s32[1]{0:T(128)} %bitcast.refs_0_.zh_ref, bf16[8,128,128]{2,1,0:T(8,128)(2,1)S(1)} %bitcast.38, bf16[16,128,128]{2,1,0:T(8,128)(2,1)S(1)} %collective-permute-done.4.u_ref, bf16[16,128,128]{2,1,0:T(8,128)(2,1)S(1)} %collective-permute-done.5.wr_ref, bf16[4,2,128,128]{3,2,1,0:T(8,128)(2,1)S(1)} %bitcast.43, ...), custom_call_target="tpu_custom_call" | custom-call | flops 4000000000 | bytes 4194304 | tf_op jit(solution)/shard_map/contract/pallas_call | solution.py:92
  62.2 15.6 %all_to_all.15 = f32[64,8,128]{2,1,0:T(8,128)S(1)} all-to-all(f32[64,8,128]{2,1,0:T(8,128)S(1)} %bitcast.46), channel_id=1, replica_groups=mesh['x'=4,'zl'=2,'y'=4,'zh'=2,'c'=2] {'x','zl','y','zh'}, dimensions={0} | all-to-all | bytes 524288 | tf_op jit(solution)/shard_map/all_to_all | solution.py:149
  77.8 0.1 reduce_sum.9
  77.9 0.6 copy.23
  (9 shorter events, 0.2 us)
Async XLA Ops:
  0.0 0.9 %copy-start = (bf16[128,4,128]{2,1,0:T(4,128)(2,1)S(1)}, bf16[128,4,128]{2,1,0:T(4,128)(2,1)}, u32[]{:S(2)}) copy-start(bf16[128,4,128]{2,1,0:T(4,128)(2,1)} %param.3) | copy-start | bytes 393220
  1.1 7.9 %copy-start.1 = (bf16[128,128]{1,0:T(8,128)(2,1)S(1)}, bf16[128,128]{1,0:T(8,128)(2,1)}, u32[]{:S(2)}) copy-start(bf16[128,128]{1,0:T(8,128)(2,1)} %param.5) | copy-start | bytes 98308
  1.1 18.2 %collective-permute-start = (bf16[16,4,128]{2,0,1:T(8,128)(2,1)S(1)}, bf16[16,4,128]{2,0,1:T(8,128)(2,1)S(1)}, u32[]{:S(2)}, u32[]{:S(2)}) collective-permute-start(bf16[16,4,128]{2,0,1:T(8,128)(2,1)S(1)} %slice.17), channel_id=1, source_target_pairs={{0,16},{16,0},{1,17},{17,1},{2,18},{18,2},{3,19},{19,3},{4,20},{20... | collective-permute-start | bytes 49160 | tf_op jit(solution)/shard_map/ppermute | solution.py:15
  4.2 26.0 %collective-permute-start.3 = (bf16[4,2,128,128]{3,2,1,0:T(8,128)(2,1)S(1)}, bf16[4,2,128,128]{3,2,1,0:T(8,128)(2,1)S(1)}, u32[]{:S(2)}, u32[]{:S(2)}) collective-permute-start(bf16[4,2,128,128]{3,2,1,0:T(8,128)(2,1)S(1)} %bitcast.39), channel_id=1, source_target_pairs={{0,18},{2,16},{16,2},{18,0},{1,19},{3,17},{17,3},{19,1},{4,22},{6,... | collective-permute-start | bytes 786440 | tf_op jit(solution)/shard_map/ppermute | solution.py:19
  6.8 23.4 %collective-permute-start.2 = (bf16[4,2,128,128]{3,2,1,0:T(8,128)(2,1)S(1)}, bf16[4,2,128,128]{3,2,1,0:T(8,128)(2,1)S(1)}, u32[]{:S(2)}, u32[]{:S(2)}) collective-permute-start(bf16[4,2,128,128]{3,2,1,0:T(8,128)(2,1)S(1)} %bitcast.40), channel_id=1, source_target_pairs={{0,16},{16,0},{1,17},{17,1},{2,18},{18,2},{3,19},{19,3},{4,20},{20... | collective-permute-start | bytes 786440 | tf_op jit(solution)/shard_map/ppermute | solution.py:15
  7.8 22.4 %collective-permute-start.1 = (bf16[4,2,128,128]{3,2,1,0:T(8,128)(2,1)S(1)}, bf16[4,2,128,128]{3,2,1,0:T(8,128)(2,1)S(1)}, u32[]{:S(2)}, u32[]{:S(2)}) collective-permute-start(bf16[4,2,128,128]{3,2,1,0:T(8,128)(2,1)S(1)} %bitcast.41), channel_id=1, source_target_pairs={{0,2},{2,0},{1,3},{3,1},{4,6},{6,4},{5,7},{7,5},{8,10},{10,8},{9,1... | collective-permute-start | bytes 786440 | tf_op jit(solution)/shard_map/ppermute | solution.py:15
  9.8 20.5 %all-to-all-start = ((bf16[128,8,128]{2,1,0:T(8,128)(2,1)}), bf16[128,8,128]{2,1,0:T(8,128)(2,1)S(1)}, u32[]{:S(2)}, u32[]{:S(2)}) async-start(bf16[128,8,128]{2,1,0:T(8,128)(2,1)} %bitcast.7), calls=%async_computation | async-start | bytes 524288 | tf_op jit(solution)/shard_map/all_to_all | solution.py:123
  31.4 21.2 %all-to-all-start.1 = ((bf16[16,256,128]{2,1,0:T(8,128)(2,1)}), bf16[16,256,128]{2,1,0:T(8,128)(2,1)S(1)}, u32[]{:S(2)}, u32[]{:S(2)}) async-start(bf16[16,256,128]{2,1,0:T(8,128)(2,1)} %broadcast_in_dim.31), calls=%async_computation.1 | async-start | bytes 2097152 | tf_op jit(solution)/shard_map/all_to_all | solution.py:137
  52.9 5.0 %collective-permute-start.4 = (bf16[16,128,128]{2,1,0:T(8,128)(2,1)S(1)}, bf16[16,128,128]{2,1,0:T(8,128)(2,1)S(1)}, u32[]{:S(2)}, u32[]{:S(2)}) collective-permute-start(bf16[16,128,128]{2,1,0:T(8,128)(2,1)S(1)} %bitcast.35), channel_id=1, source_target_pairs={{0,1},{1,0},{2,3},{3,2},{4,5},{5,4},{6,7},{7,6},{8,9},{9,8},{10,11... | collective-permute-start | bytes 1572872 | tf_op jit(solution)/shard_map/ppermute | solution.py:15
  53.0 4.9 %collective-permute-start.5 = (bf16[16,128,128]{2,1,0:T(8,128)(2,1)S(1)}, bf16[16,128,128]{2,1,0:T(8,128)(2,1)S(1)}, u32[]{:S(2)}, u32[]{:S(2)}) collective-permute-start(bf16[16,128,128]{2,1,0:T(8,128)(2,1)S(1)} %get-tuple-element.17.refs_3_), channel_id=1, source_target_pairs={{0,1},{1,0},{2,3},{3,2},{4,5},{5,4},{6,7},{7,6},{8,9},{9,8},{10,11... | collective-permute-start | bytes 1572872 | tf_op jit(solution)/shard_map/ppermute | solution.py:15
where the time goes:
time: 78.8 us; the launch traced here: 78.5 us
  waiting for transfers between devices  28.4 us (36%)
  starting transfers between devices  20.7 us (26%)
  blocking collectives  15.6 us (20%)
  Pallas kernels  8.61 us (11%)
  local copies, waits for them, and re-layouts  4.71 us (6%)
    all_to_all x1, waiting for transfers between devices, on_device(): got = lax.all_to_all(send, ('x', 'y'), 0, 0, tiled=True)  17.5 us
    all_to_all x1, blocking collectives, on_device(): parts = lax.all_to_all(parts, ('x', 'zl', 'y', 'zh'), 0, 0, tiled=True)  15.6 us
    all_to_all x1, waiting for transfers between devices, on_device(): w = lax.all_to_all(ks, ('x', 'y', 'zl', 'zh', 'c'), 0, 0, tiled=True)  10.8 us
    all_to_all x1, starting transfers between devices, on_device(): w = lax.all_to_all(ks, ('x', 'y', 'zl', 'zh', 'c'), 0, 0, tiled=True)  9.54 us
    pallas_call x2, Pallas kernels, contract(): pl.pallas_call(body, in_specs=[pl.BlockSpec(memory_space=pltpu.SMEM)] + [...  8.61 us
    ppermute x5, starting transfers between devices, swapped(): return lax.ppermute(value, axis, [(0, 1), (1, 0)])  4.87 us
    all_to_all x1, starting transfers between devices, on_device(): got = lax.all_to_all(send, ('x', 'y'), 0, 0, tiled=True)  3.65 us
    ppermute x1, starting transfers between devices, both_swapped(): return lax.ppermute(value, ('zl', 'zh'), [(i, 3 - i) for i in range(4)])  2.6 us
  transfers between devices with their start and end apart: 8, of which 2 were waited for; matrix products, arithmetic and copies ran while one was open for 2% of the time, Pallas kernels for 6%

commit v1 on v0

--- a/solution.py
+++ b/solution.py
@@ -17,6 +17,11 @@
 
 def both_swapped(value):
     return lax.ppermute(value, ("zl", "zh"), [(i, 3 - i) for i in range(4)])
+
+
+def ordered(index, own, other):
+    both = jnp.stack([own, other])
+    return jnp.where(index == 0, both, both[::-1])
 
 
 def mm(a, b):
@@ -118,9 +123,12 @@
     ).astype(BF16)
     mine, theirs = rights[:16], swapped(rights[16:], "zl")
 
-    ks = isometry.reshape(4, 2, 4, 4, 128).transpose(0, 2, 1, 3, 4)
-    ks = jnp.broadcast_to(ks.reshape(16, 1, 8, 128), (16, 8, 8, 128)).reshape(128, 8, 128)
-    w = lax.all_to_all(ks, ("x", "y", "zl", "zh", "c"), 0, 0, tiled=True)
+    pair = ordered(c, isometry, swapped(isometry, "c"))
+    others = [swapped(pair, "zh"), swapped(pair, "zl"), both_swapped(pair)]
+    planes = [ordered(zh, pair, others[0]), ordered(zh, *others[1:])]
+    column = ordered(zl, *planes).reshape(8, 4, 2, 4, 4, 128)
+    ks = column.transpose(1, 3, 2, 4, 0, 5)
+    ks = jnp.where(zl == 0, ks, ks[:, :, ::-1])
 
     l00 = lower.transpose(1, 2, 0, 3)
     l01 = swapped(l00, "zh")
@@ -131,14 +139,18 @@
     first = jnp.where(zl == 0, mine, theirs)
     second = jnp.where(zl == 0, theirs, mine)
     rights = jnp.concatenate([first, second], axis=1)
-    send = jnp.concatenate([rights.reshape(128, 128), isometry], axis=0)
-    send, w, *lowers = lax.optimization_barrier((send, w, *lowers))
-    send = jnp.broadcast_to(send[None], (16, 256, 128))
+    send = jnp.concatenate(
+        [
+            jnp.broadcast_to(rights.reshape(1, 128, 128), (16, 128, 128)),
+            ks.reshape(16, 64, 128),
+            jnp.broadcast_to(isometry[None], (16, 128, 128)),
+        ],
+        axis=1,
+    )
     got = lax.all_to_all(send, ("x", "y"), 0, 0, tiled=True)
-    w = w.transpose(1, 0, 2).reshape(2, 4, 128, 128)
-    w = jnp.where(zl == 0, w, w[::-1]).reshape(8, 128, 128)
-    u = got[:, :128].reshape(16, 16, 8, 128).transpose(1, 0, 2, 3).reshape(16, 128, 128)
-    wr = got[:, 128:]
+    mats = got[:, :192].reshape(16, 24, 8, 128).transpose(1, 0, 2, 3).reshape(24, 128, 128)
+    u, w = mats[:16], mats[16:]
+    wr = got[:, 192:]
     u_other, wr_other = swapped(u, "c"), swapped(wr, "c")
 
     at = zh.astype(jnp.int32)[None]

time: 78.8 us -> 69.5 us (0.88)
  waiting for transfers between devices: 28.4 us -> 19.2 us
  local copies, waits for them, and re-layouts: 4.71 us -> 2.52 us
  other arithmetic: 0.16 us -> 2.31 us
    all_to_all x1 -> x0, waiting for transfers between devices: 10.8 us -> none  [on_device(): w = lax.all_to_all(ks, ('x', 'y', 'zl', 'zh', 'c'), 0, 0, tiled=True)]
    all_to_all x1 -> x0, starting transfers between devices: 9.54 us -> none  [on_device(): w = lax.all_to_all(ks, ('x', 'y', 'zl', 'zh', 'c'), 0, 0, tiled=True)]
    ppermute x5 -> x8, waiting for transfers between devices: 0.01 us -> 5.2 us  [swapped(): return lax.ppermute(value, axis, [(0, 1), (1, 0)])]
    all_to_all x1, waiting for transfers between devices: 17.5 us -> 13.3 us  [on_device(): got = lax.all_to_all(send, ('x', 'y'), 0, 0, tiled=True)]
    ppermute x1 -> x2, starting transfers between devices: 2.6 us -> 6.19 us  [both_swapped(): return lax.ppermute(value, ('zl', 'zh'), [(i, 3 - i) for i in range(4)])]
    all_to_all x1, starting transfers between devices: 3.65 us -> 7.17 us  [on_device(): got = lax.all_to_all(send, ('x', 'y'), 0, 0, tiled=True)]
    ppermute x5 -> x8, starting transfers between devices: 4.87 us -> 7.13 us  [swapped(): return lax.ppermute(value, axis, [(0, 1), (1, 0)])]
    broadcast_in_dim x2, local copies, waits for them, and re-layouts: 1.92 us -> 0.19 us  [the longest x1 0.09 us: on_device(): jnp.broadcast_to(rights.reshape(1, 128, 128), (16, 128, 128))]
  transfers between devices with their start and end apart: 8 -> 11, of which waited for: 2 -> 5; matrix products, arithmetic and copies ran while one was open for 2% -> 1% of each run, Pallas kernels for 6% -> 6%
where the time goes in v1:
time: 69.5 us; the launch traced here: 69.1 us
  starting transfers between devices  20.5 us (29%)
  waiting for transfers between devices  19.2 us (28%)
  blocking collectives  15.6 us (22%)
  Pallas kernels  8.59 us (12%)
  local copies, waits for them, and re-layouts  2.52 us (4%)
  other arithmetic  2.31 us (3%)
    all_to_all x1, blocking collectives, on_device(): parts = lax.all_to_all(parts, ('x', 'zl', 'y', 'zh'), 0, 0, tiled=True)  15.6 us
    all_to_all x1, waiting for transfers between devices, on_device(): got = lax.all_to_all(send, ('x', 'y'), 0, 0, tiled=True)  13.3 us
    pallas_call x2, Pallas kernels, contract(): pl.pallas_call(body, in_specs=[pl.BlockSpec(memory_space=pltpu.SMEM)] + [...  8.59 us
    all_to_all x1, starting transfers between devices, on_device(): got = lax.all_to_all(send, ('x', 'y'), 0, 0, tiled=True)  7.17 us
    ppermute x8, starting transfers between devices, swapped(): return lax.ppermute(value, axis, [(0, 1), (1, 0)])  7.13 us
    ppermute x2, starting transfers between devices, both_swapped(): return lax.ppermute(value, ('zl', 'zh'), [(i, 3 - i) for i in range(4)])  6.19 us
    ppermute x8, waiting for transfers between devices, swapped(): return lax.ppermute(value, axis, [(0, 1), (1, 0)])  5.2 us
  transfers between devices with their start and end apart: 11, of which 5 were waited for; matrix products, arithmetic and copies ran while one was open for 1% of the time, Pallas kernels for 6%

profile of v1, /device:TPU:0, one launch (start us, length us, event | category | flops | bytes accessed | tf_op | source)
XLA Modules:
  0.0 69.1 jit_solution(1528240901228825065)
XLA Ops:
  0.0 0.9 %copy-done = bf16[128,4,128]{2,1,0:T(4,128)(2,1)S(1)} copy-done((bf16[128,4,128]{2,1,0:T(4,128)(2,1)S(1)}, bf16[128,4,128]{2,1,0:T(4,128)(2,1)}, u32[]{:S(2)}) %copy-start) | copy-done | bytes 131096
  0.9 0.2 fusion
  1.1 2.1 %collective-permute-start = (bf16[16,4,128]{2,0,1:T(8,128)(2,1)S(1)}, bf16[16,4,128]{2,0,1:T(8,128)(2,1)S(1)}, u32[]{:S(2)}, u32[]{:S(2)}) collective-permute-start(bf16[16,4,128]{2,0,1:T(8,128)(2,1)S(1)} %slice.33), channel_id=1, source_target_pairs={{0,16},{16,0},{1,17},{17,1},{2,18},{18,2},{3,19},{19,3},{4,20},{20... | collective-permute-start | bytes 49160 | tf_op jit(solution)/shard_map/ppermute | solution.py:15
  3.2 1.7 %collective-permute-done = bf16[16,4,128]{2,0,1:T(8,128)(2,1)S(1)} collective-permute-done((bf16[16,4,128]{2,0,1:T(8,128)(2,1)S(1)}, bf16[16,4,128]{2,0,1:T(8,128)(2,1)S(1)}, u32[]{:S(2)}, u32[]{:S(2)}) %collective-permute-start) | collective-permute-done | bytes 16416 | tf_op jit(solution)/shard_map/ppermute | solution.py:15
  5.0 0.8 %pad_maximum_fusion.4 = bf16[2,128,128]{2,1,0:T(8,128)(2,1)S(1)} fusion(bf16[1,128,128]{2,1,0:T(8,128)(2,1)S(1)} %bitcast.58, bf16[1,128,128]{2,1,0:T(8,128)(2,1)} %bitcast.54), kind=kLoop, calls=%fused_computation.19 | loop fusion | flops 32768 | bytes 131072 | tf_op jit(solution)/shard_map/stack | solution.py:23
  5.8 4.2 %collective-permute-start.4 = (bf16[2,128,128]{2,1,0:T(8,128)(2,1)S(1)}, bf16[2,128,128]{2,1,0:T(8,128)(2,1)S(1)}, u32[]{:S(2)}, u32[]{:S(2)}) collective-permute-start(bf16[2,128,128]{2,1,0:T(8,128)(2,1)S(1)} %reverse_select_fusion.4), channel_id=1, source_target_pairs={{0,18},{2,16},{16,2},{18,0},{1,19},{3,17},{17,3},{19,1},{4,22},{6,... | collective-permute-start | bytes 196616 | tf_op jit(solution)/shard_map/ppermute | solution.py:19
  10.0 1.6 %collective-permute-start.2 = (bf16[2,128,128]{2,1,0:T(8,128)(2,1)S(1)}, bf16[2,128,128]{2,1,0:T(8,128)(2,1)S(1)}, u32[]{:S(2)}, u32[]{:S(2)}) collective-permute-start(bf16[2,128,128]{2,1,0:T(8,128)(2,1)S(1)} %reverse_select_fusion.4), channel_id=1, source_target_pairs={{0,2},{2,0},{1,3},{3,1},{4,6},{6,4},{5,7},{7,5},{8,10},{10,8},{9,1... | collective-permute-start | bytes 196616 | tf_op jit(solution)/shard_map/ppermute | solution.py:15
  11.6 0.7 collective-permute-done.4
  12.2 2.0 %collective-permute-done.3 = bf16[2,128,128]{2,1,0:T(8,128)(2,1)S(1)} collective-permute-done((bf16[2,128,128]{2,1,0:T(8,128)(2,1)S(1)}, bf16[2,128,128]{2,1,0:T(8,128)(2,1)S(1)}, u32[]{:S(2)}, u32[]{:S(2)}) %collective-permute-start.3) | collective-permute-done | bytes 65568 | tf_op jit(solution)/shard_map/ppermute | solution.py:15
  14.3 1.5 %collective-permute-done.2 = bf16[2,128,128]{2,1,0:T(8,128)(2,1)S(1)} collective-permute-done((bf16[2,128,128]{2,1,0:T(8,128)(2,1)S(1)}, bf16[2,128,128]{2,1,0:T(8,128)(2,1)S(1)}, u32[]{:S(2)}, u32[]{:S(2)}) %collective-permute-start.2) | collective-permute-done | bytes 65568 | tf_op jit(solution)/shard_map/ppermute | solution.py:15
  15.8 0.0 copy-start.2
  15.9 0.1 reverse_select_fusion.1
  15.9 0.3 copy.25
  16.2 0.1 reverse_select_fusion
  16.3 0.1 broadcast_in_dim.30
  16.4 0.2 copy-done.2
  16.6 0.1 broadcast_in_dim.31
  16.7 1.2 %pad_maximum_fusion = bf16[16,320,128]{2,1,0:T(8,128)(2,1)} fusion(bf16[16,128,128]{2,1,0:T(8,128)(2,1)S(1)} %broadcast_in_dim.31, bf16[16,64,128]{2,1,0:T(8,128)(2,1)S(1)} %bitcast.49, bf16[16,128,128]{2,1,0:T(8,128)(2,1)S(1)} %broadcast_in_dim.30), kind=kLoop, calls=%fused_computation | loop fusion | flops 3932160 | bytes 2621440 | tf_op jit(solution)/shard_map/concatenate | solution.py:142
  17.9 7.2 %all-to-all-start = ((bf16[16,320,128]{2,1,0:T(8,128)(2,1)}), bf16[16,320,128]{2,1,0:T(8,128)(2,1)S(1)}, u32[]{:S(2)}, u32[]{:S(2)}) async-start(bf16[16,320,128]{2,1,0:T(8,128)(2,1)} %pad_maximum_fusion), calls=%async_computation | async-start | bytes 2621440 | tf_op jit(solution)/shard_map/all_to_all | solution.py:150
  25.1 1.6 %collective-permute-start.7 = (bf16[4,2,128,128]{3,2,1,0:T(8,128)(2,1)S(1)}, bf16[4,2,128,128]{3,2,1,0:T(8,128)(2,1)S(1)}, u32[]{:S(2)}, u32[]{:S(2)}) collective-permute-start(bf16[4,2,128,128]{3,2,1,0:T(8,128)(2,1)S(1)} %bitcast.43), channel_id=1, source_target_pairs={{0,2},{2,0},{1,3},{3,1},{4,6},{6,4},{5,7},{7,5},{8,10},{10,8},{9,1... | collective-permute-start | bytes 786440 | tf_op jit(solution)/shard_map/ppermute | solution.py:15
  26.7 1.2 %collective-permute-start.8 = (bf16[4,2,128,128]{3,2,1,0:T(8,128)(2,1)S(1)}, bf16[4,2,128,128]{3,2,1,0:T(8,128)(2,1)S(1)}, u32[]{:S(2)}, u32[]{:S(2)}) collective-permute-start(bf16[4,2,128,128]{3,2,1,0:T(8,128)(2,1)S(1)} %bitcast.44), channel_id=1, source_target_pairs={{0,16},{16,0},{1,17},{17,1},{2,18},{18,2},{3,19},{19,3},{4,20},{20... | collective-permute-start | bytes 786440 | tf_op jit(solution)/shard_map/ppermute | solution.py:15
  27.9 2.0 %collective-permute-start.9 = (bf16[4,2,128,128]{3,2,1,0:T(8,128)(2,1)S(1)}, bf16[4,2,128,128]{3,2,1,0:T(8,128)(2,1)S(1)}, u32[]{:S(2)}, u32[]{:S(2)}) collective-permute-start(bf16[4,2,128,128]{3,2,1,0:T(8,128)(2,1)S(1)} %bitcast.45), channel_id=1, source_target_pairs={{0,18},{2,16},{16,2},{18,0},{1,19},{3,17},{17,3},{19,1},{4,22},{6,... | collective-permute-start | bytes 786440 | tf_op jit(solution)/shard_map/ppermute | solution.py:19
  29.9 13.3 %all-to-all-done = bf16[16,320,128]{2,1,0:T(8,128)(2,1)S(1)} async-done(((bf16[16,320,128]{2,1,0:T(8,128)(2,1)}), bf16[16,320,128]{2,1,0:T(8,128)(2,1)S(1)}, u32[]{:S(2)}, u32[]{:S(2)}) %all-to-all-start) | async-done | bytes 1310752 | tf_op jit(solution)/shard_map/all_to_all | solution.py:150
  43.2 0.1 slice_bitcast_fusion
  43.2 0.1 copy_bitcast_fusion.refs_2_
  43.4 0.1 collective-permute-start.5
  43.5 0.6 collective-permute-start.6
  44.2 4.4 %contract.2.acc_ref = f32[2,2,128,128]{3,2,1,0:T(8,128)S(1)} custom-call(s32[1]{0:T(128)} %bitcast.refs_0_.zh_ref, bf16[8,128,128]{2,1,0:T(8,128)(2,1)S(1)} %copy_bitcast_fusion.2.refs_1_.w_ref, bf16[16,128,128]{2,1,0:T(8,128)(2,1)S(1)} %copy_bitcast_fusion.refs_2_, bf16[16,128,128]{2,1,0:T(8,128)(2,1)S(1)} %slice.37.refs_3_, ...), custom_call_target="tpu_custom_call" | custom-call | flops 4000000000 | bytes 4194304 | tf_op jit(solution)/shard_map/contract/pallas_call | solution.py:97
  48.5 4.2 %contract.3 = f32[2,2,128,128]{3,2,1,0:T(8,128)S(1)} custom-call(s32[1]{0:T(128)} %bitcast.refs_0_.zh_ref, bf16[8,128,128]{2,1,0:T(8,128)(2,1)S(1)} %copy_bitcast_fusion.2.refs_1_.w_ref, bf16[16,128,128]{2,1,0:T(8,128)(2,1)S(1)} %collective-permute-done.5.u_ref, bf16[16,128,128]{2,1,0:T(8,128)(2,1)S(1)} %collective-permute-done.6.wr_ref, ...), custom_call_target="tpu_custom_call" | custom-call | flops 4000000000 | bytes 4194304 | tf_op jit(solution)/shard_map/contract/pallas_call | solution.py:97
  52.8 15.6 %all_to_all.10 = f32[64,8,128]{2,1,0:T(8,128)S(1)} all-to-all(f32[64,8,128]{2,1,0:T(8,128)S(1)} %bitcast.52), channel_id=1, replica_groups=mesh['x'=4,'zl'=2,'y'=4,'zh'=2,'c'=2] {'x','zl','y','zh'}, dimensions={0} | all-to-all | bytes 524288 | tf_op jit(solution)/shard_map/all_to_all | solution.py:161
  68.5 0.1 reduce_sum.9
  68.5 0.6 copy.16
  (27 shorter events, 0.4 us)
Async XLA Ops:
  0.0 0.9 %copy-start = (bf16[128,4,128]{2,1,0:T(4,128)(2,1)S(1)}, bf16[128,4,128]{2,1,0:T(4,128)(2,1)}, u32[]{:S(2)}) copy-start(bf16[128,4,128]{2,1,0:T(4,128)(2,1)} %param.3) | copy-start | bytes 393220
  1.1 3.8 %collective-permute-start = (bf16[16,4,128]{2,0,1:T(8,128)(2,1)S(1)}, bf16[16,4,128]{2,0,1:T(8,128)(2,1)S(1)}, u32[]{:S(2)}, u32[]{:S(2)}) collective-permute-start(bf16[16,4,128]{2,0,1:T(8,128)(2,1)S(1)} %slice.33), channel_id=1, source_target_pairs={{0,16},{16,0},{1,17},{17,1},{2,18},{18,2},{3,19},{19,3},{4,20},{20... | collective-permute-start | bytes 49160 | tf_op jit(solution)/shard_map/ppermute | solution.py:15
  3.2 1.8 %collective-permute-start.1 = (bf16[128,128]{1,0:T(8,128)(2,1)}, bf16[128,128]{1,0:T(8,128)(2,1)S(1)}, u32[]{:S(2)}, u32[]{:S(2)}) collective-permute-start(bf16[128,128]{1,0:T(8,128)(2,1)} %param.5), channel_id=1, source_target_pairs={{0,1},{1,0},{2,3},{3,2},{4,5},{5,4},{6,7},{7,6},{8,9},{9,8},{10,11... | collective-permute-start | bytes 98312 | tf_op jit(solution)/shard_map/ppermute | solution.py:15
  5.8 6.5 %collective-permute-start.4 = (bf16[2,128,128]{2,1,0:T(8,128)(2,1)S(1)}, bf16[2,128,128]{2,1,0:T(8,128)(2,1)S(1)}, u32[]{:S(2)}, u32[]{:S(2)}) collective-permute-start(bf16[2,128,128]{2,1,0:T(8,128)(2,1)S(1)} %reverse_select_fusion.4), channel_id=1, source_target_pairs={{0,18},{2,16},{16,2},{18,0},{1,19},{3,17},{17,3},{19,1},{4,22},{6,... | collective-permute-start | bytes 196616 | tf_op jit(solution)/shard_map/ppermute | solution.py:19
  10.0 4.3 %collective-permute-start.3 = (bf16[2,128,128]{2,1,0:T(8,128)(2,1)S(1)}, bf16[2,128,128]{2,1,0:T(8,128)(2,1)S(1)}, u32[]{:S(2)}, u32[]{:S(2)}) collective-permute-start(bf16[2,128,128]{2,1,0:T(8,128)(2,1)S(1)} %reverse_select_fusion.4), channel_id=1, source_target_pairs={{0,16},{16,0},{1,17},{17,1},{2,18},{18,2},{3,19},{19,3},{4,20},{20... | collective-permute-start | bytes 196616 | tf_op jit(solution)/shard_map/ppermute | solution.py:15
  10.0 5.8 %collective-permute-start.2 = (bf16[2,128,128]{2,1,0:T(8,128)(2,1)S(1)}, bf16[2,128,128]{2,1,0:T(8,128)(2,1)S(1)}, u32[]{:S(2)}, u32[]{:S(2)}) collective-permute-start(bf16[2,128,128]{2,1,0:T(8,128)(2,1)S(1)} %reverse_select_fusion.4), channel_id=1, source_target_pairs={{0,2},{2,0},{1,3},{3,1},{4,6},{6,4},{5,7},{7,5},{8,10},{10,8},{9,1... | collective-permute-start | bytes 196616 | tf_op jit(solution)/shard_map/ppermute | solution.py:15
  15.8 0.8 %copy-start.2 = (bf16[128,128]{1,0:T(8,128)(2,1)S(1)}, bf16[128,128]{1,0:T(8,128)(2,1)}, u32[]{:S(2)}) copy-start(bf16[128,128]{1,0:T(8,128)(2,1)} %param.5) | copy-start | bytes 98308
  17.8 7.2 %copy-start.1 = (bf16[128,4,2,128]{3,2,1,0:T(2,128)(2,1)S(1)}, bf16[128,4,2,128]{3,2,1,0:T(2,128)(2,1)}, u32[]{:S(2)}) copy-start(bf16[128,4,2,128]{3,2,1,0:T(2,128)(2,1)} %param.4) | copy-start | bytes 786436
  17.9 25.3 %all-to-all-start = ((bf16[16,320,128]{2,1,0:T(8,128)(2,1)}), bf16[16,320,128]{2,1,0:T(8,128)(2,1)S(1)}, u32[]{:S(2)}, u32[]{:S(2)}) async-start(bf16[16,320,128]{2,1,0:T(8,128)(2,1)} %pad_maximum_fusion), calls=%async_computation | async-start | bytes 2621440 | tf_op jit(solution)/shard_map/all_to_all | solution.py:150
  25.1 19.0 %collective-permute-start.7 = (bf16[4,2,128,128]{3,2,1,0:T(8,128)(2,1)S(1)}, bf16[4,2,128,128]{3,2,1,0:T(8,128)(2,1)S(1)}, u32[]{:S(2)}, u32[]{:S(2)}) collective-permute-start(bf16[4,2,128,128]{3,2,1,0:T(8,128)(2,1)S(1)} %bitcast.43), channel_id=1, source_target_pairs={{0,2},{2,0},{1,3},{3,1},{4,6},{6,4},{5,7},{7,5},{8,10},{10,8},{9,1... | collective-permute-start | bytes 786440 | tf_op jit(solution)/shard_map/ppermute | solution.py:15
  26.7 17.4 %collective-permute-start.8 = (bf16[4,2,128,128]{3,2,1,0:T(8,128)(2,1)S(1)}, bf16[4,2,128,128]{3,2,1,0:T(8,128)(2,1)S(1)}, u32[]{:S(2)}, u32[]{:S(2)}) collective-permute-start(bf16[4,2,128,128]{3,2,1,0:T(8,128)(2,1)S(1)} %bitcast.44), channel_id=1, source_target_pairs={{0,16},{16,0},{1,17},{17,1},{2,18},{18,2},{3,19},{19,3},{4,20},{20... | collective-permute-start | bytes 786440 | tf_op jit(solution)/shard_map/ppermute | solution.py:15
  27.9 16.3 %collective-permute-start.9 = (bf16[4,2,128,128]{3,2,1,0:T(8,128)(2,1)S(1)}, bf16[4,2,128,128]{3,2,1,0:T(8,128)(2,1)S(1)}, u32[]{:S(2)}, u32[]{:S(2)}) collective-permute-start(bf16[4,2,128,128]{3,2,1,0:T(8,128)(2,1)S(1)} %bitcast.45), channel_id=1, source_target_pairs={{0,18},{2,16},{16,2},{18,0},{1,19},{3,17},{17,3},{19,1},{4,22},{6,... | collective-permute-start | bytes 786440 | tf_op jit(solution)/shard_map/ppermute | solution.py:19
  43.4 5.2 %collective-permute-start.5 = (bf16[16,128,128]{2,1,0:T(8,128)(2,1)S(1)}, bf16[16,128,128]{2,1,0:T(8,128)(2,1)S(1)}, u32[]{:S(2)}, u32[]{:S(2)}) collective-permute-start(bf16[16,128,128]{2,1,0:T(8,128)(2,1)S(1)} %copy_bitcast_fusion.refs_2_), channel_id=1, source_target_pairs={{0,1},{1,0},{2,3},{3,2},{4,5},{5,4},{6,7},{7,6},{8,9},{9,8},{10,11... | collective-permute-start | bytes 1572872 | tf_op jit(solution)/shard_map/ppermute | solution.py:15
  43.5 5.0 %collective-permute-start.6 = (bf16[16,128,128]{2,1,0:T(8,128)(2,1)S(1)}, bf16[16,128,128]{2,1,0:T(8,128)(2,1)S(1)}, u32[]{:S(2)}, u32[]{:S(2)}) collective-permute-start(bf16[16,128,128]{2,1,0:T(8,128)(2,1)S(1)} %slice.37.refs_3_), channel_id=1, source_target_pairs={{0,1},{1,0},{2,3},{3,2},{4,5},{5,4},{6,7},{7,6},{8,9},{9,8},{10,11... | collective-permute-start | bytes 1572872 | tf_op jit(solution)/shard_map/ppermute | solution.py:15

commit v2 on v1

--- a/solution.py
+++ b/solution.py
@@ -31,15 +31,15 @@
 QB = 4
 
 
-def step_kernel(zh_ref, w_ref, u_ref, wr_ref, l00, l01, l10, l11, acc_ref, out_ref, wt, lower):
+def step_kernel(zh_ref, w_ref, u_ref, wr_ref, near, far, acc_ref, out_ref, wt, lower):
     for k in range(8):
         wt[k * 128 : (k + 1) * 128, :] = w_ref[k].T
-    for zk, refs in enumerate(((l00, l01), (l10, l11))):
-        for zd, ref in enumerate(refs):
-            for j in range(4):
-                for e in range(2):
-                    row, col = (zk * 4 + j) * 128, (zd * 2 + e) * 128
-                    lower[row : row + 128, col : col + 128] = ref[j, e]
+    for zk in range(2):
+        for j in range(4):
+            for e in range(2):
+                rows = slice((zk * 4 + j) * 128, (zk * 4 + j + 1) * 128)
+                lower[rows, e * 128 : (e + 1) * 128] = near[zk, j, e]
+                lower[rows, (e + 2) * 128 : (e + 3) * 128] = far[1 - zk, j, e]
 
     for at in range(0, u_ref.shape[0], QB):
         u = jnp.concatenate([u_ref[at + q] for q in range(QB)], axis=1)
@@ -90,7 +90,7 @@
     if acc is None:
 
         def body(*refs):
-            step_kernel(*refs[:8], None, *refs[8:])
+            step_kernel(*refs[:6], None, *refs[6:])
     else:
         args.append(acc)
 
@@ -121,24 +121,24 @@
     rights = jnp.einsum(
         "qr,mlr->qlm", pick, upper, preferred_element_type=F32
     ).astype(BF16)
-    mine, theirs = rights[:16], swapped(rights[16:], "zl")
-
     pair = ordered(c, isometry, swapped(isometry, "c"))
-    others = [swapped(pair, "zh"), swapped(pair, "zl"), both_swapped(pair)]
-    planes = [ordered(zh, pair, others[0]), ordered(zh, *others[1:])]
-    column = ordered(zl, *planes).reshape(8, 4, 2, 4, 4, 128)
+    theirs = swapped(
+        jnp.concatenate([rights[16:].reshape(64, 128), pair.reshape(256, 128)]), "zl"
+    )
+    first, second = ordered(zl, rights[:16], theirs[:64].reshape(16, 4, 128))
+    rights = jnp.concatenate([first, second], axis=1)
+    near = ordered(zl, pair, theirs[64:].reshape(2, 128, 128))
+    far = both_swapped(near)
+    column = jnp.stack([ordered(zh, near[i], far[i]) for i in range(2)])
+    column = column.reshape(8, 4, 2, 4, 4, 128)
     ks = column.transpose(1, 3, 2, 4, 0, 5)
     ks = jnp.where(zl == 0, ks, ks[:, :, ::-1])
 
-    l00 = lower.transpose(1, 2, 0, 3)
-    l01 = swapped(l00, "zh")
-    l10 = swapped(l00, "zl")
-    l11 = both_swapped(l00)
-    lowers = (l00, l01, l10, l11)
+    lower = lower.transpose(1, 2, 0, 3)
+    l_near = jnp.stack([lower, swapped(lower, "zl")])
+    l_far = both_swapped(l_near)
+    lowers = (l_near, l_far)
 
-    first = jnp.where(zl == 0, mine, theirs)
-    second = jnp.where(zl == 0, theirs, mine)
-    rights = jnp.concatenate([first, second], axis=1)
     send = jnp.concatenate(
         [
             jnp.broadcast_to(rights.reshape(1, 128, 128), (16, 128, 128)),

time: 69.5 us -> 72.5 us (1.043)
  blocking collectives: 15.6 us -> 19.2 us
  starting transfers between devices: 20.5 us -> 17 us
  waiting for transfers between devices: 19.2 us -> 22.1 us
    ppermute x8 -> x5, waiting for transfers between devices: 5.2 us -> 9.69 us  [swapped(): return lax.ppermute(value, axis, [(0, 1), (1, 0)])]
    ppermute x8 -> x5, starting transfers between devices: 7.13 us -> 2.85 us  [swapped(): return lax.ppermute(value, axis, [(0, 1), (1, 0)])]
    all_to_all x1, waiting for transfers between devices: 13.3 us -> 9.52 us  [on_device(): got = lax.all_to_all(send, ('x', 'y'), 0, 0, tiled=True)]
    all_to_all x1, blocking collectives: 15.6 us -> 19.2 us  [on_device(): parts = lax.all_to_all(parts, ('x', 'zl', 'y', 'zh'), 0, 0, tiled=True)]
    ppermute x2, waiting for transfers between devices: 0.67 us -> 2.87 us  [both_swapped(): return lax.ppermute(value, ('zl', 'zh'), [(i, 3 - i) for i in range(4)])]
    ppermute x2, starting transfers between devices: 6.19 us -> 6.95 us  [both_swapped(): return lax.ppermute(value, ('zl', 'zh'), [(i, 3 - i) for i in range(4)])]
  transfers between devices with their start and end apart: 11 -> 8, of which waited for: 5 -> 5; matrix products, arithmetic and copies ran while one was open for 1% -> 1% of each run, Pallas kernels for 6% -> 6%
where the time goes in v2:
time: 72.5 us; the launch traced here: 72.2 us
  waiting for transfers between devices  22.1 us (30%)
  blocking collectives  19.2 us (26%)
  starting transfers between devices  17 us (23%)
  Pallas kernels  8.59 us (12%)
  local copies, waits for them, and re-layouts  2.55 us (4%)
  other arithmetic  2.36 us (3%)
    all_to_all x1, blocking collectives, on_device(): parts = lax.all_to_all(parts, ('x', 'zl', 'y', 'zh'), 0, 0, tiled=True)  19.2 us
    ppermute x5, waiting for transfers between devices, swapped(): return lax.ppermute(value, axis, [(0, 1), (1, 0)])  9.69 us
    all_to_all x1, waiting for transfers between devices, on_device(): got = lax.all_to_all(send, ('x', 'y'), 0, 0, tiled=True)  9.52 us
    pallas_call x2, Pallas kernels, contract(): pl.pallas_call(body, in_specs=[pl.BlockSpec(memory_space=pltpu.SMEM)] + [...  8.59 us
    all_to_all x1, starting transfers between devices, on_device(): got = lax.all_to_all(send, ('x', 'y'), 0, 0, tiled=True)  7.17 us
    ppermute x2, starting transfers between devices, both_swapped(): return lax.ppermute(value, ('zl', 'zh'), [(i, 3 - i) for i in range(4)])  6.95 us
    ppermute x2, waiting for transfers between devices, both_swapped(): return lax.ppermute(value, ('zl', 'zh'), [(i, 3 - i) for i in range(4)])  2.87 us
    ppermute x5, starting transfers between devices, swapped(): return lax.ppermute(value, axis, [(0, 1), (1, 0)])  2.85 us
  transfers between devices with their start and end apart: 8, of which 5 were waited for; matrix products, arithmetic and copies ran while one was open for 1% of the time, Pallas kernels for 6%

profile of v2, /device:TPU:0, one launch (start us, length us, event | category | flops | bytes accessed | tf_op | source)
XLA Modules:
  0.0 72.2 jit_solution(3310040772868126701)
XLA Ops:
  0.0 0.9 %copy-done = bf16[128,4,128]{2,1,0:T(4,128)(2,1)S(1)} copy-done((bf16[128,4,128]{2,1,0:T(4,128)(2,1)S(1)}, bf16[128,4,128]{2,1,0:T(4,128)(2,1)}, u32[]{:S(2)}) %copy-start) | copy-done | bytes 131096
  0.9 0.2 fusion
  1.1 0.3 collective-permute-done
  1.4 0.8 %pad_maximum_fusion.7 = bf16[2,128,128]{2,1,0:T(8,128)(2,1)S(1)} fusion(bf16[1,128,128]{2,1,0:T(8,128)(2,1)S(1)} %bitcast.68, bf16[1,128,128]{2,1,0:T(8,128)(2,1)} %bitcast.65), kind=kLoop, calls=%fused_computation.23 | loop fusion | flops 32768 | bytes 131072 | tf_op jit(solution)/shard_map/stack | solution.py:23
  2.2 2.1 %collective-permute-start.1 = (bf16[320,128]{1,0:T(8,128)(2,1)S(1)}, bf16[320,128]{1,0:T(8,128)(2,1)S(1)}, u32[]{:S(2)}, u32[]{:S(2)}) collective-permute-start(bf16[320,128]{1,0:T(8,128)(2,1)S(1)} %pad_maximum_fusion.6), channel_id=1, source_target_pairs={{0,16},{16,0},{1,17},{17,1},{2,18},{18,2},{3,19},{19,3},{4,20},{20... | collective-permute-start | bytes 245768 | tf_op jit(solution)/shard_map/ppermute | solution.py:15
  4.4 2.8 %collective-permute-done.1 = bf16[320,128]{1,0:T(8,128)(2,1)S(1)} collective-permute-done((bf16[320,128]{1,0:T(8,128)(2,1)S(1)}, bf16[320,128]{1,0:T(8,128)(2,1)S(1)}, u32[]{:S(2)}, u32[]{:S(2)}) %collective-permute-start.1) | collective-permute-done | bytes 81952 | tf_op jit(solution)/shard_map/ppermute | solution.py:15
  7.2 3.9 %collective-permute-start.2 = (bf16[2,2,128,128]{3,2,1,0:T(8,128)(2,1)S(1)}, bf16[2,2,128,128]{3,2,1,0:T(8,128)(2,1)S(1)}, u32[]{:S(2)}, u32[]{:S(2)}) collective-permute-start(bf16[2,2,128,128]{3,2,1,0:T(8,128)(2,1)S(1)} %reverse_select_fusion.3), channel_id=1, source_target_pairs={{0,18},{2,16},{16,2},{18,0},{1,19},{3,17},{17,3},{19,1},{4,22},{6,... | collective-permute-start | bytes 393224 | tf_op jit(solution)/shard_map/ppermute | solution.py:19
  11.2 2.9 %collective-permute-done.2 = bf16[2,2,128,128]{3,2,1,0:T(8,128)(2,1)S(1)} collective-permute-done((bf16[2,2,128,128]{3,2,1,0:T(8,128)(2,1)S(1)}, bf16[2,2,128,128]{3,2,1,0:T(8,128)(2,1)S(1)}, u32[]{:S(2)}, u32[]{:S(2)}) %collective-permute-start.2) | collective-permute-done | bytes 131104 | tf_op jit(solution)/shard_map/ppermute | solution.py:19
  14.1 0.0 copy-start.2
  14.2 0.3 copy.27
  14.6 0.1 reverse_select_fusion
  14.6 0.1 broadcast_in_dim.30
  14.7 0.1 copy-done.2
  14.9 0.1 broadcast_in_dim.31
  15.0 1.2 %pad_maximum_fusion = bf16[16,320,128]{2,1,0:T(8,128)(2,1)} fusion(bf16[16,128,128]{2,1,0:T(8,128)(2,1)S(1)} %broadcast_in_dim.31, bf16[16,64,128]{2,1,0:T(8,128)(2,1)S(1)} %bitcast.55, bf16[16,128,128]{2,1,0:T(8,128)(2,1)S(1)} %broadcast_in_dim.30), kind=kLoop, calls=%fused_computation | loop fusion | flops 3932160 | bytes 2621440 | tf_op jit(solution)/shard_map/concatenate | solution.py:142
  16.2 7.2 %all-to-all-start = ((bf16[16,320,128]{2,1,0:T(8,128)(2,1)}), bf16[16,320,128]{2,1,0:T(8,128)(2,1)S(1)}, u32[]{:S(2)}, u32[]{:S(2)}) async-start(bf16[16,320,128]{2,1,0:T(8,128)(2,1)} %pad_maximum_fusion), calls=%async_computation | async-start | bytes 2621440 | tf_op jit(solution)/shard_map/all_to_all | solution.py:150
  23.4 0.1 collective-permute-start.5
  23.5 6.6 %collective-permute-done.5 = bf16[4,2,128,128]{3,2,1,0:T(8,128)(2,1)S(1)} collective-permute-done((bf16[4,2,128,128]{3,2,1,0:T(8,128)(2,1)S(1)}, bf16[4,2,128,128]{3,2,1,0:T(8,128)(2,1)S(1)}, u32[]{:S(2)}, u32[]{:S(2)}) %collective-permute-start.5) | collective-permute-done | bytes 262176 | tf_op jit(solution)/shard_map/ppermute | solution.py:15
  30.1 0.1 pad_maximum_fusion.1.refs_4_.near
  30.2 3.0 %collective-permute-start.6 = (bf16[2,4,2,128,128]{4,3,2,1,0:T(8,128)(2,1)S(1)}, bf16[2,4,2,128,128]{4,3,2,1,0:T(8,128)(2,1)S(1)}, u32[]{:S(2)}, u32[]{:S(2)}) collective-permute-start(bf16[2,4,2,128,128]{4,3,2,1,0:T(8,128)(2,1)S(1)} %pad_maximum_fusion.1.refs_4_.near), channel_id=1, source_target_pairs={{0,18},{2,16},{16,2},{18,0},{1,19},{3,17},{17,3},{19,1},{4,22},{6,... | collective-permute-start | bytes 1572872 | tf_op jit(solution)/shard_map/ppermute | solution.py:19
  33.2 9.5 %all-to-all-done = bf16[16,320,128]{2,1,0:T(8,128)(2,1)S(1)} async-done(((bf16[16,320,128]{2,1,0:T(8,128)(2,1)}), bf16[16,320,128]{2,1,0:T(8,128)(2,1)S(1)}, u32[]{:S(2)}, u32[]{:S(2)}) %all-to-all-start) | async-done | bytes 1310752 | tf_op jit(solution)/shard_map/all_to_all | solution.py:150
  42.7 0.1 slice_bitcast_fusion
  42.8 0.1 copy_bitcast_fusion.refs_2_
  42.9 0.1 collective-permute-start.3
  43.0 0.6 collective-permute-start.4
  43.7 4.4 %contract.2.acc_ref = f32[2,2,128,128]{3,2,1,0:T(8,128)S(1)} custom-call(s32[1]{0:T(128)} %bitcast.refs_0_.zh_ref, bf16[8,128,128]{2,1,0:T(8,128)(2,1)S(1)} %copy_bitcast_fusion.1.refs_1_.w_ref, bf16[16,128,128]{2,1,0:T(8,128)(2,1)S(1)} %copy_bitcast_fusion.refs_2_, bf16[16,128,128]{2,1,0:T(8,128)(2,1)S(1)} %slice.67.refs_3_, ...), custom_call_target="tpu_custom_call" | custom-call | flops 4000000000 | bytes 4194304 | tf_op jit(solution)/shard_map/contract/pallas_call | solution.py:97
  48.0 0.0 collective-permute-done.3.u_ref
  48.0 0.0 collective-permute-done.4.wr_ref
  48.1 4.2 %contract.3 = f32[2,2,128,128]{3,2,1,0:T(8,128)S(1)} custom-call(s32[1]{0:T(128)} %bitcast.refs_0_.zh_ref, bf16[8,128,128]{2,1,0:T(8,128)(2,1)S(1)} %copy_bitcast_fusion.1.refs_1_.w_ref, bf16[16,128,128]{2,1,0:T(8,128)(2,1)S(1)} %collective-permute-done.3.u_ref, bf16[16,128,128]{2,1,0:T(8,128)(2,1)S(1)} %collective-permute-done.4.wr_ref, ...), custom_call_target="tpu_custom_call" | custom-call | flops 4000000000 | bytes 4194304 | tf_op jit(solution)/shard_map/contract/pallas_call | solution.py:97
  52.3 19.2 %all_to_all.10 = f32[64,8,128]{2,1,0:T(8,128)S(1)} all-to-all(f32[64,8,128]{2,1,0:T(8,128)S(1)} %bitcast.58), channel_id=1, replica_groups=mesh['x'=4,'zl'=2,'y'=4,'zh'=2,'c'=2] {'x','zl','y','zh'}, dimensions={0} | all-to-all | bytes 524288 | tf_op jit(solution)/shard_map/all_to_all | solution.py:161
  71.5 0.1 reduce_sum.9
  71.6 0.6 copy.18
  (31 shorter events, 0.5 us)
Async XLA Ops:
  0.0 0.9 %copy-start = (bf16[128,4,128]{2,1,0:T(4,128)(2,1)S(1)}, bf16[128,4,128]{2,1,0:T(4,128)(2,1)}, u32[]{:S(2)}) copy-start(bf16[128,4,128]{2,1,0:T(4,128)(2,1)} %param.3) | copy-start | bytes 393220
  0.0 1.4 %collective-permute-start = (bf16[128,128]{1,0:T(8,128)(2,1)}, bf16[128,128]{1,0:T(8,128)(2,1)S(1)}, u32[]{:S(2)}, u32[]{:S(2)}) collective-permute-start(bf16[128,128]{1,0:T(8,128)(2,1)} %param.5), channel_id=1, source_target_pairs={{0,1},{1,0},{2,3},{3,2},{4,5},{5,4},{6,7},{7,6},{8,9},{9,8},{10,11... | collective-permute-start | bytes 98312 | tf_op jit(solution)/shard_map/ppermute | solution.py:15
  2.2 4.9 %collective-permute-start.1 = (bf16[320,128]{1,0:T(8,128)(2,1)S(1)}, bf16[320,128]{1,0:T(8,128)(2,1)S(1)}, u32[]{:S(2)}, u32[]{:S(2)}) collective-permute-start(bf16[320,128]{1,0:T(8,128)(2,1)S(1)} %pad_maximum_fusion.6), channel_id=1, source_target_pairs={{0,16},{16,0},{1,17},{17,1},{2,18},{18,2},{3,19},{19,3},{4,20},{20... | collective-permute-start | bytes 245768 | tf_op jit(solution)/shard_map/ppermute | solution.py:15
  7.2 6.9 %collective-permute-start.2 = (bf16[2,2,128,128]{3,2,1,0:T(8,128)(2,1)S(1)}, bf16[2,2,128,128]{3,2,1,0:T(8,128)(2,1)S(1)}, u32[]{:S(2)}, u32[]{:S(2)}) collective-permute-start(bf16[2,2,128,128]{3,2,1,0:T(8,128)(2,1)S(1)} %reverse_select_fusion.3), channel_id=1, source_target_pairs={{0,18},{2,16},{16,2},{18,0},{1,19},{3,17},{17,3},{19,1},{4,22},{6,... | collective-permute-start | bytes 393224 | tf_op jit(solution)/shard_map/ppermute | solution.py:19
  14.1 0.8 %copy-start.2 = (bf16[128,128]{1,0:T(8,128)(2,1)S(1)}, bf16[128,128]{1,0:T(8,128)(2,1)}, u32[]{:S(2)}) copy-start(bf16[128,128]{1,0:T(8,128)(2,1)} %param.5) | copy-start | bytes 98308
  16.1 7.2 %copy-start.1 = (bf16[128,4,2,128]{3,2,1,0:T(2,128)(2,1)S(1)}, bf16[128,4,2,128]{3,2,1,0:T(2,128)(2,1)}, u32[]{:S(2)}) copy-start(bf16[128,4,2,128]{3,2,1,0:T(2,128)(2,1)} %param.4) | copy-start | bytes 786436
  16.2 26.5 %all-to-all-start = ((bf16[16,320,128]{2,1,0:T(8,128)(2,1)}), bf16[16,320,128]{2,1,0:T(8,128)(2,1)S(1)}, u32[]{:S(2)}, u32[]{:S(2)}) async-start(bf16[16,320,128]{2,1,0:T(8,128)(2,1)} %pad_maximum_fusion), calls=%async_computation | async-start | bytes 2621440 | tf_op jit(solution)/shard_map/all_to_all | solution.py:150
  23.4 6.7 %collective-permute-start.5 = (bf16[4,2,128,128]{3,2,1,0:T(8,128)(2,1)S(1)}, bf16[4,2,128,128]{3,2,1,0:T(8,128)(2,1)S(1)}, u32[]{:S(2)}, u32[]{:S(2)}) collective-permute-start(bf16[4,2,128,128]{3,2,1,0:T(8,128)(2,1)S(1)} %bitcast.59), channel_id=1, source_target_pairs={{0,16},{16,0},{1,17},{17,1},{2,18},{18,2},{3,19},{19,3},{4,20},{20... | collective-permute-start | bytes 786440 | tf_op jit(solution)/shard_map/ppermute | solution.py:15
  30.2 13.5 %collective-permute-start.6 = (bf16[2,4,2,128,128]{4,3,2,1,0:T(8,128)(2,1)S(1)}, bf16[2,4,2,128,128]{4,3,2,1,0:T(8,128)(2,1)S(1)}, u32[]{:S(2)}, u32[]{:S(2)}) collective-permute-start(bf16[2,4,2,128,128]{4,3,2,1,0:T(8,128)(2,1)S(1)} %pad_maximum_fusion.1.refs_4_.near), channel_id=1, source_target_pairs={{0,18},{2,16},{16,2},{18,0},{1,19},{3,17},{17,3},{19,1},{4,22},{6,... | collective-permute-start | bytes 1572872 | tf_op jit(solution)/shard_map/ppermute | solution.py:19
  42.9 5.1 %collective-permute-start.3 = (bf16[16,128,128]{2,1,0:T(8,128)(2,1)S(1)}, bf16[16,128,128]{2,1,0:T(8,128)(2,1)S(1)}, u32[]{:S(2)}, u32[]{:S(2)}) collective-permute-start(bf16[16,128,128]{2,1,0:T(8,128)(2,1)S(1)} %copy_bitcast_fusion.refs_2_), channel_id=1, source_target_pairs={{0,1},{1,0},{2,3},{3,2},{4,5},{5,4},{6,7},{7,6},{8,9},{9,8},{10,11... | collective-permute-start | bytes 1572872 | tf_op jit(solution)/shard_map/ppermute | solution.py:15
  43.0 5.0 %collective-permute-start.4 = (bf16[16,128,128]{2,1,0:T(8,128)(2,1)S(1)}, bf16[16,128,128]{2,1,0:T(8,128)(2,1)S(1)}, u32[]{:S(2)}, u32[]{:S(2)}) collective-permute-start(bf16[16,128,128]{2,1,0:T(8,128)(2,1)S(1)} %slice.67.refs_3_), channel_id=1, source_target_pairs={{0,1},{1,0},{2,3},{3,2},{4,5},{5,4},{6,7},{7,6},{8,9},{9,8},{10,11... | collective-permute-start | bytes 1572872 | tf_op jit(solution)/shard_map/ppermute | solution.py:15

commit v3 on v1

v3 whole, which is shorter than its diff:
```python
import jax
import jax.numpy as jnp
from jax import lax
from jax.experimental import pallas as pl
from jax.experimental.pallas import tpu as pltpu
from jax.sharding import Mesh, PartitionSpec as P

SIZES = (4, 2, 4, 2, 2)
NAMES = ("x", "zl", "y", "zh", "c")
BF16 = jnp.bfloat16
F32 = jnp.float32


def from_everyone(value, axes, peers):
    return lax.all_to_all(
        jnp.broadcast_to(value[None], (peers, *value.shape)), axes, 0, 0, tiled=True
    )


def swapped(value, axis):
    return lax.ppermute(value, axis, [(0, 1), (1, 0)])


def both_swapped(value):
    return lax.ppermute(value, ("zl", "zh"), [(i, 3 - i) for i in range(4)])


def mm(a, b):
    return lax.dot_general(a, b, (((1,), (0,)), ((), ())), preferred_element_type=F32)


QB = 4


def step_kernel(zl_ref, zh_ref, w_ref, u0, u1, wr0, wr1, l00, l01, l10, l11, out_ref, wt, lower):
    for k in range(8):
        wt[k * 128 : (k + 1) * 128, :] = w_ref[k].T
    for zk, refs in enumerate(((l00, l01), (l10, l11))):
        plane = zl_ref[0] if zk == 0 else 1 - zl_ref[0]
        for j in range(4):
            row = pl.multiple_of((plane * 4 + j) * 128, 128)
            for zd, ref in enumerate(refs):
                for e in range(2):
                    col = (zd * 2 + e) * 128
                    lower[pl.ds(row, 128), col : col + 128] = ref[j, e]

    for half, (u_ref, wr_ref) in enumerate(((u0, wr0), (u1, wr1))):
        for at in range(0, u_ref.shape[0], QB):
            u = jnp.concatenate([u_ref[at + q] for q in range(QB)], axis=1)
            joined = mm(wt[...], u).astype(BF16)
            left = jnp.concatenate(
                [
                    jnp.concatenate(
                        [
                            joined[k * 128 : (k + 1) * 128, q * 128 : (q + 1) * 128]
                            for k in range(8)
                        ],
                        axis=1,
                    )
                    for q in range(QB)
                ],
                axis=0,
            )
            paired = mm(left, lower[...]).astype(BF16)
            rows = jnp.concatenate(
                [
                    jnp.concatenate(
                        [
                            paired[q * 128 : (q + 1) * 128, d * 128 : (d + 1) * 128]
                            for q in range(QB)
                        ],
                        axis=1,
                    )
                    for d in range(4)
                ],
                axis=0,
            )
            part = mm(rows, wr_ref[at : at + QB].reshape(QB * 128, 128))
            part = part.reshape(2, 2, 128, 128)
            for zd in range(2):
                to = zh_ref[0] if zd == 0 else 1 - zh_ref[0]
                if half + at == 0:
                    out_ref[to] = part[zd]
                else:
                    out_ref[to] += part[zd]


def contract(zl, zh, w, u, wr, lowers):
    vmem = pl.BlockSpec(memory_space=pltpu.VMEM)
    args = [zl, zh, w, *u, *wr, *lowers]
    return pl.pallas_call(
        step_kernel,
        in_specs=[pl.BlockSpec(memory_space=pltpu.SMEM)] * 2 + [vmem] * (len(args) - 2),
        out_specs=vmem,
        out_shape=jax.ShapeDtypeStruct((2, 2, 128, 128), F32),
        scratch_shapes=[pltpu.VMEM((1024, 128), BF16), pltpu.VMEM((1024, 512), BF16)],
        compiler_params=pltpu.CompilerParams(vmem_limit_bytes=40 * 1024 * 1024),
        cost_estimate=pl.CostEstimate(
            flops=8 * 10**9, bytes_accessed=6 * 2**20, transcendentals=0
        ),
        name="contract",
    )(*args)


def on_device(upper, lower, isometry):
    zl = lax.axis_index("zl")
    zh = lax.axis_index("zh")
    c = lax.axis_index("c")

    t = jnp.arange(32)
    plane = jnp.where(t < 16, zl, 1 - zl)
    xy = t % 16
    wanted = 4 * ((xy // 4) * 8 + plane * 4 + xy % 4) + 2 * zh + c
    pick = (wanted[:, None] == jnp.arange(128)[None, :]).astype(BF16)
    rights = jnp.einsum(
        "qr,mlr->qlm", pick, upper, preferred_element_type=F32
    ).astype(BF16)
    theirs = swapped(rights[16:], "zl")
    mine = rights[:16]

    l00 = lower.transpose(1, 2, 0, 3)
    l01 = swapped(l00, "zh")
    l10 = swapped(l00, "zl")
    l11 = both_swapped(l00)
    lowers = (l00, l01, l10, l11)

    first = jnp.where(zl == 0, mine, theirs)
    second = jnp.where(zl == 0, theirs, mine)
    rights = jnp.concatenate([first, second], axis=1)
    ks = isometry.reshape(4, 2, 4, 4, 128).transpose(0, 2, 1, 3, 4)
    send = jnp.concatenate(
        [
            jnp.broadcast_to(rights.reshape(1, 128, 128), (16, 128, 128)),
            jnp.broadcast_to(isometry[None], (16, 128, 128)),
            ks.reshape(16, 8, 128),
        ],
        axis=1,
    )
    got = lax.all_to_all(send, ("x", "y"), 0, 0, tiled=True)
    u = got[:, :128].reshape(16, 16, 8, 128).transpose(1, 0, 2, 3).reshape(16, 128, 128)
    wr = got[:, 128:256]
    u_other, wr_other = swapped(u, "c"), swapped(wr, "c")

    w = from_everyone(got[:, 256:], ("zl", "zh", "c"), 8)
    w = w.transpose(2, 1, 0, 3).reshape(8, 128, 128)

    here = (zl.astype(jnp.int32)[None], zh.astype(jnp.int32)[None])
    acc = contract(*here, w, (u, u_other), (wr, wr_other), lowers)

    parts = acc.reshape(2, 2, 32, 4, 128).transpose(2, 0, 1, 3, 4).reshape(64, 8, 128)
    parts = lax.all_to_all(parts, ("x", "zl", "y", "zh"), 0, 0, tiled=True)
    return jnp.sum(parts, axis=0).reshape(2, 4, 128).transpose(1, 0, 2)


def solution(mesh):
    return jax.shard_map(
        on_device,
        mesh=Mesh(mesh.devices.reshape(SIZES), NAMES),
        in_specs=(
            P(None, ("x", "zl", "y"), None),
            P(None, ("x", "zl", "y"), ("zh", "c"), None),
            P(NAMES, None),
        ),
        out_specs=P(("x", "zl", "y"), ("zh", "c"), None),
        check_vma=False,
    )
```

time: 69.5 us -> 76.5 us (1.10)
  blocking collectives: 15.6 us -> 54.3 us
  waiting for transfers between devices: 19.2 us -> 0.96 us
  starting transfers between devices: 20.5 us -> 8.19 us
  other arithmetic: 2.31 us -> 0.18 us
  local copies, waits for them, and re-layouts: 2.52 us -> 3.88 us
    all_to_all x0 -> x2, blocking collectives: none -> 38.4 us  [the longest x1 23.6 us: on_device(): got = lax.all_to_all(send, ('x', 'y'), 0, 0, tiled=True)]
    all_to_all x1 -> x0, waiting for transfers between devices: 13.3 us -> none  [on_device(): got = lax.all_to_all(send, ('x', 'y'), 0, 0, tiled=True)]
    all_to_all x1 -> x0, starting transfers between devices: 7.17 us -> none  [on_device(): got = lax.all_to_all(send, ('x', 'y'), 0, 0, tiled=True)]
    ppermute x8 -> x5, waiting for transfers between devices: 5.2 us -> 0.96 us  [swapped(): return lax.ppermute(value, axis, [(0, 1), (1, 0)])]
    ppermute x8 -> x5, starting transfers between devices: 7.13 us -> 4.25 us  [swapped(): return lax.ppermute(value, axis, [(0, 1), (1, 0)])]
    ppermute x2 -> x1, starting transfers between devices: 6.19 us -> 3.94 us  [both_swapped(): return lax.ppermute(value, ('zl', 'zh'), [(i, 3 - i) for i in range(4)])]
    concatenate x1, other arithmetic: 1.17 us -> 0.08 us  [on_device(): jnp.concatenate([jnp.broadcast_to(rights.reshape(1, 128, 128), (16, 128,...]
    another operation x7 -> x0, other arithmetic: 0.9 us -> none  [ordered(): both = jnp.stack([own, other])]
  transfers between devices with their start and end apart: 11 -> 6, of which waited for: 5 -> 1; matrix products, arithmetic and copies ran while one was open for 1% -> 1% of each run, Pallas kernels for 6% -> 0%
where the time goes in v3:
time: 76.5 us; the launch traced here: 76.1 us
  blocking collectives  54.3 us (71%)
  Pallas kernels  8.29 us (11%)
  starting transfers between devices  8.19 us (11%)
  local copies, waits for them, and re-layouts  3.88 us (5%)
  waiting for transfers between devices  0.96 us (1%)
    all_to_all x1, blocking collectives, on_device(): got = lax.all_to_all(send, ('x', 'y'), 0, 0, tiled=True)  23.6 us
    all_to_all x1, blocking collectives, on_device(): parts = lax.all_to_all(parts, ('x', 'zl', 'y', 'zh'), 0, 0, tiled=True)  16 us
    all_to_all x1, blocking collectives, from_everyone(): lax.all_to_all(jnp.broadcast_to(value[None], (peers, *value.shape)), axes...  14.8 us
    pallas_call x1, Pallas kernels, contract(): pl.pallas_call(step_kernel, in_specs=[pl.BlockSpec(memory_space=pltpu.SME...  8.29 us
    ppermute x5, starting transfers between devices, swapped(): return lax.ppermute(value, axis, [(0, 1), (1, 0)])  4.25 us
    ppermute x1, starting transfers between devices, both_swapped(): return lax.ppermute(value, ('zl', 'zh'), [(i, 3 - i) for i in range(4)])  3.94 us
  transfers between devices with their start and end apart: 6, of which 1 were waited for; matrix products, arithmetic and copies ran while one was open for 1% of the time, Pallas kernels for 0%

profile of v3, /device:TPU:0, one launch (start us, length us, event | category | flops | bytes accessed | tf_op | source)
XLA Modules:
  0.0 76.1 jit_solution(14289507778709162281)
XLA Ops:
  0.0 0.0 copy-start
  0.0 0.9 %copy-done = bf16[128,4,128]{2,1,0:T(4,128)(2,1)S(1)} copy-done((bf16[128,4,128]{2,1,0:T(4,128)(2,1)S(1)}, bf16[128,4,128]{2,1,0:T(4,128)(2,1)}, u32[]{:S(2)}) %copy-start) | copy-done | bytes 131096
  0.9 0.2 fusion
  1.1 2.1 %collective-permute-start = (bf16[16,4,128]{2,0,1:T(8,128)(2,1)S(1)}, bf16[16,4,128]{2,0,1:T(8,128)(2,1)S(1)}, u32[]{:S(2)}, u32[]{:S(2)}) collective-permute-start(bf16[16,4,128]{2,0,1:T(8,128)(2,1)S(1)} %slice.21), channel_id=1, source_target_pairs={{0,16},{16,0},{1,17},{17,1},{2,18},{18,2},{3,19},{19,3},{4,20},{20... | collective-permute-start | bytes 49160 | tf_op jit(solution)/shard_map/ppermute | solution.py:21
  3.2 0.8 %copy.19 = bf16[4,2,4,4,128]{4,3,1,2,0:T(4,128)(2,1)S(1)} copy(bf16[4,2,4,4,128]{4,3,2,1,0:T(4,128)(2,1)} %bitcast.46) | data formatting | bytes 65536 | tf_op jit(solution)/shard_map/reshape | solution.py:130
  4.0 0.9 %collective-permute-done = bf16[16,4,128]{2,0,1:T(8,128)(2,1)S(1)} collective-permute-done((bf16[16,4,128]{2,0,1:T(8,128)(2,1)S(1)}, bf16[16,4,128]{2,0,1:T(8,128)(2,1)S(1)}, u32[]{:S(2)}, u32[]{:S(2)}) %collective-permute-start) | collective-permute-done | bytes 16416 | tf_op jit(solution)/shard_map/ppermute | solution.py:21
  5.0 0.1 broadcast_in_dim.40
  5.1 0.9 %broadcast_in_dim.41 = bf16[16,128,128]{2,1,0:T(8,128)(2,1)S(1)} broadcast(bf16[128,128]{1,0:T(8,128)(2,1)} %param.5), dimensions={1,2} | broadcast | bytes 557056 | tf_op jit(solution)/shard_map/broadcast_in_dim | solution.py:134
  5.9 0.1 pad_maximum_fusion
  6.0 23.6 %all_to_all.15 = bf16[16,264,128]{2,1,0:T(8,128)(2,1)S(1)} all-to-all(bf16[16,264,128]{2,1,0:T(8,128)(2,1)S(1)} %pad_maximum_fusion), channel_id=1, replica_groups=mesh['x'=4,'zl'=2,'y'=4,'zh'=2,'c'=2] {'x','y'}, dimensions={0} | all-to-all | bytes 2162688 | tf_op jit(solution)/shard_map/all_to_all | solution.py:139
  29.6 0.0 copy-start.1
  29.6 0.1 fusion.8
  29.7 0.1 copy.32
  29.9 0.1 collective-permute-start.1
  30.0 0.5 collective-permute-start.2
  30.5 0.1 copy-done.1
  30.6 3.9 %collective-permute-start.5 = (bf16[4,2,128,128]{3,2,1,0:T(8,128)(2,1)S(1)}, bf16[4,2,128,128]{3,2,1,0:T(8,128)(2,1)S(1)}, u32[]{:S(2)}, u32[]{:S(2)}) collective-permute-start(bf16[4,2,128,128]{3,2,1,0:T(8,128)(2,1)S(1)} %bitcast.37), channel_id=1, source_target_pairs={{0,18},{2,16},{16,2},{18,0},{1,19},{3,17},{17,3},{19,1},{4,22},{6,... | collective-permute-start | bytes 786440 | tf_op jit(solution)/shard_map/ppermute | solution.py:25
  34.5 0.0 collective-permute-start.4
  34.5 1.6 %collective-permute-start.3 = (bf16[4,2,128,128]{3,2,1,0:T(8,128)(2,1)S(1)}, bf16[4,2,128,128]{3,2,1,0:T(8,128)(2,1)S(1)}, u32[]{:S(2)}, u32[]{:S(2)}) collective-permute-start(bf16[4,2,128,128]{3,2,1,0:T(8,128)(2,1)S(1)} %bitcast.39), channel_id=1, source_target_pairs={{0,2},{2,0},{1,3},{3,1},{4,6},{6,4},{5,7},{7,5},{8,10},{10,8},{9,1... | collective-permute-start | bytes 786440 | tf_op jit(solution)/shard_map/ppermute | solution.py:21
  36.1 14.8 %all_to_all.16 = bf16[8,16,8,128]{3,1,2,0:T(8,128)(2,1)S(1)} all-to-all(bf16[8,16,8,128]{3,1,2,0:T(8,128)(2,1)S(1)} %broadcast_in_dim.42), channel_id=1, replica_groups=mesh['x'=4,'zl'=2,'y'=4,'zh'=2,'c'=2] {'zl','zh','c'}, dimensions={0} | all-to-all | bytes 524288 | tf_op jit(solution)/shard_map/all_to_all | solution.py:15
  50.9 0.2 copy.34
  51.1 0.0 collective-permute-done.5.l11
  51.1 0.0 collective-permute-done.4.l10
  51.1 0.0 collective-permute-done.3.l01
  51.1 0.0 collective-permute-done.1.u1
  51.1 0.0 collective-permute-done.2.wr1
  51.2 8.3 %contract.1 = f32[2,2,128,128]{3,2,1,0:T(8,128)S(1)} custom-call(s32[1]{0:T(128)} %bitcast.zl_ref, s32[1]{0:T(128)} %bitcast.1.zh_ref, bf16[8,128,128]{2,1,0:T(8,128)(2,1)S(1)} %bitcast.41, bf16[16,128,128]{2,1,0:T(8,128)(2,1)S(1)} %bitcast.36, bf16[16,128,128]{2,1,0:T(8,128)(2,1)S(1)} %collective-permute-done.1.u1, ...), custom_call_target="tpu_custom_call" | custom-call | flops 8000000000 | bytes 6291456 | tf_op jit(solution)/shard_map/contract/pallas_call | solution.py:91
  59.5 16.0 %all_to_all.17 = f32[64,8,128]{2,1,0:T(8,128)S(1)} all-to-all(f32[64,8,128]{2,1,0:T(8,128)S(1)} %bitcast.44), channel_id=1, replica_groups=mesh['x'=4,'zl'=2,'y'=4,'zh'=2,'c'=2] {'x','zl','y','zh'}, dimensions={0} | all-to-all | bytes 524288 | tf_op jit(solution)/shard_map/all_to_all | solution.py:151
  75.5 0.1 reduce_sum.9
  75.5 0.6 copy.25
  (10 shorter events, 0.2 us)
Async XLA Ops:
  0.0 0.9 %copy-start = (bf16[128,4,128]{2,1,0:T(4,128)(2,1)S(1)}, bf16[128,4,128]{2,1,0:T(4,128)(2,1)}, u32[]{:S(2)}) copy-start(bf16[128,4,128]{2,1,0:T(4,128)(2,1)} %param.3) | copy-start | bytes 393220
  1.1 3.8 %collective-permute-start = (bf16[16,4,128]{2,0,1:T(8,128)(2,1)S(1)}, bf16[16,4,128]{2,0,1:T(8,128)(2,1)S(1)}, u32[]{:S(2)}, u32[]{:S(2)}) collective-permute-start(bf16[16,4,128]{2,0,1:T(8,128)(2,1)S(1)} %slice.21), channel_id=1, source_target_pairs={{0,16},{16,0},{1,17},{17,1},{2,18},{18,2},{3,19},{19,3},{4,20},{20... | collective-permute-start | bytes 49160 | tf_op jit(solution)/shard_map/ppermute | solution.py:21
  29.6 1.0 %copy-start.1 = (bf16[128,4,2,128]{3,2,1,0:T(2,128)(2,1)S(1)}, bf16[128,4,2,128]{3,2,1,0:T(2,128)(2,1)}, u32[]{:S(2)}) copy-start(bf16[128,4,2,128]{3,2,1,0:T(2,128)(2,1)} %param.4) | copy-start | bytes 786436
  29.9 21.3 %collective-permute-start.1 = (bf16[16,128,128]{2,1,0:T(8,128)(2,1)S(1)}, bf16[16,128,128]{2,1,0:T(8,128)(2,1)S(1)}, u32[]{:S(2)}, u32[]{:S(2)}) collective-permute-start(bf16[16,128,128]{2,1,0:T(8,128)(2,1)S(1)} %bitcast.35), channel_id=1, source_target_pairs={{0,1},{1,0},{2,3},{3,2},{4,5},{5,4},{6,7},{7,6},{8,9},{9,8},{10,11... | collective-permute-start | bytes 1572872 | tf_op jit(solution)/shard_map/ppermute | solution.py:21
  30.0 21.2 %collective-permute-start.2 = (bf16[16,128,128]{2,1,0:T(8,128)(2,1)S(1)}, bf16[16,128,128]{2,1,0:T(8,128)(2,1)S(1)}, u32[]{:S(2)}, u32[]{:S(2)}) collective-permute-start(bf16[16,128,128]{2,1,0:T(8,128)(2,1)S(1)} %get-tuple-element.5.wr0), channel_id=1, source_target_pairs={{0,1},{1,0},{2,3},{3,2},{4,5},{5,4},{6,7},{7,6},{8,9},{9,8},{10,11... | collective-permute-start | bytes 1572872 | tf_op jit(solution)/shard_map/ppermute | solution.py:21
  30.6 20.5 %collective-permute-start.5 = (bf16[4,2,128,128]{3,2,1,0:T(8,128)(2,1)S(1)}, bf16[4,2,128,128]{3,2,1,0:T(8,128)(2,1)S(1)}, u32[]{:S(2)}, u32[]{:S(2)}) collective-permute-start(bf16[4,2,128,128]{3,2,1,0:T(8,128)(2,1)S(1)} %bitcast.37), channel_id=1, source_target_pairs={{0,18},{2,16},{16,2},{18,0},{1,19},{3,17},{17,3},{19,1},{4,22},{6,... | collective-permute-start | bytes 786440 | tf_op jit(solution)/shard_map/ppermute | solution.py:25
  34.5 16.6 %collective-permute-start.4 = (bf16[4,2,128,128]{3,2,1,0:T(8,128)(2,1)S(1)}, bf16[4,2,128,128]{3,2,1,0:T(8,128)(2,1)S(1)}, u32[]{:S(2)}, u32[]{:S(2)}) collective-permute-start(bf16[4,2,128,128]{3,2,1,0:T(8,128)(2,1)S(1)} %bitcast.38), channel_id=1, source_target_pairs={{0,16},{16,0},{1,17},{17,1},{2,18},{18,2},{3,19},{19,3},{4,20},{20... | collective-permute-start | bytes 786440 | tf_op jit(solution)/shard_map/ppermute | solution.py:21
  34.5 16.6 %collective-permute-start.3 = (bf16[4,2,128,128]{3,2,1,0:T(8,128)(2,1)S(1)}, bf16[4,2,128,128]{3,2,1,0:T(8,128)(2,1)S(1)}, u32[]{:S(2)}, u32[]{:S(2)}) collective-permute-start(bf16[4,2,128,128]{3,2,1,0:T(8,128)(2,1)S(1)} %bitcast.39), channel_id=1, source_target_pairs={{0,2},{2,0},{1,3},{3,1},{4,6},{6,4},{5,7},{7,5},{8,10},{10,8},{9,1... | collective-permute-start | bytes 786440 | tf_op jit(solution)/shard_map/ppermute | solution.py:21

commit v4 on v3

--- a/solution.py
+++ b/solution.py
@@ -23,6 +23,11 @@
 
 def both_swapped(value):
     return lax.ppermute(value, ("zl", "zh"), [(i, 3 - i) for i in range(4)])
+
+
+def ordered(index, own, other):
+    both = jnp.stack([own, other])
+    return jnp.where(index == 0, both, both[::-1])
 
 
 def mm(a, b):
@@ -115,8 +120,13 @@
     rights = jnp.einsum(
         "qr,mlr->qlm", pick, upper, preferred_element_type=F32
     ).astype(BF16)
-    theirs = swapped(rights[16:], "zl")
-    mine = rights[:16]
+    theirs = swapped(
+        jnp.concatenate([rights[16:].reshape(64, 128), isometry], axis=0), "zl"
+    )
+    rights = ordered(zl, rights[:16], theirs[:64].reshape(16, 4, 128))
+    rights = rights.transpose(1, 2, 0, 3)
+    slabs = ordered(zl, isometry, theirs[64:]).reshape(2, 4, 2, 4, 4, 128)
+    ks = slabs.transpose(1, 3, 0, 2, 4, 5)
 
     l00 = lower.transpose(1, 2, 0, 3)
     l01 = swapped(l00, "zh")
@@ -124,25 +134,23 @@
     l11 = both_swapped(l00)
     lowers = (l00, l01, l10, l11)
 
-    first = jnp.where(zl == 0, mine, theirs)
-    second = jnp.where(zl == 0, theirs, mine)
-    rights = jnp.concatenate([first, second], axis=1)
-    ks = isometry.reshape(4, 2, 4, 4, 128).transpose(0, 2, 1, 3, 4)
     send = jnp.concatenate(
         [
             jnp.broadcast_to(rights.reshape(1, 128, 128), (16, 128, 128)),
             jnp.broadcast_to(isometry[None], (16, 128, 128)),
-            ks.reshape(16, 8, 128),
+            ks.reshape(16, 16, 128),
         ],
         axis=1,
     )
     got = lax.all_to_all(send, ("x", "y"), 0, 0, tiled=True)
+    got, *lowers = lax.optimization_barrier((got, *lowers))
     u = got[:, :128].reshape(16, 16, 8, 128).transpose(1, 0, 2, 3).reshape(16, 128, 128)
     wr = got[:, 128:256]
     u_other, wr_other = swapped(u, "c"), swapped(wr, "c")
 
-    w = from_everyone(got[:, 256:], ("zl", "zh", "c"), 8)
-    w = w.transpose(2, 1, 0, 3).reshape(8, 128, 128)
+    mine = got[:, 256:].reshape(16, 2, 8, 128).transpose(1, 2, 0, 3)
+    w = from_everyone(mine, ("zh", "c"), 4).reshape(8, 8, 16, 128)
+    w = w.transpose(1, 2, 0, 3).reshape(8, 128, 128)
 
     here = (zl.astype(jnp.int32)[None], zh.astype(jnp.int32)[None])
     acc = contract(*here, w, (u, u_other), (wr, wr_other), lowers)

time: 76.5 us -> 72.1 us (0.942)
  blocking collectives: 54.3 us -> 28.8 us
  waiting for transfers between devices: 0.96 us -> 13.4 us
  starting transfers between devices: 8.19 us -> 15.6 us
  other arithmetic: 0.18 us -> 2.73 us
  local copies, waits for them, and re-layouts: 3.88 us -> 2.53 us
    all_to_all x1 -> x0, blocking collectives: 23.6 us -> none  [on_device(): got = lax.all_to_all(send, ('x', 'y'), 0, 0, tiled=True)]
    all_to_all x0 -> x1, starting transfers between devices: none -> 7.27 us  [on_device(): got = lax.all_to_all(send, ('x', 'y'), 0, 0, tiled=True)]
    ppermute x5, waiting for transfers between devices: 0.96 us -> 7.67 us  [swapped(): return lax.ppermute(value, axis, [(0, 1), (1, 0)])]
    ppermute x1, waiting for transfers between devices: 0.01 us -> 4.61 us  [both_swapped(): return lax.ppermute(value, ('zl', 'zh'), [(i, 3 - i) for i in range(4)])]
    all_to_all x1, blocking collectives: 14.8 us -> 12.1 us  [from_everyone(): lax.all_to_all(jnp.broadcast_to(value[None], (peers, *value.shape)), axes...]
    all_to_all x0 -> x1, waiting for transfers between devices: none -> 1.13 us  [on_device(): got = lax.all_to_all(send, ('x', 'y'), 0, 0, tiled=True)]
    concatenate x1, other arithmetic: 0.08 us -> 1.08 us  [on_device(): jnp.concatenate([jnp.broadcast_to(rights.reshape(1, 128, 128), (16, 128,...]
    another operation x0 -> x2, other arithmetic: none -> 0.78 us  [ordered(): both = jnp.stack([own, other])]
  transfers between devices with their start and end apart: 6 -> 7, of which waited for: 1 -> 5; matrix products, arithmetic and copies ran while one was open for 1% -> 1% of each run, Pallas kernels for 0% -> 0%
where the time goes in v4:
time: 72.1 us; the launch traced here: 71.6 us
  blocking collectives  28.8 us (40%)
  starting transfers between devices  15.6 us (22%)
  waiting for transfers between devices  13.4 us (19%)
  Pallas kernels  8.29 us (11%)
  other arithmetic  2.73 us (4%)
  local copies, waits for them, and re-layouts  2.53 us (4%)
    all_to_all x1, blocking collectives, on_device(): parts = lax.all_to_all(parts, ('x', 'zl', 'y', 'zh'), 0, 0, tiled=True)  16.7 us
    all_to_all x1, blocking collectives, from_everyone(): lax.all_to_all(jnp.broadcast_to(value[None], (peers, *value.shape)), axes...  12.1 us
    pallas_call x1, Pallas kernels, contract(): pl.pallas_call(step_kernel, in_specs=[pl.BlockSpec(memory_space=pltpu.SME...  8.29 us
    ppermute x5, waiting for transfers between devices, swapped(): return lax.ppermute(value, axis, [(0, 1), (1, 0)])  7.67 us
    all_to_all x1, starting transfers between devices, on_device(): got = lax.all_to_all(send, ('x', 'y'), 0, 0, tiled=True)  7.27 us
    ppermute x1, waiting for transfers between devices, both_swapped(): return lax.ppermute(value, ('zl', 'zh'), [(i, 3 - i) for i in range(4)])  4.61 us
    ppermute x5, starting transfers between devices, swapped(): return lax.ppermute(value, axis, [(0, 1), (1, 0)])  4.17 us
    ppermute x1, starting transfers between devices, both_swapped(): return lax.ppermute(value, ('zl', 'zh'), [(i, 3 - i) for i in range(4)])  4.12 us
  transfers between devices with their start and end apart: 7, of which 5 were waited for; matrix products, arithmetic and copies ran while one was open for 1% of the time, Pallas kernels for 0%

profile of v4, /device:TPU:0, one launch (start us, length us, event | category | flops | bytes accessed | tf_op | source)
XLA Modules:
  0.0 71.6 jit_solution(4457092633850398509)
XLA Ops:
  0.0 0.0 copy-start
  0.0 0.9 %copy-done = bf16[128,4,128]{2,1,0:T(4,128)(2,1)S(1)} copy-done((bf16[128,4,128]{2,1,0:T(4,128)(2,1)S(1)}, bf16[128,4,128]{2,1,0:T(4,128)(2,1)}, u32[]{:S(2)}) %copy-start) | copy-done | bytes 131096
  0.9 0.2 fusion
  1.1 0.8 %pad_maximum_fusion.2 = bf16[192,128]{1,0:T(8,128)(2,1)S(1)} fusion(bf16[128,128]{1,0:T(8,128)(2,1)} %param.5, bf16[64,128]{1,0:T(8,128)(2,1)S(1)} %bitcast.63), kind=kLoop, calls=%fused_computation.11 | loop fusion | flops 98304 | bytes 98304 | tf_op jit(solution)/shard_map/concatenate | solution.py:124
  1.9 2.0 %collective-permute-start = (bf16[192,128]{1,0:T(8,128)(2,1)S(1)}, bf16[192,128]{1,0:T(8,128)(2,1)S(1)}, u32[]{:S(2)}, u32[]{:S(2)}) collective-permute-start(bf16[192,128]{1,0:T(8,128)(2,1)S(1)} %pad_maximum_fusion.2), channel_id=1, source_target_pairs={{0,16},{16,0},{1,17},{17,1},{2,18},{18,2},{3,19},{19,3},{4,20},{20... | collective-permute-start | bytes 147464 | tf_op jit(solution)/shard_map/ppermute | solution.py:21
  3.9 2.1 %collective-permute-done = bf16[192,128]{1,0:T(8,128)(2,1)S(1)} collective-permute-done((bf16[192,128]{1,0:T(8,128)(2,1)S(1)}, bf16[192,128]{1,0:T(8,128)(2,1)S(1)}, u32[]{:S(2)}, u32[]{:S(2)}) %collective-permute-start) | collective-permute-done | bytes 49184 | tf_op jit(solution)/shard_map/ppermute | solution.py:21
  6.1 0.8 %pad_maximum_fusion.1 = bf16[2,128,128]{2,1,0:T(8,128)(2,1)S(1)} fusion(bf16[1,128,128]{2,1,0:T(8,128)(2,1)S(1)} %slice_bitcast_fusion.2, bf16[1,128,128]{2,1,0:T(8,128)(2,1)} %bitcast.58), kind=kLoop, calls=%fused_computation.9 | loop fusion | flops 32768 | bytes 131072 | tf_op jit(solution)/shard_map/stack | solution.py:29
  6.9 0.1 broadcast_in_dim.42
  7.0 0.1 broadcast_in_dim.43
  7.1 1.1 %pad_maximum_fusion = bf16[16,272,128]{2,1,0:T(8,128)(2,1)} fusion(bf16[16,16,128]{2,1,0:T(8,128)(2,1)S(1)} %bitcast.59, bf16[16,128,128]{2,1,0:T(8,128)(2,1)S(1)} %broadcast_in_dim.43, bf16[16,128,128]{2,1,0:T(8,128)(2,1)S(1)} %broadcast_in_dim.42), kind=kLoop, calls=%fused_computation.1 | loop fusion | flops 3342336 | bytes 2228224 | tf_op jit(solution)/shard_map/concatenate | solution.py:137
  8.2 7.3 %all-to-all-start = ((bf16[16,272,128]{2,1,0:T(8,128)(2,1)}), bf16[16,272,128]{2,1,0:T(8,128)(2,1)S(1)}, u32[]{:S(2)}, u32[]{:S(2)}) async-start(bf16[16,272,128]{2,1,0:T(8,128)(2,1)} %pad_maximum_fusion), calls=%async_computation | async-start | bytes 2228224 | tf_op jit(solution)/shard_map/all_to_all | solution.py:145
  15.5 4.1 %collective-permute-start.3 = (bf16[4,2,128,128]{3,2,1,0:T(8,128)(2,1)S(1)}, bf16[4,2,128,128]{3,2,1,0:T(8,128)(2,1)S(1)}, u32[]{:S(2)}, u32[]{:S(2)}) collective-permute-start(bf16[4,2,128,128]{3,2,1,0:T(8,128)(2,1)S(1)} %bitcast.50), channel_id=1, source_target_pairs={{0,18},{2,16},{16,2},{18,0},{1,19},{3,17},{17,3},{19,1},{4,22},{6,... | collective-permute-start | bytes 786440 | tf_op jit(solution)/shard_map/ppermute | solution.py:25
  19.7 0.0 collective-permute-start.2
  19.7 1.6 %collective-permute-start.1 = (bf16[4,2,128,128]{3,2,1,0:T(8,128)(2,1)S(1)}, bf16[4,2,128,128]{3,2,1,0:T(8,128)(2,1)S(1)}, u32[]{:S(2)}, u32[]{:S(2)}) collective-permute-start(bf16[4,2,128,128]{3,2,1,0:T(8,128)(2,1)S(1)} %bitcast.52), channel_id=1, source_target_pairs={{0,2},{2,0},{1,3},{3,1},{4,6},{6,4},{5,7},{7,5},{8,10},{10,8},{9,1... | collective-permute-start | bytes 786440 | tf_op jit(solution)/shard_map/ppermute | solution.py:21
  21.2 4.6 %collective-permute-done.3.l11 = bf16[4,2,128,128]{3,2,1,0:T(8,128)(2,1)S(1)} collective-permute-done((bf16[4,2,128,128]{3,2,1,0:T(8,128)(2,1)S(1)}, bf16[4,2,128,128]{3,2,1,0:T(8,128)(2,1)S(1)}, u32[]{:S(2)}, u32[]{:S(2)}) %collective-permute-start.3) | collective-permute-done | bytes 262176 | tf_op jit(solution)/shard_map/ppermute | solution.py:25
  25.8 3.0 %collective-permute-done.2.l10 = bf16[4,2,128,128]{3,2,1,0:T(8,128)(2,1)S(1)} collective-permute-done((bf16[4,2,128,128]{3,2,1,0:T(8,128)(2,1)S(1)}, bf16[4,2,128,128]{3,2,1,0:T(8,128)(2,1)S(1)}, u32[]{:S(2)}, u32[]{:S(2)}) %collective-permute-start.2) | collective-permute-done | bytes 262176 | tf_op jit(solution)/shard_map/ppermute | solution.py:21
  28.8 2.6 %collective-permute-done.1.l01 = bf16[4,2,128,128]{3,2,1,0:T(8,128)(2,1)S(1)} collective-permute-done((bf16[4,2,128,128]{3,2,1,0:T(8,128)(2,1)S(1)}, bf16[4,2,128,128]{3,2,1,0:T(8,128)(2,1)S(1)}, u32[]{:S(2)}, u32[]{:S(2)}) %collective-permute-start.1) | collective-permute-done | bytes 262176 | tf_op jit(solution)/shard_map/ppermute | solution.py:21
  31.4 1.1 %all-to-all-done = bf16[16,272,128]{2,1,0:T(8,128)(2,1)S(1)} async-done(((bf16[16,272,128]{2,1,0:T(8,128)(2,1)}), bf16[16,272,128]{2,1,0:T(8,128)(2,1)S(1)}, u32[]{:S(2)}, u32[]{:S(2)}) %all-to-all-start) | async-done | bytes 1114144 | tf_op jit(solution)/shard_map/all_to_all | solution.py:145
  32.5 0.1 fusion.9
  32.7 0.1 copy.46
  32.8 0.1 collective-permute-start.4
  32.9 0.5 collective-permute-start.5
  33.4 0.1 copy.35
  33.5 0.2 broadcast_in_dim.45
  33.6 12.1 %all_to_all.15 = bf16[4,2,8,16,128]{4,1,3,2,0:T(2,128)(2,1)S(1)} all-to-all(bf16[4,2,8,16,128]{4,1,3,2,0:T(2,128)(2,1)S(1)} %broadcast_in_dim.45), channel_id=1, replica_groups=mesh['x'=4,'zl'=2,'y'=4,'zh'=2,'c'=2] {'zh','c'}, dimensions={0} | all-to-all | bytes 524288 | tf_op jit(solution)/shard_map/all_to_all | solution.py:15
  45.8 0.2 copy.47
  46.0 0.0 collective-permute-done.4.u1
  46.0 0.0 collective-permute-done.5.wr1
  46.0 8.3 %contract.1 = f32[2,2,128,128]{3,2,1,0:T(8,128)S(1)} custom-call(s32[1]{0:T(128)} %bitcast.zl_ref, s32[1]{0:T(128)} %bitcast.1.zh_ref, bf16[8,128,128]{2,1,0:T(8,128)(2,1)S(1)} %bitcast.54, bf16[16,128,128]{2,1,0:T(8,128)(2,1)S(1)} %bitcast.49, bf16[16,128,128]{2,1,0:T(8,128)(2,1)S(1)} %collective-permute-done.4.u1, ...), custom_call_target="tpu_custom_call" | custom-call | flops 8000000000 | bytes 6291456 | tf_op jit(solution)/shard_map/contract/pallas_call | solution.py:96
  54.3 16.7 %all_to_all.16 = f32[64,8,128]{2,1,0:T(8,128)S(1)} all-to-all(f32[64,8,128]{2,1,0:T(8,128)S(1)} %bitcast.57), channel_id=1, replica_groups=mesh['x'=4,'zl'=2,'y'=4,'zh'=2,'c'=2] {'x','zl','y','zh'}, dimensions={0} | all-to-all | bytes 524288 | tf_op jit(solution)/shard_map/all_to_all | solution.py:159
  71.0 0.1 reduce_sum.9
  71.0 0.6 copy.40
  (19 shorter events, 0.3 us)
Async XLA Ops:
  0.0 0.9 %copy-start = (bf16[128,4,128]{2,1,0:T(4,128)(2,1)S(1)}, bf16[128,4,128]{2,1,0:T(4,128)(2,1)}, u32[]{:S(2)}) copy-start(bf16[128,4,128]{2,1,0:T(4,128)(2,1)} %param.3) | copy-start | bytes 393220
  0.0 7.0 %copy-start.1 = (bf16[128,128]{1,0:T(8,128)(2,1)S(1)}, bf16[128,128]{1,0:T(8,128)(2,1)}, u32[]{:S(2)}) copy-start(bf16[128,128]{1,0:T(8,128)(2,1)} %param.5) | copy-start | bytes 98308
  1.9 4.1 %collective-permute-start = (bf16[192,128]{1,0:T(8,128)(2,1)S(1)}, bf16[192,128]{1,0:T(8,128)(2,1)S(1)}, u32[]{:S(2)}, u32[]{:S(2)}) collective-permute-start(bf16[192,128]{1,0:T(8,128)(2,1)S(1)} %pad_maximum_fusion.2), channel_id=1, source_target_pairs={{0,16},{16,0},{1,17},{17,1},{2,18},{18,2},{3,19},{19,3},{4,20},{20... | collective-permute-start | bytes 147464 | tf_op jit(solution)/shard_map/ppermute | solution.py:21
  8.2 7.3 %copy-start.2 = (bf16[128,4,2,128]{3,2,1,0:T(2,128)(2,1)S(1)}, bf16[128,4,2,128]{3,2,1,0:T(2,128)(2,1)}, u32[]{:S(2)}) copy-start(bf16[128,4,2,128]{3,2,1,0:T(2,128)(2,1)} %param.4) | copy-start | bytes 786436
  8.2 24.3 %all-to-all-start = ((bf16[16,272,128]{2,1,0:T(8,128)(2,1)}), bf16[16,272,128]{2,1,0:T(8,128)(2,1)S(1)}, u32[]{:S(2)}, u32[]{:S(2)}) async-start(bf16[16,272,128]{2,1,0:T(8,128)(2,1)} %pad_maximum_fusion), calls=%async_computation | async-start | bytes 2228224 | tf_op jit(solution)/shard_map/all_to_all | solution.py:145
  15.5 10.3 %collective-permute-start.3 = (bf16[4,2,128,128]{3,2,1,0:T(8,128)(2,1)S(1)}, bf16[4,2,128,128]{3,2,1,0:T(8,128)(2,1)S(1)}, u32[]{:S(2)}, u32[]{:S(2)}) collective-permute-start(bf16[4,2,128,128]{3,2,1,0:T(8,128)(2,1)S(1)} %bitcast.50), channel_id=1, source_target_pairs={{0,18},{2,16},{16,2},{18,0},{1,19},{3,17},{17,3},{19,1},{4,22},{6,... | collective-permute-start | bytes 786440 | tf_op jit(solution)/shard_map/ppermute | solution.py:25
  19.7 9.1 %collective-permute-start.2 = (bf16[4,2,128,128]{3,2,1,0:T(8,128)(2,1)S(1)}, bf16[4,2,128,128]{3,2,1,0:T(8,128)(2,1)S(1)}, u32[]{:S(2)}, u32[]{:S(2)}) collective-permute-start(bf16[4,2,128,128]{3,2,1,0:T(8,128)(2,1)S(1)} %bitcast.51), channel_id=1, source_target_pairs={{0,16},{16,0},{1,17},{17,1},{2,18},{18,2},{3,19},{19,3},{4,20},{20... | collective-permute-start | bytes 786440 | tf_op jit(solution)/shard_map/ppermute | solution.py:21
  19.7 11.8 %collective-permute-start.1 = (bf16[4,2,128,128]{3,2,1,0:T(8,128)(2,1)S(1)}, bf16[4,2,128,128]{3,2,1,0:T(8,128)(2,1)S(1)}, u32[]{:S(2)}, u32[]{:S(2)}) collective-permute-start(bf16[4,2,128,128]{3,2,1,0:T(8,128)(2,1)S(1)} %bitcast.52), channel_id=1, source_target_pairs={{0,2},{2,0},{1,3},{3,1},{4,6},{6,4},{5,7},{7,5},{8,10},{10,8},{9,1... | collective-permute-start | bytes 786440 | tf_op jit(solution)/shard_map/ppermute | solution.py:21
  32.8 13.1 %collective-permute-start.4 = (bf16[16,128,128]{2,1,0:T(8,128)(2,1)S(1)}, bf16[16,128,128]{2,1,0:T(8,128)(2,1)S(1)}, u32[]{:S(2)}, u32[]{:S(2)}) collective-permute-start(bf16[16,128,128]{2,1,0:T(8,128)(2,1)S(1)} %bitcast.48), channel_id=1, source_target_pairs={{0,1},{1,0},{2,3},{3,2},{4,5},{5,4},{6,7},{7,6},{8,9},{9,8},{10,11... | collective-permute-start | bytes 1572872 | tf_op jit(solution)/shard_map/ppermute | solution.py:21
  32.9 13.1 %collective-permute-start.5 = (bf16[16,128,128]{2,1,0:T(8,128)(2,1)S(1)}, bf16[16,128,128]{2,1,0:T(8,128)(2,1)S(1)}, u32[]{:S(2)}, u32[]{:S(2)}) collective-permute-start(bf16[16,128,128]{2,1,0:T(8,128)(2,1)S(1)} %get-tuple-element.15.wr0), channel_id=1, source_target_pairs={{0,1},{1,0},{2,3},{3,2},{4,5},{5,4},{6,7},{7,6},{8,9},{9,8},{10,11... | collective-permute-start | bytes 1572872 | tf_op jit(solution)/shard_map/ppermute | solution.py:21

commit v5 on v1

--- a/solution.py
+++ b/solution.py
@@ -113,6 +113,10 @@
     zh = lax.axis_index("zh")
     c = lax.axis_index("c")
 
+    lower = lower.transpose(1, 2, 0, 3)
+    pair = ordered(c, isometry, swapped(isometry, "c"))
+    upper, lower = lax.optimization_barrier((upper, lower))
+
     t = jnp.arange(32)
     plane = jnp.where(t < 16, zl, 1 - zl)
     xy = t % 16
@@ -121,23 +125,22 @@
     rights = jnp.einsum(
         "qr,mlr->qlm", pick, upper, preferred_element_type=F32
     ).astype(BF16)
-    mine, theirs = rights[:16], swapped(rights[16:], "zl")
 
-    pair = ordered(c, isometry, swapped(isometry, "c"))
-    others = [swapped(pair, "zh"), swapped(pair, "zl"), both_swapped(pair)]
-    planes = [ordered(zh, pair, others[0]), ordered(zh, *others[1:])]
-    column = ordered(zl, *planes).reshape(8, 4, 2, 4, 4, 128)
+    theirs = swapped(
+        jnp.concatenate([rights[16:].reshape(64, 128), pair.reshape(256, 128)]), "zl"
+    )
+    far = swapped(pair, "zh"), both_swapped(pair)
+    own = ordered(zh, pair, far[0])
+    other = ordered(zh, theirs[64:].reshape(2, 128, 128), far[1])
+    column = ordered(zl, own, other).reshape(8, 4, 2, 4, 4, 128)
     ks = column.transpose(1, 3, 2, 4, 0, 5)
     ks = jnp.where(zl == 0, ks, ks[:, :, ::-1])
 
-    l00 = lower.transpose(1, 2, 0, 3)
-    l01 = swapped(l00, "zh")
-    l10 = swapped(l00, "zl")
-    l11 = both_swapped(l00)
-    lowers = (l00, l01, l10, l11)
+    lowers = (lower, swapped(lower, "zh"), swapped(lower, "zl"), both_swapped(lower))
 
-    first = jnp.where(zl == 0, mine, theirs)
-    second = jnp.where(zl == 0, theirs, mine)
+    theirs = theirs[:64].reshape(16, 4, 128)
+    first = jnp.where(zl == 0, rights[:16], theirs)
+    second = jnp.where(zl == 0, theirs, rights[:16])
     rights = jnp.concatenate([first, second], axis=1)
     send = jnp.concatenate(
         [

time: 69.5 us -> 69.4 us (level)
  starting transfers between devices: 20.5 us -> 17.1 us
  blocking collectives: 15.6 us -> 17 us
  waiting for transfers between devices: 19.2 us -> 20.1 us
  matrix products: 0.18 us -> 1.08 us
    ppermute x8 -> x7, starting transfers between devices: 7.13 us -> 4.12 us  [swapped(): return lax.ppermute(value, axis, [(0, 1), (1, 0)])]
    all_to_all x1, waiting for transfers between devices: 13.3 us -> 14.6 us  [on_device(): got = lax.all_to_all(send, ('x', 'y'), 0, 0, tiled=True)]
    all_to_all x1, blocking collectives: 15.6 us -> 17 us  [on_device(): parts = lax.all_to_all(parts, ('x', 'zl', 'y', 'zh'), 0, 0, tiled=True)]
    dot_general x1, matrix products: 0.18 us -> 1.08 us  [on_device(): jnp.einsum('qr,mlr->qlm', pick, upper, preferred_element_type=F32)]
    ppermute x8 -> x7, waiting for transfers between devices: 5.2 us -> 5.42 us  [swapped(): return lax.ppermute(value, axis, [(0, 1), (1, 0)])]
  transfers between devices with their start and end apart: 11 -> 10, of which waited for: 5 -> 2; matrix products, arithmetic and copies ran while one was open for 1% -> 4% of each run, Pallas kernels for 6% -> 6%
where the time goes in v5:
time: 69.4 us; the launch traced here: 69 us
  waiting for transfers between devices  20.1 us (29%)
  starting transfers between devices  17.1 us (25%)
  blocking collectives  17 us (24%)
  Pallas kernels  8.6 us (12%)
  local copies, waits for them, and re-layouts  2.58 us (4%)
  other arithmetic  2.33 us (3%)
  matrix products  1.08 us (2%)
    all_to_all x1, blocking collectives, on_device(): parts = lax.all_to_all(parts, ('x', 'zl', 'y', 'zh'), 0, 0, tiled=True)  17 us
    all_to_all x1, waiting for transfers between devices, on_device(): got = lax.all_to_all(send, ('x', 'y'), 0, 0, tiled=True)  14.6 us
    pallas_call x2, Pallas kernels, contract(): pl.pallas_call(body, in_specs=[pl.BlockSpec(memory_space=pltpu.SMEM)] + [...  8.6 us
    all_to_all x1, starting transfers between devices, on_device(): got = lax.all_to_all(send, ('x', 'y'), 0, 0, tiled=True)  7.03 us
    ppermute x2, starting transfers between devices, both_swapped(): return lax.ppermute(value, ('zl', 'zh'), [(i, 3 - i) for i in range(4)])  5.97 us
    ppermute x7, waiting for transfers between devices, swapped(): return lax.ppermute(value, axis, [(0, 1), (1, 0)])  5.42 us
    ppermute x7, starting transfers between devices, swapped(): return lax.ppermute(value, axis, [(0, 1), (1, 0)])  4.12 us
  transfers between devices with their start and end apart: 10, of which 2 were waited for; matrix products, arithmetic and copies ran while one was open for 4% of the time, Pallas kernels for 6%

profile of v5, /device:TPU:0, one launch (start us, length us, event | category | flops | bytes accessed | tf_op | source)
XLA Modules:
  0.0 69.0 jit_solution(16097808622731784311)
XLA Ops:
  0.0 0.0 collective-permute-start
  0.0 1.0 %copy.30 = bf16[128,4,2,128]{3,0,2,1:T(8,128)(2,1)S(1)} copy(bf16[128,4,2,128]{3,2,1,0:T(2,128)(2,1)} %param.4) | data formatting | bytes 524288 | tf_op args[1]
  1.0 1.1 %fusion = bf16[32,4,128]{2,0,1:T(8,128)(2,1)S(1)} fusion(bf16[128,4,128]{2,1,0:T(4,128)(2,1)} %param.3, s32[32]{0:T(128)S(1)} %add_add_fusion), kind=kOutput, calls=%fused_computation.2 | convolution fusion | flops 4214784 | bytes 163968 | tf_op jit(solution)/shard_map/qr,mlr->qlm/dot_general | solution.py:125
  2.1 0.0 collective-permute-done
  2.2 0.8 %pad_maximum_fusion.5 = bf16[2,128,128]{2,1,0:T(8,128)(2,1)S(1)} fusion(bf16[1,128,128]{2,1,0:T(8,128)(2,1)S(1)} %bitcast.64, bf16[1,128,128]{2,1,0:T(8,128)(2,1)} %bitcast.59), kind=kLoop, calls=%fused_computation.20 | loop fusion | flops 32768 | bytes 131072 | tf_op jit(solution)/shard_map/stack | solution.py:23
  2.9 4.2 %collective-permute-start.3 = (bf16[2,128,128]{2,1,0:T(8,128)(2,1)S(1)}, bf16[2,128,128]{2,1,0:T(8,128)(2,1)S(1)}, u32[]{:S(2)}, u32[]{:S(2)}) collective-permute-start(bf16[2,128,128]{2,1,0:T(8,128)(2,1)S(1)} %reverse_select_fusion.4), channel_id=1, source_target_pairs={{0,18},{2,16},{16,2},{18,0},{1,19},{3,17},{17,3},{19,1},{4,22},{6,... | collective-permute-start | bytes 196616 | tf_op jit(solution)/shard_map/ppermute | solution.py:19
  7.2 1.0 %collective-permute-start.1 = (bf16[320,128]{1,0:T(8,128)(2,1)S(1)}, bf16[320,128]{1,0:T(8,128)(2,1)S(1)}, u32[]{:S(2)}, u32[]{:S(2)}) collective-permute-start(bf16[320,128]{1,0:T(8,128)(2,1)S(1)} %pad_maximum_fusion.4), channel_id=1, source_target_pairs={{0,16},{16,0},{1,17},{17,1},{2,18},{18,2},{3,19},{19,3},{4,20},{20... | collective-permute-start | bytes 245768 | tf_op jit(solution)/shard_map/ppermute | solution.py:15
  8.2 5.4 %collective-permute-done.2 = bf16[2,128,128]{2,1,0:T(8,128)(2,1)S(1)} collective-permute-done((bf16[2,128,128]{2,1,0:T(8,128)(2,1)S(1)}, bf16[2,128,128]{2,1,0:T(8,128)(2,1)S(1)}, u32[]{:S(2)}, u32[]{:S(2)}) %collective-permute-start.2) | collective-permute-done | bytes 65568 | tf_op jit(solution)/shard_map/ppermute | solution.py:15
  13.9 0.0 copy-start
  13.9 0.1 reverse_select_fusion.1
  14.0 0.3 copy.29
  14.3 0.1 reverse_select_fusion
  14.4 0.1 broadcast_in_dim.30
  14.5 0.2 copy-done
  14.6 0.1 broadcast_in_dim.31
  14.7 1.2 %pad_maximum_fusion = bf16[16,320,128]{2,1,0:T(8,128)(2,1)} fusion(bf16[16,128,128]{2,1,0:T(8,128)(2,1)S(1)} %broadcast_in_dim.31, bf16[16,64,128]{2,1,0:T(8,128)(2,1)S(1)} %bitcast.52, bf16[16,128,128]{2,1,0:T(8,128)(2,1)S(1)} %broadcast_in_dim.30), kind=kLoop, calls=%fused_computation | loop fusion | flops 3932160 | bytes 2621440 | tf_op jit(solution)/shard_map/concatenate | solution.py:145
  15.9 7.0 %all-to-all-start = ((bf16[16,320,128]{2,1,0:T(8,128)(2,1)}), bf16[16,320,128]{2,1,0:T(8,128)(2,1)S(1)}, u32[]{:S(2)}, u32[]{:S(2)}) async-start(bf16[16,320,128]{2,1,0:T(8,128)(2,1)} %pad_maximum_fusion), calls=%async_computation | async-start | bytes 2621440 | tf_op jit(solution)/shard_map/all_to_all | solution.py:153
  22.9 1.6 %collective-permute-start.6 = (bf16[4,2,128,128]{3,2,1,0:T(8,128)(2,1)S(1)}, bf16[4,2,128,128]{3,2,1,0:T(8,128)(2,1)S(1)}, u32[]{:S(2)}, u32[]{:S(2)}) collective-permute-start(bf16[4,2,128,128]{3,2,1,0:T(8,128)(2,1)S(1)} %bitcast.46), channel_id=1, source_target_pairs={{0,2},{2,0},{1,3},{3,1},{4,6},{6,4},{5,7},{7,5},{8,10},{10,8},{9,1... | collective-permute-start | bytes 786440 | tf_op jit(solution)/shard_map/ppermute | solution.py:15
  24.6 0.8 %collective-permute-start.7 = (bf16[4,2,128,128]{3,2,1,0:T(8,128)(2,1)S(1)}, bf16[4,2,128,128]{3,2,1,0:T(8,128)(2,1)S(1)}, u32[]{:S(2)}, u32[]{:S(2)}) collective-permute-start(bf16[4,2,128,128]{3,2,1,0:T(8,128)(2,1)S(1)} %bitcast.47), channel_id=1, source_target_pairs={{0,16},{16,0},{1,17},{17,1},{2,18},{18,2},{3,19},{19,3},{4,20},{20... | collective-permute-start | bytes 786440 | tf_op jit(solution)/shard_map/ppermute | solution.py:15
  25.4 1.7 %collective-permute-start.8 = (bf16[4,2,128,128]{3,2,1,0:T(8,128)(2,1)S(1)}, bf16[4,2,128,128]{3,2,1,0:T(8,128)(2,1)S(1)}, u32[]{:S(2)}, u32[]{:S(2)}) collective-permute-start(bf16[4,2,128,128]{3,2,1,0:T(8,128)(2,1)S(1)} %bitcast.48), channel_id=1, source_target_pairs={{0,18},{2,16},{16,2},{18,0},{1,19},{3,17},{17,3},{19,1},{4,22},{6,... | collective-permute-start | bytes 786440 | tf_op jit(solution)/shard_map/ppermute | solution.py:19
  27.1 14.6 %all-to-all-done = bf16[16,320,128]{2,1,0:T(8,128)(2,1)S(1)} async-done(((bf16[16,320,128]{2,1,0:T(8,128)(2,1)}), bf16[16,320,128]{2,1,0:T(8,128)(2,1)S(1)}, u32[]{:S(2)}, u32[]{:S(2)}) %all-to-all-start) | async-done | bytes 1310752 | tf_op jit(solution)/shard_map/all_to_all | solution.py:153
  41.8 0.1 slice_bitcast_fusion
  41.8 0.1 copy_bitcast_fusion.refs_2_
  41.9 0.1 collective-permute-start.4
  42.1 0.6 collective-permute-start.5
  42.7 0.0 collective-permute-done.6.refs_5_.l01
  42.7 0.0 collective-permute-done.8.refs_7_.l11
  42.7 4.4 %contract.2.acc_ref = f32[2,2,128,128]{3,2,1,0:T(8,128)S(1)} custom-call(s32[1]{0:T(128)} %bitcast.refs_0_.zh_ref, bf16[8,128,128]{2,1,0:T(8,128)(2,1)S(1)} %copy_bitcast_fusion.1.refs_1_.w_ref, bf16[16,128,128]{2,1,0:T(8,128)(2,1)S(1)} %copy_bitcast_fusion.refs_2_, bf16[16,128,128]{2,1,0:T(8,128)(2,1)S(1)} %slice.48.refs_3_, ...), custom_call_target="tpu_custom_call" | custom-call | flops 4000000000 | bytes 4194304 | tf_op jit(solution)/shard_map/contract/pallas_call | solution.py:97
  47.1 4.2 %contract.3 = f32[2,2,128,128]{3,2,1,0:T(8,128)S(1)} custom-call(s32[1]{0:T(128)} %bitcast.refs_0_.zh_ref, bf16[8,128,128]{2,1,0:T(8,128)(2,1)S(1)} %copy_bitcast_fusion.1.refs_1_.w_ref, bf16[16,128,128]{2,1,0:T(8,128)(2,1)S(1)} %collective-permute-done.4.u_ref, bf16[16,128,128]{2,1,0:T(8,128)(2,1)S(1)} %collective-permute-done.5.wr_ref, ...), custom_call_target="tpu_custom_call" | custom-call | flops 4000000000 | bytes 4194304 | tf_op jit(solution)/shard_map/contract/pallas_call | solution.py:97
  51.4 17.0 %all_to_all.10 = f32[64,8,128]{2,1,0:T(8,128)S(1)} all-to-all(f32[64,8,128]{2,1,0:T(8,128)S(1)} %bitcast.55), channel_id=1, replica_groups=mesh['x'=4,'zl'=2,'y'=4,'zh'=2,'c'=2] {'x','zl','y','zh'}, dimensions={0} | all-to-all | bytes 524288 | tf_op jit(solution)/shard_map/all_to_all | solution.py:164
  68.4 0.1 reduce_sum.9
  68.4 0.6 copy.19
  (25 shorter events, 0.4 us)
Async XLA Ops:
  0.0 2.1 %collective-permute-start = (bf16[128,128]{1,0:T(8,128)(2,1)}, bf16[128,128]{1,0:T(8,128)(2,1)S(1)}, u32[]{:S(2)}, u32[]{:S(2)}) collective-permute-start(bf16[128,128]{1,0:T(8,128)(2,1)} %param.5), channel_id=1, source_target_pairs={{0,1},{1,0},{2,3},{3,2},{4,5},{5,4},{6,7},{7,6},{8,9},{9,8},{10,11... | collective-permute-start | bytes 98312 | tf_op jit(solution)/shard_map/ppermute | solution.py:15
  2.9 10.8 %collective-permute-start.3 = (bf16[2,128,128]{2,1,0:T(8,128)(2,1)S(1)}, bf16[2,128,128]{2,1,0:T(8,128)(2,1)S(1)}, u32[]{:S(2)}, u32[]{:S(2)}) collective-permute-start(bf16[2,128,128]{2,1,0:T(8,128)(2,1)S(1)} %reverse_select_fusion.4), channel_id=1, source_target_pairs={{0,18},{2,16},{16,2},{18,0},{1,19},{3,17},{17,3},{19,1},{4,22},{6,... | collective-permute-start | bytes 196616 | tf_op jit(solution)/shard_map/ppermute | solution.py:19
  7.2 6.5 %collective-permute-start.2 = (bf16[2,128,128]{2,1,0:T(8,128)(2,1)S(1)}, bf16[2,128,128]{2,1,0:T(8,128)(2,1)S(1)}, u32[]{:S(2)}, u32[]{:S(2)}) collective-permute-start(bf16[2,128,128]{2,1,0:T(8,128)(2,1)S(1)} %reverse_select_fusion.4), channel_id=1, source_target_pairs={{0,2},{2,0},{1,3},{3,1},{4,6},{6,4},{5,7},{7,5},{8,10},{10,8},{9,1... | collective-permute-start | bytes 196616 | tf_op jit(solution)/shard_map/ppermute | solution.py:15
  7.2 6.5 %collective-permute-start.1 = (bf16[320,128]{1,0:T(8,128)(2,1)S(1)}, bf16[320,128]{1,0:T(8,128)(2,1)S(1)}, u32[]{:S(2)}, u32[]{:S(2)}) collective-permute-start(bf16[320,128]{1,0:T(8,128)(2,1)S(1)} %pad_maximum_fusion.4), channel_id=1, source_target_pairs={{0,16},{16,0},{1,17},{17,1},{2,18},{18,2},{3,19},{19,3},{4,20},{20... | collective-permute-start | bytes 245768 | tf_op jit(solution)/shard_map/ppermute | solution.py:15
  13.9 0.8 %copy-start = (bf16[128,128]{1,0:T(8,128)(2,1)S(1)}, bf16[128,128]{1,0:T(8,128)(2,1)}, u32[]{:S(2)}) copy-start(bf16[128,128]{1,0:T(8,128)(2,1)} %param.5) | copy-start | bytes 98308
  15.9 25.8 %all-to-all-start = ((bf16[16,320,128]{2,1,0:T(8,128)(2,1)}), bf16[16,320,128]{2,1,0:T(8,128)(2,1)S(1)}, u32[]{:S(2)}, u32[]{:S(2)}) async-start(bf16[16,320,128]{2,1,0:T(8,128)(2,1)} %pad_maximum_fusion), calls=%async_computation | async-start | bytes 2621440 | tf_op jit(solution)/shard_map/all_to_all | solution.py:153
  22.9 19.8 %collective-permute-start.6 = (bf16[4,2,128,128]{3,2,1,0:T(8,128)(2,1)S(1)}, bf16[4,2,128,128]{3,2,1,0:T(8,128)(2,1)S(1)}, u32[]{:S(2)}, u32[]{:S(2)}) collective-permute-start(bf16[4,2,128,128]{3,2,1,0:T(8,128)(2,1)S(1)} %bitcast.46), channel_id=1, source_target_pairs={{0,2},{2,0},{1,3},{3,1},{4,6},{6,4},{5,7},{7,5},{8,10},{10,8},{9,1... | collective-permute-start | bytes 786440 | tf_op jit(solution)/shard_map/ppermute | solution.py:15
  24.6 18.2 %collective-permute-start.7 = (bf16[4,2,128,128]{3,2,1,0:T(8,128)(2,1)S(1)}, bf16[4,2,128,128]{3,2,1,0:T(8,128)(2,1)S(1)}, u32[]{:S(2)}, u32[]{:S(2)}) collective-permute-start(bf16[4,2,128,128]{3,2,1,0:T(8,128)(2,1)S(1)} %bitcast.47), channel_id=1, source_target_pairs={{0,16},{16,0},{1,17},{17,1},{2,18},{18,2},{3,19},{19,3},{4,20},{20... | collective-permute-start | bytes 786440 | tf_op jit(solution)/shard_map/ppermute | solution.py:15
  25.4 17.3 %collective-permute-start.8 = (bf16[4,2,128,128]{3,2,1,0:T(8,128)(2,1)S(1)}, bf16[4,2,128,128]{3,2,1,0:T(8,128)(2,1)S(1)}, u32[]{:S(2)}, u32[]{:S(2)}) collective-permute-start(bf16[4,2,128,128]{3,2,1,0:T(8,128)(2,1)S(1)} %bitcast.48), channel_id=1, source_target_pairs={{0,18},{2,16},{16,2},{18,0},{1,19},{3,17},{17,3},{19,1},{4,22},{6,... | collective-permute-start | bytes 786440 | tf_op jit(solution)/shard_map/ppermute | solution.py:19
  41.9 5.2 %collective-permute-start.4 = (bf16[16,128,128]{2,1,0:T(8,128)(2,1)S(1)}, bf16[16,128,128]{2,1,0:T(8,128)(2,1)S(1)}, u32[]{:S(2)}, u32[]{:S(2)}) collective-permute-start(bf16[16,128,128]{2,1,0:T(8,128)(2,1)S(1)} %copy_bitcast_fusion.refs_2_), channel_id=1, source_target_pairs={{0,1},{1,0},{2,3},{3,2},{4,5},{5,4},{6,7},{7,6},{8,9},{9,8},{10,11... | collective-permute-start | bytes 1572872 | tf_op jit(solution)/shard_map/ppermute | solution.py:15
  42.1 5.0 %collective-permute-start.5 = (bf16[16,128,128]{2,1,0:T(8,128)(2,1)S(1)}, bf16[16,128,128]{2,1,0:T(8,128)(2,1)S(1)}, u32[]{:S(2)}, u32[]{:S(2)}) collective-permute-start(bf16[16,128,128]{2,1,0:T(8,128)(2,1)S(1)} %slice.48.refs_3_), channel_id=1, source_target_pairs={{0,1},{1,0},{2,3},{3,2},{4,5},{5,4},{6,7},{7,6},{8,9},{9,8},{10,11... | collective-permute-start | bytes 1572872 | tf_op jit(solution)/shard_map/ppermute | solution.py:15

commit v6 on v5

--- a/solution.py
+++ b/solution.py
@@ -31,18 +31,21 @@
 QB = 4
 
 
-def step_kernel(zh_ref, w_ref, u_ref, wr_ref, l00, l01, l10, l11, acc_ref, out_ref, wt, lower):
+def prepare(w_ref, lows, wt, lower):
     for k in range(8):
         wt[k * 128 : (k + 1) * 128, :] = w_ref[k].T
-    for zk, refs in enumerate(((l00, l01), (l10, l11))):
-        for zd, ref in enumerate(refs):
+    for zk in range(2):
+        for zd in range(2):
             for j in range(4):
                 for e in range(2):
                     row, col = (zk * 4 + j) * 128, (zd * 2 + e) * 128
-                    lower[row : row + 128, col : col + 128] = ref[j, e]
-
-    for at in range(0, u_ref.shape[0], QB):
-        u = jnp.concatenate([u_ref[at + q] for q in range(QB)], axis=1)
+                    lower[row : row + 128, col : col + 128] = lows[2 * zk + zd][j, e]
+
+
+def products(zh_ref, uw_ref, acc_ref, out_ref, wt, lower):
+    count = uw_ref.shape[0] // 2
+    for at in range(0, count, QB):
+        u = jnp.concatenate([uw_ref[at + q] for q in range(QB)], axis=1)
         joined = mm(wt[...], u).astype(BF16)
         left = jnp.concatenate(
             [
@@ -71,8 +74,8 @@
             ],
             axis=0,
         )
-        part = mm(rows, wr_ref[at : at + QB].reshape(QB * 128, 128))
-        part = part.reshape(2, 2, 128, 128)
+        slabs = uw_ref[count + at : count + at + QB].reshape(QB * 128, 128)
+        part = mm(rows, slabs).reshape(2, 2, 128, 128)
         for zd in range(2):
             to = zh_ref[0] if zd == 0 else 1 - zh_ref[0]
             if at > 0:
@@ -83,23 +86,22 @@
                 out_ref[to] = acc_ref[to] + part[zd]
 
 
-def contract(zh, w, u, wr, lowers, acc):
+def first_kernel(zh_ref, w_ref, uw_ref, l00, l01, l10, l11, out_ref, wt, lower):
+    prepare(w_ref, (l00, l01, l10, l11), wt, lower)
+    products(zh_ref, uw_ref, None, out_ref, wt, lower)
+
+
+def second_kernel(zh_ref, wt, uw_ref, lower, acc_ref, out_ref):
+    products(zh_ref, uw_ref, acc_ref, out_ref, wt, lower)
+
+
+def contract(body, args, outs):
     vmem = pl.BlockSpec(memory_space=pltpu.VMEM)
-    body = step_kernel
-    args = [zh, w, u, wr, *lowers]
-    if acc is None:
-
-        def body(*refs):
-            step_kernel(*refs[:8], None, *refs[8:])
-    else:
-        args.append(acc)
-
     return pl.pallas_call(
         body,
         in_specs=[pl.BlockSpec(memory_space=pltpu.SMEM)] + [vmem] * (len(args) - 1),
-        out_specs=vmem,
-        out_shape=jax.ShapeDtypeStruct((2, 2, 128, 128), F32),
-        scratch_shapes=[pltpu.VMEM((1024, 128), BF16), pltpu.VMEM((1024, 512), BF16)],
+        out_specs=[vmem] * len(outs),
+        out_shape=[jax.ShapeDtypeStruct(*out) for out in outs],
         compiler_params=pltpu.CompilerParams(vmem_limit_bytes=40 * 1024 * 1024),
         cost_estimate=pl.CostEstimate(
             flops=4 * 10**9, bytes_accessed=4 * 2**20, transcendentals=0
@@ -108,14 +110,37 @@
     )(*args)
 
 
+def fetch_kernel(*refs):
+    count = len(refs) // 3
+    copies = [
+        pltpu.make_async_copy(refs[i], refs[count + i], refs[2 * count + i])
+        for i in range(count)
+    ]
+    for copy in copies:
+        copy.start()
+    for copy in copies:
+        copy.wait()
+
+
+def fetched(*arrays):
+    return pl.pallas_call(
+        fetch_kernel,
+        in_specs=[pl.BlockSpec(memory_space=pltpu.HBM)] * len(arrays),
+        out_specs=[pl.BlockSpec(memory_space=pltpu.VMEM)] * len(arrays),
+        out_shape=[pltpu.VMEM(a.shape, a.dtype) for a in arrays],
+        scratch_shapes=[pltpu.SemaphoreType.DMA] * len(arrays),
+        name="fetch",
+    )(*arrays)
+
+
 def on_device(upper, lower, isometry):
+    isometry, upper, lower = fetched(isometry, upper, lower)
     zl = lax.axis_index("zl")
     zh = lax.axis_index("zh")
     c = lax.axis_index("c")
 
     lower = lower.transpose(1, 2, 0, 3)
     pair = ordered(c, isometry, swapped(isometry, "c"))
-    upper, lower = lax.optimization_barrier((upper, lower))
 
     t = jnp.arange(32)
     plane = jnp.where(t < 16, zl, 1 - zl)
@@ -152,13 +177,16 @@
     )
     got = lax.all_to_all(send, ("x", "y"), 0, 0, tiled=True)
     mats = got[:, :192].reshape(16, 24, 8, 128).transpose(1, 0, 2, 3).reshape(24, 128, 128)
-    u, w = mats[:16], mats[16:]
-    wr = got[:, 192:]
-    u_other, wr_other = swapped(u, "c"), swapped(wr, "c")
+    uw = jnp.concatenate([mats[:16], got[:, 192:]])
+    uw_other = swapped(uw, "c")
 
     at = zh.astype(jnp.int32)[None]
-    acc = contract(at, w, u, wr, lowers, None)
-    acc = contract(at, w, u_other, wr_other, lowers, acc)
+    total = ((2, 2, 128, 128), F32)
+    kept = ((1024, 128), BF16), ((1024, 512), BF16)
+    acc, wt, low = contract(
+        first_kernel, (at, mats[16:], uw, *lowers), (total, *kept)
+    )
+    (acc,) = contract(second_kernel, (at, wt, uw_other, low, acc), (total,))
 
     parts = acc.reshape(2, 2, 32, 4, 128).transpose(2, 0, 1, 3, 4).reshape(64, 8, 128)
     parts = lax.all_to_all(parts, ("x", "zl", "y", "zh"), 0, 0, tiled=True)

time: 69.4 us -> 82.3 us (1.19)
  blocking collectives: 17 us -> 42.7 us
  starting transfers between devices: 17.1 us -> 10.1 us
  waiting for transfers between devices: 20.1 us -> 17.3 us
  other arithmetic: 2.33 us -> 0.58 us
  local copies, waits for them, and re-layouts: 2.58 us -> 1.48 us
  Pallas kernels: 8.6 us -> 9.54 us
  matrix products: 1.08 us -> 0.18 us
    all_to_all x0 -> x1, blocking collectives: none -> 25.5 us  [on_device(): got = lax.all_to_all(send, ('x', 'y'), 0, 0, tiled=True)]
    all_to_all x1 -> x0, waiting for transfers between devices: 14.6 us -> none  [on_device(): got = lax.all_to_all(send, ('x', 'y'), 0, 0, tiled=True)]
    all_to_all x1 -> x0, starting transfers between devices: 7.03 us -> none  [on_device(): got = lax.all_to_all(send, ('x', 'y'), 0, 0, tiled=True)]
    ppermute x7 -> x6, waiting for transfers between devices: 5.42 us -> 11.8 us  [swapped(): return lax.ppermute(value, axis, [(0, 1), (1, 0)])]
    ppermute x2, waiting for transfers between devices: 0.01 us -> 5.5 us  [both_swapped(): return lax.ppermute(value, ('zl', 'zh'), [(i, 3 - i) for i in range(4)])]
    ppermute x7 -> x6, starting transfers between devices: 4.12 us -> 6.35 us  [swapped(): return lax.ppermute(value, axis, [(0, 1), (1, 0)])]
    ppermute x2, starting transfers between devices: 5.97 us -> 3.77 us  [both_swapped(): return lax.ppermute(value, ('zl', 'zh'), [(i, 3 - i) for i in range(4)])]
    unnamed x3 -> x0, local copies, waits for them, and re-layouts: 1.15 us -> none
  transfers between devices with their start and end apart: 10 -> 8, of which waited for: 2 -> 7; matrix products, arithmetic and copies ran while one was open for 4% -> 0% of each run, Pallas kernels for 6% -> 5%
where the time goes in v6:
time: 82.3 us; the launch traced here: 82.2 us
  blocking collectives  42.7 us (52%)
  waiting for transfers between devices  17.3 us (21%)
  starting transfers between devices  10.1 us (12%)
  Pallas kernels  9.54 us (12%)
  local copies, waits for them, and re-layouts  1.48 us (2%)
    all_to_all x1, blocking collectives, on_device(): got = lax.all_to_all(send, ('x', 'y'), 0, 0, tiled=True)  25.5 us
    all_to_all x1, blocking collectives, on_device(): parts = lax.all_to_all(parts, ('x', 'zl', 'y', 'zh'), 0, 0, tiled=True)  17.2 us
    ppermute x6, waiting for transfers between devices, swapped(): return lax.ppermute(value, axis, [(0, 1), (1, 0)])  11.8 us
    pallas_call x2, Pallas kernels, contract(): pl.pallas_call(body, in_specs=[pl.BlockSpec(memory_space=pltpu.SMEM)] + [...  8.48 us
    ppermute x6, starting transfers between devices, swapped(): return lax.ppermute(value, axis, [(0, 1), (1, 0)])  6.35 us
    ppermute x2, waiting for transfers between devices, both_swapped(): return lax.ppermute(value, ('zl', 'zh'), [(i, 3 - i) for i in range(4)])  5.5 us
    ppermute x2, starting transfers between devices, both_swapped(): return lax.ppermute(value, ('zl', 'zh'), [(i, 3 - i) for i in range(4)])  3.77 us
  transfers between devices with their start and end apart: 8, of which 7 were waited for; matrix products, arithmetic and copies ran while one was open for 0% of the time, Pallas kernels for 5%

profile of v6, /device:TPU:0, one launch (start us, length us, event | category | flops | bytes accessed | tf_op | source)
XLA Modules:
  0.0 82.2 jit_solution(7448882865037817661)
XLA Ops:
  0.0 1.1 %fetch.1 = (bf16[128,128]{1,0:T(8,128)(2,1)S(1)}, bf16[128,4,128]{2,1,0:T(4,128)(2,1)S(1)}, bf16[128,4,2,128]{3,2,1,0:T(2,128)(2,1)S(1)}) custom-call(bf16[128,128]{1,0:T(8,128)(2,1)} %refs_0_.1, bf16[128,4,128]{2,1,0:T(4,128)(2,1)} %refs_1_.1, bf16[128,4,2,128]{3,2,1,0:T(2,128)(2,1)} %refs_2_.1), custom_call_target="tpu_custom_call" | custom-call | tf_op jit(solution)/shard_map/fetch/pallas_call | solution.py:126
  1.1 0.1 collective-permute-start
  1.2 0.2 fusion
  1.4 1.0 %collective-permute-done = bf16[128,128]{1,0:T(8,128)(2,1)S(1)} collective-permute-done((bf16[128,128]{1,0:T(8,128)(2,1)S(1)}, bf16[128,128]{1,0:T(8,128)(2,1)S(1)}, u32[]{:S(2)}, u32[]{:S(2)}) %collective-permute-start) | collective-permute-done | bytes 32800 | tf_op jit(solution)/shard_map/ppermute | solution.py:15
  2.4 4.1 %collective-permute-start.2 = (bf16[2,128,128]{2,1,0:T(8,128)(2,1)S(1)}, bf16[2,128,128]{2,1,0:T(8,128)(2,1)S(1)}, u32[]{:S(2)}, u32[]{:S(2)}) collective-permute-start(bf16[2,128,128]{2,1,0:T(8,128)(2,1)S(1)} %reverse_select_fusion.4), channel_id=1, source_target_pairs={{0,2},{2,0},{1,3},{3,1},{4,6},{6,4},{5,7},{7,5},{8,10},{10,8},{9,1... | collective-permute-start | bytes 196616 | tf_op jit(solution)/shard_map/ppermute | solution.py:15
  6.5 0.7 collective-permute-start.3
  7.2 0.4 collective-permute-start.1
  7.6 1.4 %collective-permute-done.2 = bf16[2,128,128]{2,1,0:T(8,128)(2,1)S(1)} collective-permute-done((bf16[2,128,128]{2,1,0:T(8,128)(2,1)S(1)}, bf16[2,128,128]{2,1,0:T(8,128)(2,1)S(1)}, u32[]{:S(2)}, u32[]{:S(2)}) %collective-permute-start.2) | collective-permute-done | bytes 65568 | tf_op jit(solution)/shard_map/ppermute | solution.py:15
  9.0 2.6 %collective-permute-done.1 = bf16[320,128]{1,0:T(8,128)(2,1)S(1)} collective-permute-done((bf16[320,128]{1,0:T(8,128)(2,1)S(1)}, bf16[320,128]{1,0:T(8,128)(2,1)S(1)}, u32[]{:S(2)}, u32[]{:S(2)}) %collective-permute-start.1) | collective-permute-done | bytes 81952 | tf_op jit(solution)/shard_map/ppermute | solution.py:15
  11.7 0.3 collective-permute-done.3
  12.1 0.1 reverse_select_fusion.1
  12.1 0.3 copy.30
  12.4 0.1 reverse_select_fusion
  12.6 0.1 broadcast_in_dim.30
  12.7 0.1 broadcast_in_dim.31
  12.8 0.1 pad_maximum_fusion
  12.9 25.5 %all_to_all.10 = bf16[16,320,128]{2,1,0:T(8,128)(2,1)S(1)} all-to-all(bf16[16,320,128]{2,1,0:T(8,128)(2,1)S(1)} %pad_maximum_fusion), channel_id=1, replica_groups=mesh['x'=4,'zl'=2,'y'=4,'zh'=2,'c'=2] {'x','y'}, dimensions={0} | all-to-all | bytes 2621440 | tf_op jit(solution)/shard_map/all_to_all | solution.py:178
  38.3 0.1 slice_bitcast_fusion
  38.4 0.1 copy_bitcast_fusion
  38.6 0.1 pad_maximum_fusion.1.uw_ref
  38.7 0.1 collective-permute-start.7
  38.8 3.1 %collective-permute-start.6 = (bf16[4,2,128,128]{3,2,1,0:T(8,128)(2,1)S(1)}, bf16[4,2,128,128]{3,2,1,0:T(8,128)(2,1)S(1)}, u32[]{:S(2)}, u32[]{:S(2)}) collective-permute-start(bf16[4,2,128,128]{3,2,1,0:T(8,128)(2,1)S(1)} %bitcast.46), channel_id=1, source_target_pairs={{0,18},{2,16},{16,2},{18,0},{1,19},{3,17},{17,3},{19,1},{4,22},{6,... | collective-permute-start | bytes 786440 | tf_op jit(solution)/shard_map/ppermute | solution.py:19
  41.9 0.0 collective-permute-start.5
  41.9 1.7 %collective-permute-start.4 = (bf16[4,2,128,128]{3,2,1,0:T(8,128)(2,1)S(1)}, bf16[4,2,128,128]{3,2,1,0:T(8,128)(2,1)S(1)}, u32[]{:S(2)}, u32[]{:S(2)}) collective-permute-start(bf16[4,2,128,128]{3,2,1,0:T(8,128)(2,1)S(1)} %bitcast.48), channel_id=1, source_target_pairs={{0,2},{2,0},{1,3},{3,1},{4,6},{6,4},{5,7},{7,5},{8,10},{10,8},{9,1... | collective-permute-start | bytes 786440 | tf_op jit(solution)/shard_map/ppermute | solution.py:15
  43.7 5.2 %collective-permute-done.6.l11 = bf16[4,2,128,128]{3,2,1,0:T(8,128)(2,1)S(1)} collective-permute-done((bf16[4,2,128,128]{3,2,1,0:T(8,128)(2,1)S(1)}, bf16[4,2,128,128]{3,2,1,0:T(8,128)(2,1)S(1)}, u32[]{:S(2)}, u32[]{:S(2)}) %collective-permute-start.6) | collective-permute-done | bytes 262176 | tf_op jit(solution)/shard_map/ppermute | solution.py:19
  48.8 2.2 %collective-permute-done.5.l10 = bf16[4,2,128,128]{3,2,1,0:T(8,128)(2,1)S(1)} collective-permute-done((bf16[4,2,128,128]{3,2,1,0:T(8,128)(2,1)S(1)}, bf16[4,2,128,128]{3,2,1,0:T(8,128)(2,1)S(1)}, u32[]{:S(2)}, u32[]{:S(2)}) %collective-permute-start.5) | collective-permute-done | bytes 262176 | tf_op jit(solution)/shard_map/ppermute | solution.py:15
  51.1 4.7 %collective-permute-done.4.l01 = bf16[4,2,128,128]{3,2,1,0:T(8,128)(2,1)S(1)} collective-permute-done((bf16[4,2,128,128]{3,2,1,0:T(8,128)(2,1)S(1)}, bf16[4,2,128,128]{3,2,1,0:T(8,128)(2,1)S(1)}, u32[]{:S(2)}, u32[]{:S(2)}) %collective-permute-start.4) | collective-permute-done | bytes 262176 | tf_op jit(solution)/shard_map/ppermute | solution.py:15
  55.7 4.4 %contract.2 = (f32[2,2,128,128]{3,2,1,0:T(8,128)S(1)}, bf16[1024,128]{1,0:T(8,128)(2,1)S(1)}, bf16[1024,512]{1,0:T(8,128)(2,1)S(1)}) custom-call(s32[1]{0:T(128)} %bitcast.zh_ref, bf16[8,128,128]{2,1,0:T(8,128)(2,1)S(1)} %copy_bitcast_fusion.2.w_ref, bf16[32,128,128]{2,1,0:T(8,128)(2,1)S(1)} %pad_maximum_fusion.1.uw_ref, ...), custom_call_target="tpu_custom_call" | custom-call | flops 4000000000 | bytes 4194304 | tf_op jit(solution)/shard_map/contract/pallas_call | solution.py:100
  60.1 4.1 %contract.3 = f32[2,2,128,128]{3,2,1,0:T(8,128)S(1)} custom-call(s32[1]{0:T(128)} %bitcast.zh_ref, bf16[1024,128]{1,0:T(8,128)(2,1)S(1)} %get-tuple-element.14.wt, bf16[32,128,128]{2,1,0:T(8,128)(2,1)S(1)} %collective-permute-done.7.uw_ref, bf16[1024,512]{1,0:T(8,128)(2,1)S(1)} %get-tuple-element.15.lower, f32[2,2,128,128]{3,2,1,0:T(8,128)S(1)} %get-tuple-element.16.acc_ref), custom_call_target="tpu_custom_call" | custom-call | flops 4000000000 | bytes 4194304 | tf_op jit(solution)/shard_map/contract/pallas_call | solution.py:100
  64.3 17.2 %all_to_all.11 = f32[64,8,128]{2,1,0:T(8,128)S(1)} all-to-all(f32[64,8,128]{2,1,0:T(8,128)S(1)} %bitcast.55), channel_id=1, replica_groups=mesh['x'=4,'zl'=2,'y'=4,'zh'=2,'c'=2] {'x','zl','y','zh'}, dimensions={0} | all-to-all | bytes 524288 | tf_op jit(solution)/shard_map/all_to_all | solution.py:192
  81.5 0.1 reduce_sum.9
  81.6 0.6 copy.19
  (22 shorter events, 0.4 us)
Async XLA Ops:
  1.1 1.3 %collective-permute-start = (bf16[128,128]{1,0:T(8,128)(2,1)S(1)}, bf16[128,128]{1,0:T(8,128)(2,1)S(1)}, u32[]{:S(2)}, u32[]{:S(2)}) collective-permute-start(bf16[128,128]{1,0:T(8,128)(2,1)S(1)} %get-tuple-element.12), channel_id=1, source_target_pairs={{0,1},{1,0},{2,3},{3,2},{4,5},{5,4},{6,7},{7,6},{8,9},{9,8},{10,11... | collective-permute-start | bytes 98312 | tf_op jit(solution)/shard_map/ppermute | solution.py:15
  2.4 6.5 %collective-permute-start.2 = (bf16[2,128,128]{2,1,0:T(8,128)(2,1)S(1)}, bf16[2,128,128]{2,1,0:T(8,128)(2,1)S(1)}, u32[]{:S(2)}, u32[]{:S(2)}) collective-permute-start(bf16[2,128,128]{2,1,0:T(8,128)(2,1)S(1)} %reverse_select_fusion.4), channel_id=1, source_target_pairs={{0,2},{2,0},{1,3},{3,1},{4,6},{6,4},{5,7},{7,5},{8,10},{10,8},{9,1... | collective-permute-start | bytes 196616 | tf_op jit(solution)/shard_map/ppermute | solution.py:15
  6.5 5.5 %collective-permute-start.3 = (bf16[2,128,128]{2,1,0:T(8,128)(2,1)S(1)}, bf16[2,128,128]{2,1,0:T(8,128)(2,1)S(1)}, u32[]{:S(2)}, u32[]{:S(2)}) collective-permute-start(bf16[2,128,128]{2,1,0:T(8,128)(2,1)S(1)} %reverse_select_fusion.4), channel_id=1, source_target_pairs={{0,18},{2,16},{16,2},{18,0},{1,19},{3,17},{17,3},{19,1},{4,22},{6,... | collective-permute-start | bytes 196616 | tf_op jit(solution)/shard_map/ppermute | solution.py:19
  7.2 4.4 %collective-permute-start.1 = (bf16[320,128]{1,0:T(8,128)(2,1)S(1)}, bf16[320,128]{1,0:T(8,128)(2,1)S(1)}, u32[]{:S(2)}, u32[]{:S(2)}) collective-permute-start(bf16[320,128]{1,0:T(8,128)(2,1)S(1)} %pad_maximum_fusion.5), channel_id=1, source_target_pairs={{0,16},{16,0},{1,17},{17,1},{2,18},{18,2},{3,19},{19,3},{4,20},{20... | collective-permute-start | bytes 245768 | tf_op jit(solution)/shard_map/ppermute | solution.py:15
  38.7 21.4 %collective-permute-start.7 = (bf16[32,128,128]{2,1,0:T(8,128)(2,1)S(1)}, bf16[32,128,128]{2,1,0:T(8,128)(2,1)S(1)}, u32[]{:S(2)}, u32[]{:S(2)}) collective-permute-start(bf16[32,128,128]{2,1,0:T(8,128)(2,1)S(1)} %pad_maximum_fusion.1.uw_ref), channel_id=1, source_target_pairs={{0,1},{1,0},{2,3},{3,2},{4,5},{5,4},{6,7},{7,6},{8,9},{9,8},{10,11... | collective-permute-start | bytes 3145736 | tf_op jit(solution)/shard_map/ppermute | solution.py:15
  38.8 10.0 %collective-permute-start.6 = (bf16[4,2,128,128]{3,2,1,0:T(8,128)(2,1)S(1)}, bf16[4,2,128,128]{3,2,1,0:T(8,128)(2,1)S(1)}, u32[]{:S(2)}, u32[]{:S(2)}) collective-permute-start(bf16[4,2,128,128]{3,2,1,0:T(8,128)(2,1)S(1)} %bitcast.46), channel_id=1, source_target_pairs={{0,18},{2,16},{16,2},{18,0},{1,19},{3,17},{17,3},{19,1},{4,22},{6,... | collective-permute-start | bytes 786440 | tf_op jit(solution)/shard_map/ppermute | solution.py:19
  41.9 9.2 %collective-permute-start.5 = (bf16[4,2,128,128]{3,2,1,0:T(8,128)(2,1)S(1)}, bf16[4,2,128,128]{3,2,1,0:T(8,128)(2,1)S(1)}, u32[]{:S(2)}, u32[]{:S(2)}) collective-permute-start(bf16[4,2,128,128]{3,2,1,0:T(8,128)(2,1)S(1)} %bitcast.47), channel_id=1, source_target_pairs={{0,16},{16,0},{1,17},{17,1},{2,18},{18,2},{3,19},{19,3},{4,20},{20... | collective-permute-start | bytes 786440 | tf_op jit(solution)/shard_map/ppermute | solution.py:15
  41.9 13.8 %collective-permute-start.4 = (bf16[4,2,128,128]{3,2,1,0:T(8,128)(2,1)S(1)}, bf16[4,2,128,128]{3,2,1,0:T(8,128)(2,1)S(1)}, u32[]{:S(2)}, u32[]{:S(2)}) collective-permute-start(bf16[4,2,128,128]{3,2,1,0:T(8,128)(2,1)S(1)} %bitcast.48), channel_id=1, source_target_pairs={{0,2},{2,0},{1,3},{3,1},{4,6},{6,4},{5,7},{7,5},{8,10},{10,8},{9,1... | collective-permute-start | bytes 786440 | tf_op jit(solution)/shard_map/ppermute | solution.py:15

commit v7 on v6

--- a/solution.py
+++ b/solution.py
@@ -140,8 +140,6 @@
     c = lax.axis_index("c")
 
     lower = lower.transpose(1, 2, 0, 3)
-    pair = ordered(c, isometry, swapped(isometry, "c"))
-
     t = jnp.arange(32)
     plane = jnp.where(t < 16, zl, 1 - zl)
     xy = t % 16
@@ -152,39 +150,43 @@
     ).astype(BF16)
 
     theirs = swapped(
-        jnp.concatenate([rights[16:].reshape(64, 128), pair.reshape(256, 128)]), "zl"
-    )
-    far = swapped(pair, "zh"), both_swapped(pair)
-    own = ordered(zh, pair, far[0])
-    other = ordered(zh, theirs[64:].reshape(2, 128, 128), far[1])
-    column = ordered(zl, own, other).reshape(8, 4, 2, 4, 4, 128)
+        jnp.concatenate([rights[16:].reshape(64, 128), isometry], axis=0), "zl"
+    )
+    far = swapped(isometry, "zh"), both_swapped(isometry)
+    own = ordered(zh, isometry, far[0])
+    other = ordered(zh, theirs[64:], far[1])
+    column = ordered(zl, own, other).reshape(4, 4, 2, 4, 4, 128)
     ks = column.transpose(1, 3, 2, 4, 0, 5)
     ks = jnp.where(zl == 0, ks, ks[:, :, ::-1])
 
-    lowers = (lower, swapped(lower, "zh"), swapped(lower, "zl"), both_swapped(lower))
-
-    theirs = theirs[:64].reshape(16, 4, 128)
-    first = jnp.where(zl == 0, rights[:16], theirs)
-    second = jnp.where(zl == 0, theirs, rights[:16])
-    rights = jnp.concatenate([first, second], axis=1)
+    l01 = swapped(lower, "zh")
+    l10 = swapped(lower, "zl")
+    l11 = both_swapped(lower)
+    lowers = (lower, l01, l10, l11)
+
+    rights = ordered(zl, rights[:16], theirs[:64].reshape(16, 4, 128))
+    rights = rights.reshape(2, 16, 2, 2, 128).transpose(1, 3, 0, 2, 4)
     send = jnp.concatenate(
         [
             jnp.broadcast_to(rights.reshape(1, 128, 128), (16, 128, 128)),
-            ks.reshape(16, 64, 128),
+            ks.reshape(16, 32, 128),
             jnp.broadcast_to(isometry[None], (16, 128, 128)),
         ],
         axis=1,
     )
     got = lax.all_to_all(send, ("x", "y"), 0, 0, tiled=True)
-    mats = got[:, :192].reshape(16, 24, 8, 128).transpose(1, 0, 2, 3).reshape(24, 128, 128)
-    uw = jnp.concatenate([mats[:16], got[:, 192:]])
+    w = got[:, 128:160].reshape(16, 8, 4, 128).transpose(1, 0, 2, 3)
+    u = got[:, :128].reshape(16, 16, 8, 128).transpose(1, 0, 2, 3).reshape(16, 128, 128)
+    w = ordered(c, w, swapped(w, "c"))
+    w = w.transpose(1, 2, 0, 3, 4).reshape(8, 128, 128)
+    uw = jnp.concatenate([u, got[:, 160:]])
     uw_other = swapped(uw, "c")
 
     at = zh.astype(jnp.int32)[None]
     total = ((2, 2, 128, 128), F32)
     kept = ((1024, 128), BF16), ((1024, 512), BF16)
     acc, wt, low = contract(
-        first_kernel, (at, mats[16:], uw, *lowers), (total, *kept)
+        first_kernel, (at, w, uw, *lowers), (total, *kept)
     )
     (acc,) = contract(second_kernel, (at, wt, uw_other, low, acc), (total,))
 

time: 82.3 us -> 77.8 us (0.945)
  blocking collectives: 42.7 us -> 39.6 us
  waiting for transfers between devices: 17.3 us -> 14.4 us
  other arithmetic: 0.58 us -> 1.63 us
    ppermute x2, waiting for transfers between devices: 5.5 us -> 3.47 us  [both_swapped(): return lax.ppermute(value, ('zl', 'zh'), [(i, 3 - i) for i in range(4)])]
    ppermute x2, starting transfers between devices: 3.77 us -> 5.75 us  [both_swapped(): return lax.ppermute(value, ('zl', 'zh'), [(i, 3 - i) for i in range(4)])]
    all_to_all x1, blocking collectives: 25.5 us -> 23.8 us  [on_device(): got = lax.all_to_all(send, ('x', 'y'), 0, 0, tiled=True)]
    all_to_all x1, blocking collectives: 17.2 us -> 15.7 us  [on_device(): parts = lax.all_to_all(parts, ('x', 'zl', 'y', 'zh'), 0, 0, tiled=True)]
    ppermute x6, starting transfers between devices: 6.35 us -> 4.94 us  [swapped(): return lax.ppermute(value, axis, [(0, 1), (1, 0)])]
    another operation x7 -> x6, other arithmetic: 0.14 us -> 1.17 us  [ordered(): both = jnp.stack([own, other])]
    ppermute x6, waiting for transfers between devices: 11.8 us -> 10.9 us  [swapped(): return lax.ppermute(value, axis, [(0, 1), (1, 0)])]
  transfers between devices with their start and end apart: 8 -> 8, of which waited for: 7 -> 4; matrix products, arithmetic and copies ran while one was open for 0% -> 2% of each run, Pallas kernels for 5% -> 6%
where the time goes in v7:
time: 77.8 us; the launch traced here: 77.6 us
  blocking collectives  39.6 us (51%)
  waiting for transfers between devices  14.4 us (19%)
  starting transfers between devices  10.7 us (14%)
  Pallas kernels  9.54 us (12%)
  other arithmetic  1.63 us (2%)
  local copies, waits for them, and re-layouts  1.34 us (2%)
    all_to_all x1, blocking collectives, on_device(): got = lax.all_to_all(send, ('x', 'y'), 0, 0, tiled=True)  23.8 us
    all_to_all x1, blocking collectives, on_device(): parts = lax.all_to_all(parts, ('x', 'zl', 'y', 'zh'), 0, 0, tiled=True)  15.7 us
    ppermute x6, waiting for transfers between devices, swapped(): return lax.ppermute(value, axis, [(0, 1), (1, 0)])  10.9 us
    pallas_call x2, Pallas kernels, contract(): pl.pallas_call(body, in_specs=[pl.BlockSpec(memory_space=pltpu.SMEM)] + [...  8.48 us
    ppermute x2, starting transfers between devices, both_swapped(): return lax.ppermute(value, ('zl', 'zh'), [(i, 3 - i) for i in range(4)])  5.75 us
    ppermute x6, starting transfers between devices, swapped(): return lax.ppermute(value, axis, [(0, 1), (1, 0)])  4.94 us
    ppermute x2, waiting for transfers between devices, both_swapped(): return lax.ppermute(value, ('zl', 'zh'), [(i, 3 - i) for i in range(4)])  3.47 us
  transfers between devices with their start and end apart: 8, of which 4 were waited for; matrix products, arithmetic and copies ran while one was open for 2% of the time, Pallas kernels for 6%

profile of v7, /device:TPU:0, one launch (start us, length us, event | category | flops | bytes accessed | tf_op | source)
XLA Modules:
  0.0 77.6 jit_solution(10487045018527467494)
XLA Ops:
  0.0 1.1 %fetch.1 = (bf16[128,128]{1,0:T(8,128)(2,1)S(1)}, bf16[128,4,128]{2,1,0:T(4,128)(2,1)S(1)}, bf16[128,4,2,128]{3,2,1,0:T(2,128)(2,1)S(1)}) custom-call(bf16[128,128]{1,0:T(8,128)(2,1)} %refs_0_.1, bf16[128,4,128]{2,1,0:T(4,128)(2,1)} %refs_1_.1, bf16[128,4,2,128]{3,2,1,0:T(2,128)(2,1)} %refs_2_.1), custom_call_target="tpu_custom_call" | custom-call | tf_op jit(solution)/shard_map/fetch/pallas_call | solution.py:126
  1.1 4.2 %collective-permute-start.2 = (bf16[128,128]{1,0:T(8,128)(2,1)S(1)}, bf16[128,128]{1,0:T(8,128)(2,1)S(1)}, u32[]{:S(2)}, u32[]{:S(2)}) collective-permute-start(bf16[128,128]{1,0:T(8,128)(2,1)S(1)} %get-tuple-element.12), channel_id=1, source_target_pairs={{0,18},{2,16},{16,2},{18,0},{1,19},{3,17},{17,3},{19,1},{4,22},{6,... | collective-permute-start | bytes 98312 | tf_op jit(solution)/shard_map/ppermute | solution.py:19
  5.3 0.0 collective-permute-start.1
  5.3 0.2 fusion
  5.5 1.0 %collective-permute-start = (bf16[192,128]{1,0:T(8,128)(2,1)S(1)}, bf16[192,128]{1,0:T(8,128)(2,1)S(1)}, u32[]{:S(2)}, u32[]{:S(2)}) collective-permute-start(bf16[192,128]{1,0:T(8,128)(2,1)S(1)} %pad_maximum_fusion.6), channel_id=1, source_target_pairs={{0,16},{16,0},{1,17},{17,1},{2,18},{18,2},{3,19},{19,3},{4,20},{20... | collective-permute-start | bytes 147464 | tf_op jit(solution)/shard_map/ppermute | solution.py:15
  6.6 4.1 %collective-permute-done.1 = bf16[128,128]{1,0:T(8,128)(2,1)S(1)} collective-permute-done((bf16[128,128]{1,0:T(8,128)(2,1)S(1)}, bf16[128,128]{1,0:T(8,128)(2,1)S(1)}, u32[]{:S(2)}, u32[]{:S(2)}) %collective-permute-start.1) | collective-permute-done | bytes 32800 | tf_op jit(solution)/shard_map/ppermute | solution.py:15
  10.7 0.0 collective-permute-done
  10.9 0.1 copy.29
  11.0 0.1 reverse_select_fusion.1
  11.1 0.1 broadcast_in_dim.30
  11.2 0.1 broadcast_in_dim.31
  11.3 0.1 pad_maximum_fusion
  11.4 23.8 %all_to_all.10 = bf16[16,288,128]{2,1,0:T(8,128)(2,1)S(1)} all-to-all(bf16[16,288,128]{2,1,0:T(8,128)(2,1)S(1)} %pad_maximum_fusion), channel_id=1, replica_groups=mesh['x'=4,'zl'=2,'y'=4,'zh'=2,'c'=2] {'x','y'}, dimensions={0} | all-to-all | bytes 2359296 | tf_op jit(solution)/shard_map/all_to_all | solution.py:177
  35.3 0.1 slice_bitcast_fusion
  35.3 0.1 copy.27
  35.5 0.1 pad_maximum_fusion.1.uw_ref
  35.6 0.1 collective-permute-start.7
  35.7 0.6 collective-permute-start.3
  36.3 1.5 %collective-permute-start.6 = (bf16[4,2,128,128]{3,2,1,0:T(8,128)(2,1)S(1)}, bf16[4,2,128,128]{3,2,1,0:T(8,128)(2,1)S(1)}, u32[]{:S(2)}, u32[]{:S(2)}) collective-permute-start(bf16[4,2,128,128]{3,2,1,0:T(8,128)(2,1)S(1)} %bitcast.55), channel_id=1, source_target_pairs={{0,18},{2,16},{16,2},{18,0},{1,19},{3,17},{17,3},{19,1},{4,22},{6,... | collective-permute-start | bytes 786440 | tf_op jit(solution)/shard_map/ppermute | solution.py:19
  37.8 0.8 collective-permute-start.5
  38.6 2.5 %collective-permute-start.4 = (bf16[4,2,128,128]{3,2,1,0:T(8,128)(2,1)S(1)}, bf16[4,2,128,128]{3,2,1,0:T(8,128)(2,1)S(1)}, u32[]{:S(2)}, u32[]{:S(2)}) collective-permute-start(bf16[4,2,128,128]{3,2,1,0:T(8,128)(2,1)S(1)} %bitcast.57), channel_id=1, source_target_pairs={{0,2},{2,0},{1,3},{3,1},{4,6},{6,4},{5,7},{7,5},{8,10},{10,8},{9,1... | collective-permute-start | bytes 786440 | tf_op jit(solution)/shard_map/ppermute | solution.py:15
  41.1 1.1 %pad_maximum_fusion.2 = bf16[2,8,16,4,128]{4,3,1,2,0:T(4,128)(2,1)S(1)} fusion(bf16[1,8,16,4,128]{4,3,1,2,0:T(4,128)(2,1)} %bitcast.22, bf16[1,8,16,4,128]{4,3,1,2,0:T(4,128)(2,1)S(1)} %bitcast.67), kind=kLoop, calls=%fused_computation.8 | loop fusion | flops 131072 | bytes 524288 | tf_op jit(solution)/shard_map/stack | solution.py:23
  42.2 0.1 fusion.1
  42.3 0.1 copy.17
  42.4 3.5 %collective-permute-done.6.l11 = bf16[4,2,128,128]{3,2,1,0:T(8,128)(2,1)S(1)} collective-permute-done((bf16[4,2,128,128]{3,2,1,0:T(8,128)(2,1)S(1)}, bf16[4,2,128,128]{3,2,1,0:T(8,128)(2,1)S(1)}, u32[]{:S(2)}, u32[]{:S(2)}) %collective-permute-start.6) | collective-permute-done | bytes 262176 | tf_op jit(solution)/shard_map/ppermute | solution.py:19
  45.9 1.1 %collective-permute-done.5.l10 = bf16[4,2,128,128]{3,2,1,0:T(8,128)(2,1)S(1)} collective-permute-done((bf16[4,2,128,128]{3,2,1,0:T(8,128)(2,1)S(1)}, bf16[4,2,128,128]{3,2,1,0:T(8,128)(2,1)S(1)}, u32[]{:S(2)}, u32[]{:S(2)}) %collective-permute-start.5) | collective-permute-done | bytes 262176 | tf_op jit(solution)/shard_map/ppermute | solution.py:15
  47.0 5.6 %collective-permute-done.4.l01 = bf16[4,2,128,128]{3,2,1,0:T(8,128)(2,1)S(1)} collective-permute-done((bf16[4,2,128,128]{3,2,1,0:T(8,128)(2,1)S(1)}, bf16[4,2,128,128]{3,2,1,0:T(8,128)(2,1)S(1)}, u32[]{:S(2)}, u32[]{:S(2)}) %collective-permute-start.4) | collective-permute-done | bytes 262176 | tf_op jit(solution)/shard_map/ppermute | solution.py:15
  52.6 4.4 %contract.2 = (f32[2,2,128,128]{3,2,1,0:T(8,128)S(1)}, bf16[1024,128]{1,0:T(8,128)(2,1)S(1)}, bf16[1024,512]{1,0:T(8,128)(2,1)S(1)}) custom-call(s32[1]{0:T(128)} %bitcast.zh_ref, bf16[8,128,128]{2,1,0:T(8,128)(2,1)S(1)} %bitcast.59, bf16[32,128,128]{2,1,0:T(8,128)(2,1)S(1)} %pad_maximum_fusion.1.uw_ref, bf16[4,2,128,128]{3,2,1,0:T(8,128)(2,1)S(1)} %bitcast.58, ...), custom_call_target="tpu_custom_call" | custom-call | flops 4000000000 | bytes 4194304 | tf_op jit(solution)/shard_map/contract/pallas_call | solution.py:100
  57.0 4.1 %contract.3 = f32[2,2,128,128]{3,2,1,0:T(8,128)S(1)} custom-call(s32[1]{0:T(128)} %bitcast.zh_ref, bf16[1024,128]{1,0:T(8,128)(2,1)S(1)} %get-tuple-element.14.wt, bf16[32,128,128]{2,1,0:T(8,128)(2,1)S(1)} %collective-permute-done.7.uw_ref, bf16[1024,512]{1,0:T(8,128)(2,1)S(1)} %get-tuple-element.15.lower, f32[2,2,128,128]{3,2,1,0:T(8,128)S(1)} %get-tuple-element.16.acc_ref), custom_call_target="tpu_custom_call" | custom-call | flops 4000000000 | bytes 4194304 | tf_op jit(solution)/shard_map/contract/pallas_call | solution.py:100
  61.2 15.7 %all_to_all.11 = f32[64,8,128]{2,1,0:T(8,128)S(1)} all-to-all(f32[64,8,128]{2,1,0:T(8,128)S(1)} %bitcast.62), channel_id=1, replica_groups=mesh['x'=4,'zl'=2,'y'=4,'zh'=2,'c'=2] {'x','zl','y','zh'}, dimensions={0} | all-to-all | bytes 524288 | tf_op jit(solution)/shard_map/all_to_all | solution.py:194
  76.9 0.1 reduce_sum.9
  77.0 0.6 copy.21
  (21 shorter events, 0.3 us)
Async XLA Ops:
  1.1 9.7 %collective-permute-start.2 = (bf16[128,128]{1,0:T(8,128)(2,1)S(1)}, bf16[128,128]{1,0:T(8,128)(2,1)S(1)}, u32[]{:S(2)}, u32[]{:S(2)}) collective-permute-start(bf16[128,128]{1,0:T(8,128)(2,1)S(1)} %get-tuple-element.12), channel_id=1, source_target_pairs={{0,18},{2,16},{16,2},{18,0},{1,19},{3,17},{17,3},{19,1},{4,22},{6,... | collective-permute-start | bytes 98312 | tf_op jit(solution)/shard_map/ppermute | solution.py:19
  5.3 5.4 %collective-permute-start.1 = (bf16[128,128]{1,0:T(8,128)(2,1)S(1)}, bf16[128,128]{1,0:T(8,128)(2,1)S(1)}, u32[]{:S(2)}, u32[]{:S(2)}) collective-permute-start(bf16[128,128]{1,0:T(8,128)(2,1)S(1)} %get-tuple-element.12), channel_id=1, source_target_pairs={{0,2},{2,0},{1,3},{3,1},{4,6},{6,4},{5,7},{7,5},{8,10},{10,8},{9,1... | collective-permute-start | bytes 98312 | tf_op jit(solution)/shard_map/ppermute | solution.py:15
  5.5 5.2 %collective-permute-start = (bf16[192,128]{1,0:T(8,128)(2,1)S(1)}, bf16[192,128]{1,0:T(8,128)(2,1)S(1)}, u32[]{:S(2)}, u32[]{:S(2)}) collective-permute-start(bf16[192,128]{1,0:T(8,128)(2,1)S(1)} %pad_maximum_fusion.6), channel_id=1, source_target_pairs={{0,16},{16,0},{1,17},{17,1},{2,18},{18,2},{3,19},{19,3},{4,20},{20... | collective-permute-start | bytes 147464 | tf_op jit(solution)/shard_map/ppermute | solution.py:15
  35.6 21.4 %collective-permute-start.7 = (bf16[32,128,128]{2,1,0:T(8,128)(2,1)S(1)}, bf16[32,128,128]{2,1,0:T(8,128)(2,1)S(1)}, u32[]{:S(2)}, u32[]{:S(2)}) collective-permute-start(bf16[32,128,128]{2,1,0:T(8,128)(2,1)S(1)} %pad_maximum_fusion.1.uw_ref), channel_id=1, source_target_pairs={{0,1},{1,0},{2,3},{3,2},{4,5},{5,4},{6,7},{7,6},{8,9},{9,8},{10,11... | collective-permute-start | bytes 3145736 | tf_op jit(solution)/shard_map/ppermute | solution.py:15
  35.7 5.4 %collective-permute-start.3 = (bf16[8,16,4,128]{3,2,0,1:T(4,128)(2,1)S(1)}, bf16[8,16,4,128]{3,2,0,1:T(4,128)(2,1)}, u32[]{:S(2)}, u32[]{:S(2)}) collective-permute-start(bf16[8,16,4,128]{3,2,0,1:T(4,128)(2,1)S(1)} %bitcast.66), channel_id=1, source_target_pairs={{0,1},{1,0},{2,3},{3,2},{4,5},{5,4},{6,7},{7,6},{8,9},{9,8},{10,11... | collective-permute-start | bytes 393224 | tf_op jit(solution)/shard_map/ppermute | solution.py:15
  36.3 9.6 %collective-permute-start.6 = (bf16[4,2,128,128]{3,2,1,0:T(8,128)(2,1)S(1)}, bf16[4,2,128,128]{3,2,1,0:T(8,128)(2,1)S(1)}, u32[]{:S(2)}, u32[]{:S(2)}) collective-permute-start(bf16[4,2,128,128]{3,2,1,0:T(8,128)(2,1)S(1)} %bitcast.55), channel_id=1, source_target_pairs={{0,18},{2,16},{16,2},{18,0},{1,19},{3,17},{17,3},{19,1},{4,22},{6,... | collective-permute-start | bytes 786440 | tf_op jit(solution)/shard_map/ppermute | solution.py:19
  37.8 9.2 %collective-permute-start.5 = (bf16[4,2,128,128]{3,2,1,0:T(8,128)(2,1)S(1)}, bf16[4,2,128,128]{3,2,1,0:T(8,128)(2,1)S(1)}, u32[]{:S(2)}, u32[]{:S(2)}) collective-permute-start(bf16[4,2,128,128]{3,2,1,0:T(8,128)(2,1)S(1)} %bitcast.56), channel_id=1, source_target_pairs={{0,16},{16,0},{1,17},{17,1},{2,18},{18,2},{3,19},{19,3},{4,20},{20... | collective-permute-start | bytes 786440 | tf_op jit(solution)/shard_map/ppermute | solution.py:15
  38.6 14.0 %collective-permute-start.4 = (bf16[4,2,128,128]{3,2,1,0:T(8,128)(2,1)S(1)}, bf16[4,2,128,128]{3,2,1,0:T(8,128)(2,1)S(1)}, u32[]{:S(2)}, u32[]{:S(2)}) collective-permute-start(bf16[4,2,128,128]{3,2,1,0:T(8,128)(2,1)S(1)} %bitcast.57), channel_id=1, source_target_pairs={{0,2},{2,0},{1,3},{3,1},{4,6},{6,4},{5,7},{7,5},{8,10},{10,8},{9,1... | collective-permute-start | bytes 786440 | tf_op jit(solution)/shard_map/ppermute | solution.py:15

commit v8 on v7

--- a/solution.py
+++ b/solution.py
@@ -15,8 +15,13 @@
     return lax.ppermute(value, axis, [(0, 1), (1, 0)])
 
 
-def both_swapped(value):
-    return lax.ppermute(value, ("zl", "zh"), [(i, 3 - i) for i in range(4)])
+def along_z(value, shift):
+    def at(z):
+        return (z % 2) * 2 + z // 2
+
+    return lax.ppermute(
+        value, ("zl", "zh"), [(at(z), at((z + shift) % 4)) for z in range(4)]
+    )
 
 
 def ordered(index, own, other):
@@ -31,18 +36,19 @@
 QB = 4
 
 
-def prepare(w_ref, lows, wt, lower):
+def prepare(z_ref, w_ref, lows, wt, lower):
     for k in range(8):
         wt[k * 128 : (k + 1) * 128, :] = w_ref[k].T
-    for zk in range(2):
-        for zd in range(2):
-            for j in range(4):
-                for e in range(2):
-                    row, col = (zk * 4 + j) * 128, (zd * 2 + e) * 128
-                    lower[row : row + 128, col : col + 128] = lows[2 * zk + zd][j, e]
-
-
-def products(zh_ref, uw_ref, acc_ref, out_ref, wt, lower):
+    for shift in range(4):
+        z = (z_ref[0] + 4 - shift) % 4
+        for j in range(4):
+            row = pl.multiple_of(((z % 2) * 4 + j) * 128, 128)
+            for e in range(2):
+                block = lows[shift][j, e]
+                lower[z // 2, pl.ds(row, 128), e * 128 : (e + 1) * 128] = block
+
+
+def products(uw_ref, acc_ref, out_ref, wt, lower):
     count = uw_ref.shape[0] // 2
     for at in range(0, count, QB):
         u = jnp.concatenate([uw_ref[at + q] for q in range(QB)], axis=1)
@@ -60,39 +66,38 @@
             ],
             axis=0,
         )
-        paired = mm(left, lower[...]).astype(BF16)
+        paired = [mm(left, lower[zh]).astype(BF16) for zh in range(2)]
         rows = jnp.concatenate(
             [
                 jnp.concatenate(
                     [
-                        paired[q * 128 : (q + 1) * 128, d * 128 : (d + 1) * 128]
+                        paired[zh][q * 128 : (q + 1) * 128, e * 128 : (e + 1) * 128]
                         for q in range(QB)
                     ],
                     axis=1,
                 )
-                for d in range(4)
+                for zh in range(2)
+                for e in range(2)
             ],
             axis=0,
         )
         slabs = uw_ref[count + at : count + at + QB].reshape(QB * 128, 128)
         part = mm(rows, slabs).reshape(2, 2, 128, 128)
-        for zd in range(2):
-            to = zh_ref[0] if zd == 0 else 1 - zh_ref[0]
-            if at > 0:
-                out_ref[to] += part[zd]
-            elif acc_ref is None:
-                out_ref[to] = part[zd]
-            else:
-                out_ref[to] = acc_ref[to] + part[zd]
-
-
-def first_kernel(zh_ref, w_ref, uw_ref, l00, l01, l10, l11, out_ref, wt, lower):
-    prepare(w_ref, (l00, l01, l10, l11), wt, lower)
-    products(zh_ref, uw_ref, None, out_ref, wt, lower)
-
-
-def second_kernel(zh_ref, wt, uw_ref, lower, acc_ref, out_ref):
-    products(zh_ref, uw_ref, acc_ref, out_ref, wt, lower)
+        if at > 0:
+            out_ref[...] += part
+        elif acc_ref is None:
+            out_ref[...] = part
+        else:
+            out_ref[...] = acc_ref[...] + part
+
+
+def first_kernel(z_ref, w_ref, uw_ref, l0, l1, l2, l3, out_ref, wt, lower):
+    prepare(z_ref, w_ref, (l0, l1, l2, l3), wt, lower)
+    products(uw_ref, None, out_ref, wt, lower)
+
+
+def second_kernel(z_ref, wt, uw_ref, lower, acc_ref, out_ref):
+    products(uw_ref, acc_ref, out_ref, wt, lower)
 
 
 def contract(body, args, outs):
@@ -149,23 +154,19 @@
         "qr,mlr->qlm", pick, upper, preferred_element_type=F32
     ).astype(BF16)
 
-    theirs = swapped(
-        jnp.concatenate([rights[16:].reshape(64, 128), isometry], axis=0), "zl"
-    )
-    far = swapped(isometry, "zh"), both_swapped(isometry)
-    own = ordered(zh, isometry, far[0])
-    other = ordered(zh, theirs[64:], far[1])
-    column = ordered(zl, own, other).reshape(4, 4, 2, 4, 4, 128)
+    both = jnp.concatenate([rights[16:].reshape(64, 128), isometry], axis=0)
+    before, after, across = along_z(both, 1), along_z(both, 3), along_z(isometry, 2)
+    column = jnp.stack([isometry, after[64:], across, before[64:]])
+    column = jnp.where(zl == 0, column, jnp.roll(column, 1, axis=0))
+    column = jnp.where(zh == 0, column, jnp.roll(column, 2, axis=0))
+    column = lax.optimization_barrier(column).reshape(4, 4, 2, 4, 4, 128)
     ks = column.transpose(1, 3, 2, 4, 0, 5)
-    ks = jnp.where(zl == 0, ks, ks[:, :, ::-1])
-
-    l01 = swapped(lower, "zh")
-    l10 = swapped(lower, "zl")
-    l11 = both_swapped(lower)
-    lowers = (lower, l01, l10, l11)
-
-    rights = ordered(zl, rights[:16], theirs[:64].reshape(16, 4, 128))
-    rights = rights.reshape(2, 16, 2, 2, 128).transpose(1, 3, 0, 2, 4)
+
+    lowers = (lower, along_z(lower, 1), along_z(lower, 2), along_z(lower, 3))
+
+    theirs = jnp.where(zl == 0, after[:64], before[:64]).reshape(16, 4, 128)
+    rights = ordered(zl, rights[:16], theirs)
+    rights = rights.reshape(2, 16, 2, 2, 128).transpose(1, 3, 2, 0, 4)
     send = jnp.concatenate(
         [
             jnp.broadcast_to(rights.reshape(1, 128, 128), (16, 128, 128)),
@@ -182,9 +183,9 @@
     uw = jnp.concatenate([u, got[:, 160:]])
     uw_other = swapped(uw, "c")
 
-    at = zh.astype(jnp.int32)[None]
+    at = (2 * zh + zl).astype(jnp.int32)[None]
     total = ((2, 2, 128, 128), F32)
-    kept = ((1024, 128), BF16), ((1024, 512), BF16)
+    kept = ((1024, 128), BF16), ((2, 1024, 256), BF16)
     acc, wt, low = contract(
         first_kernel, (at, w, uw, *lowers), (total, *kept)
     )

time: 77.8 us -> 78.2 us (level)
  waiting for transfers between devices: 14.4 us -> 15.8 us
  starting transfers between devices: 10.7 us -> 9.69 us
    ppermute x2 -> x6, waiting for transfers between devices: 3.47 us -> 15.8 us  [along_z(): lax.ppermute(value, ('zl', 'zh'), [(at(z), at((z + shift) % 4)) for z in...]
    ppermute x6 -> x2, waiting for transfers between devices: 10.9 us -> 0.01 us  [swapped(): return lax.ppermute(value, axis, [(0, 1), (1, 0)])]
    ppermute x6 -> x2, starting transfers between devices: 4.94 us -> 0.66 us  [swapped(): return lax.ppermute(value, axis, [(0, 1), (1, 0)])]
    ppermute x2 -> x6, starting transfers between devices: 5.75 us -> 9.03 us  [along_z(): lax.ppermute(value, ('zl', 'zh'), [(at(z), at((z + shift) % 4)) for z in...]
  transfers between devices with their start and end apart: 8 -> 8, of which waited for: 4 -> 5; matrix products, arithmetic and copies ran while one was open for 2% -> 2% of each run, Pallas kernels for 6% -> 6%
where the time goes in v8:
time: 78.2 us; the launch traced here: 77.9 us
  blocking collectives  39 us (50%)
  waiting for transfers between devices  15.8 us (20%)
  Pallas kernels  10.2 us (13%)
  starting transfers between devices  9.69 us (12%)
  other arithmetic  1.56 us (2%)
  local copies, waits for them, and re-layouts  1.36 us (2%)
    all_to_all x1, blocking collectives, on_device(): got = lax.all_to_all(send, ('x', 'y'), 0, 0, tiled=True)  23.8 us
    ppermute x6, waiting for transfers between devices, along_z(): lax.ppermute(value, ('zl', 'zh'), [(at(z), at((z + shift) % 4)) for z in...  15.8 us
    all_to_all x1, blocking collectives, on_device(): parts = lax.all_to_all(parts, ('x', 'zl', 'y', 'zh'), 0, 0, tiled=True)  15.1 us
    pallas_call x2, Pallas kernels, contract(): pl.pallas_call(body, in_specs=[pl.BlockSpec(memory_space=pltpu.SMEM)] + [...  9.13 us
    ppermute x6, starting transfers between devices, along_z(): lax.ppermute(value, ('zl', 'zh'), [(at(z), at((z + shift) % 4)) for z in...  9.03 us
  transfers between devices with their start and end apart: 8, of which 5 were waited for; matrix products, arithmetic and copies ran while one was open for 2% of the time, Pallas kernels for 6%

profile of v8, /device:TPU:0, one launch (start us, length us, event | category | flops | bytes accessed | tf_op | source)
XLA Modules:
  0.0 77.9 jit_solution(16978327413596370930)
XLA Ops:
  0.0 1.1 %fetch.1 = (bf16[128,128]{1,0:T(8,128)(2,1)S(1)}, bf16[128,4,128]{2,1,0:T(4,128)(2,1)S(1)}, bf16[128,4,2,128]{3,2,1,0:T(2,128)(2,1)S(1)}) custom-call(bf16[128,128]{1,0:T(8,128)(2,1)} %refs_0_.1, bf16[128,4,128]{2,1,0:T(4,128)(2,1)} %refs_1_.1, bf16[128,4,2,128]{3,2,1,0:T(2,128)(2,1)} %refs_2_.1), custom_call_target="tpu_custom_call" | custom-call | tf_op jit(solution)/shard_map/fetch/pallas_call | solution.py:131
  1.1 0.2 fusion
  1.3 2.1 %collective-permute-start.1 = (bf16[192,128]{1,0:T(8,128)(2,1)S(1)}, bf16[192,128]{1,0:T(8,128)(2,1)S(1)}, u32[]{:S(2)}, u32[]{:S(2)}) collective-permute-start(bf16[192,128]{1,0:T(8,128)(2,1)S(1)} %pad_maximum_fusion.3), channel_id=1, source_target_pairs={{0,16},{16,2},{2,18},{18,0},{1,17},{17,3},{3,19},{19,1},{4,20},{20... | collective-permute-start | bytes 147464 | tf_op jit(solution)/shard_map/ppermute | solution.py:22
  3.4 2.2 %collective-permute-start = (bf16[192,128]{1,0:T(8,128)(2,1)S(1)}, bf16[192,128]{1,0:T(8,128)(2,1)S(1)}, u32[]{:S(2)}, u32[]{:S(2)}) collective-permute-start(bf16[192,128]{1,0:T(8,128)(2,1)S(1)} %pad_maximum_fusion.3), channel_id=1, source_target_pairs={{0,18},{16,0},{2,16},{18,2},{1,19},{17,1},{3,17},{19,3},{4,22},{20... | collective-permute-start | bytes 147464 | tf_op jit(solution)/shard_map/ppermute | solution.py:22
  5.6 1.8 %collective-permute-start.2 = (bf16[128,128]{1,0:T(8,128)(2,1)S(1)}, bf16[128,128]{1,0:T(8,128)(2,1)S(1)}, u32[]{:S(2)}, u32[]{:S(2)}) collective-permute-start(bf16[128,128]{1,0:T(8,128)(2,1)S(1)} %get-tuple-element.12), channel_id=1, source_target_pairs={{0,2},{16,18},{2,0},{18,16},{1,3},{17,19},{3,1},{19,17},{4,6},{20,... | collective-permute-start | bytes 98312 | tf_op jit(solution)/shard_map/ppermute | solution.py:22
  7.4 0.2 collective-permute-done.1
  7.6 0.0 collective-permute-done
  7.7 3.3 %collective-permute-done.2 = bf16[128,128]{1,0:T(8,128)(2,1)S(1)} collective-permute-done((bf16[128,128]{1,0:T(8,128)(2,1)S(1)}, bf16[128,128]{1,0:T(8,128)(2,1)S(1)}, u32[]{:S(2)}, u32[]{:S(2)}) %collective-permute-start.2) | collective-permute-done | bytes 32800 | tf_op jit(solution)/shard_map/ppermute | solution.py:22
  11.1 0.1 copy.16
  11.2 0.1 broadcast_in_dim.30
  11.4 0.1 broadcast_in_dim.31
  11.5 0.1 pad_maximum_fusion
  11.5 23.8 %all_to_all.10 = bf16[16,288,128]{2,1,0:T(8,128)(2,1)S(1)} all-to-all(bf16[16,288,128]{2,1,0:T(8,128)(2,1)S(1)} %pad_maximum_fusion), channel_id=1, replica_groups=mesh['x'=4,'zl'=2,'y'=4,'zh'=2,'c'=2] {'x','y'}, dimensions={0} | all-to-all | bytes 2359296 | tf_op jit(solution)/shard_map/all_to_all | solution.py:178
  35.4 0.1 slice_bitcast_fusion
  35.4 0.1 copy.26
  35.6 0.1 pad_maximum_fusion.1.uw_ref
  35.7 0.1 collective-permute-start.7
  35.8 0.6 collective-permute-start.3
  36.4 1.7 %collective-permute-start.6 = (bf16[4,2,128,128]{3,2,1,0:T(8,128)(2,1)S(1)}, bf16[4,2,128,128]{3,2,1,0:T(8,128)(2,1)S(1)}, u32[]{:S(2)}, u32[]{:S(2)}) collective-permute-start(bf16[4,2,128,128]{3,2,1,0:T(8,128)(2,1)S(1)} %bitcast.52), channel_id=1, source_target_pairs={{0,18},{16,0},{2,16},{18,2},{1,19},{17,1},{3,17},{19,3},{4,22},{20... | collective-permute-start | bytes 786440 | tf_op jit(solution)/shard_map/ppermute | solution.py:22
  38.1 0.4 collective-permute-start.5
  38.4 0.9 %collective-permute-start.4 = (bf16[4,2,128,128]{3,2,1,0:T(8,128)(2,1)S(1)}, bf16[4,2,128,128]{3,2,1,0:T(8,128)(2,1)S(1)}, u32[]{:S(2)}, u32[]{:S(2)}) collective-permute-start(bf16[4,2,128,128]{3,2,1,0:T(8,128)(2,1)S(1)} %bitcast.54), channel_id=1, source_target_pairs={{0,16},{16,2},{2,18},{18,0},{1,17},{17,3},{3,19},{19,1},{4,20},{20... | collective-permute-start | bytes 786440 | tf_op jit(solution)/shard_map/ppermute | solution.py:22
  39.3 1.1 %pad_maximum_fusion.2 = bf16[2,8,16,4,128]{4,3,1,2,0:T(4,128)(2,1)S(1)} fusion(bf16[1,8,16,4,128]{4,3,1,2,0:T(4,128)(2,1)} %bitcast.20, bf16[1,8,16,4,128]{4,3,1,2,0:T(4,128)(2,1)S(1)} %bitcast.63), kind=kLoop, calls=%fused_computation.8 | loop fusion | flops 131072 | bytes 524288 | tf_op jit(solution)/shard_map/stack | solution.py:28
  40.4 0.1 fusion.1
  40.6 0.1 copy.17
  40.7 5.0 %collective-permute-done.6.l3 = bf16[4,2,128,128]{3,2,1,0:T(8,128)(2,1)S(1)} collective-permute-done((bf16[4,2,128,128]{3,2,1,0:T(8,128)(2,1)S(1)}, bf16[4,2,128,128]{3,2,1,0:T(8,128)(2,1)S(1)}, u32[]{:S(2)}, u32[]{:S(2)}) %collective-permute-start.6) | collective-permute-done | bytes 262176 | tf_op jit(solution)/shard_map/ppermute | solution.py:22
  45.6 3.1 %collective-permute-done.5.l2 = bf16[4,2,128,128]{3,2,1,0:T(8,128)(2,1)S(1)} collective-permute-done((bf16[4,2,128,128]{3,2,1,0:T(8,128)(2,1)S(1)}, bf16[4,2,128,128]{3,2,1,0:T(8,128)(2,1)S(1)}, u32[]{:S(2)}, u32[]{:S(2)}) %collective-permute-start.5) | collective-permute-done | bytes 262176 | tf_op jit(solution)/shard_map/ppermute | solution.py:22
  48.8 4.2 %collective-permute-done.4.l1 = bf16[4,2,128,128]{3,2,1,0:T(8,128)(2,1)S(1)} collective-permute-done((bf16[4,2,128,128]{3,2,1,0:T(8,128)(2,1)S(1)}, bf16[4,2,128,128]{3,2,1,0:T(8,128)(2,1)S(1)}, u32[]{:S(2)}, u32[]{:S(2)}) %collective-permute-start.4) | collective-permute-done | bytes 262176 | tf_op jit(solution)/shard_map/ppermute | solution.py:22
  52.9 4.7 %contract.2 = (f32[2,2,128,128]{3,2,1,0:T(8,128)S(1)}, bf16[1024,128]{1,0:T(8,128)(2,1)S(1)}, bf16[2,1024,256]{2,1,0:T(8,128)(2,1)S(1)}) custom-call(s32[1]{0:T(128)} %bitcast.z_ref, bf16[8,128,128]{2,1,0:T(8,128)(2,1)S(1)} %bitcast.56, bf16[32,128,128]{2,1,0:T(8,128)(2,1)S(1)} %pad_maximum_fusion.1.uw_ref, bf16[4,2,128,128]{3,2,1,0:T(8,128)(2,1)S(1)} %bitcast.55, ...), custom_call_target="tpu_custom_call" | custom-call | flops 4000000000 | bytes 4194304 | tf_op jit(solution)/shard_map/contract/pallas_call | solution.py:105
  57.6 4.5 %contract.3 = f32[2,2,128,128]{3,2,1,0:T(8,128)S(1)} custom-call(s32[1]{0:T(128)} %bitcast.z_ref, bf16[1024,128]{1,0:T(8,128)(2,1)S(1)} %get-tuple-element.14.wt, bf16[32,128,128]{2,1,0:T(8,128)(2,1)S(1)} %collective-permute-done.7.uw_ref, bf16[2,1024,256]{2,1,0:T(8,128)(2,1)S(1)} %get-tuple-element.15.lower, f32[2,2,128,128]{3,2,1,0:T(8,128)S(1)} %get-tuple-element.16.acc_ref), custom_call_target="tpu_custom_call" | custom-call | flops 4000000000 | bytes 4194304 | tf_op jit(solution)/shard_map/contract/pallas_call | solution.py:105
  62.1 15.1 %all_to_all.11 = f32[64,8,128]{2,1,0:T(8,128)S(1)} all-to-all(f32[64,8,128]{2,1,0:T(8,128)S(1)} %bitcast.59), channel_id=1, replica_groups=mesh['x'=4,'zl'=2,'y'=4,'zh'=2,'c'=2] {'x','zl','y','zh'}, dimensions={0} | all-to-all | bytes 524288 | tf_op jit(solution)/shard_map/all_to_all | solution.py:195
  77.3 0.1 reduce_sum.9
  77.3 0.6 copy.21
  (19 shorter events, 0.3 us)
Async XLA Ops:
  1.3 6.3 %collective-permute-start.1 = (bf16[192,128]{1,0:T(8,128)(2,1)S(1)}, bf16[192,128]{1,0:T(8,128)(2,1)S(1)}, u32[]{:S(2)}, u32[]{:S(2)}) collective-permute-start(bf16[192,128]{1,0:T(8,128)(2,1)S(1)} %pad_maximum_fusion.3), channel_id=1, source_target_pairs={{0,16},{16,2},{2,18},{18,0},{1,17},{17,3},{3,19},{19,1},{4,20},{20... | collective-permute-start | bytes 147464 | tf_op jit(solution)/shard_map/ppermute | solution.py:22
  3.4 4.2 %collective-permute-start = (bf16[192,128]{1,0:T(8,128)(2,1)S(1)}, bf16[192,128]{1,0:T(8,128)(2,1)S(1)}, u32[]{:S(2)}, u32[]{:S(2)}) collective-permute-start(bf16[192,128]{1,0:T(8,128)(2,1)S(1)} %pad_maximum_fusion.3), channel_id=1, source_target_pairs={{0,18},{16,0},{2,16},{18,2},{1,19},{17,1},{3,17},{19,3},{4,22},{20... | collective-permute-start | bytes 147464 | tf_op jit(solution)/shard_map/ppermute | solution.py:22
  5.6 5.4 %collective-permute-start.2 = (bf16[128,128]{1,0:T(8,128)(2,1)S(1)}, bf16[128,128]{1,0:T(8,128)(2,1)S(1)}, u32[]{:S(2)}, u32[]{:S(2)}) collective-permute-start(bf16[128,128]{1,0:T(8,128)(2,1)S(1)} %get-tuple-element.12), channel_id=1, source_target_pairs={{0,2},{16,18},{2,0},{18,16},{1,3},{17,19},{3,1},{19,17},{4,6},{20,... | collective-permute-start | bytes 98312 | tf_op jit(solution)/shard_map/ppermute | solution.py:22
  35.7 21.9 %collective-permute-start.7 = (bf16[32,128,128]{2,1,0:T(8,128)(2,1)S(1)}, bf16[32,128,128]{2,1,0:T(8,128)(2,1)S(1)}, u32[]{:S(2)}, u32[]{:S(2)}) collective-permute-start(bf16[32,128,128]{2,1,0:T(8,128)(2,1)S(1)} %pad_maximum_fusion.1.uw_ref), channel_id=1, source_target_pairs={{0,1},{1,0},{2,3},{3,2},{4,5},{5,4},{6,7},{7,6},{8,9},{9,8},{10,11... | collective-permute-start | bytes 3145736 | tf_op jit(solution)/shard_map/ppermute | solution.py:15
  35.8 3.6 %collective-permute-start.3 = (bf16[8,16,4,128]{3,2,0,1:T(4,128)(2,1)S(1)}, bf16[8,16,4,128]{3,2,0,1:T(4,128)(2,1)}, u32[]{:S(2)}, u32[]{:S(2)}) collective-permute-start(bf16[8,16,4,128]{3,2,0,1:T(4,128)(2,1)S(1)} %bitcast.62), channel_id=1, source_target_pairs={{0,1},{1,0},{2,3},{3,2},{4,5},{5,4},{6,7},{7,6},{8,9},{9,8},{10,11... | collective-permute-start | bytes 393224 | tf_op jit(solution)/shard_map/ppermute | solution.py:15
  36.4 9.2 %collective-permute-start.6 = (bf16[4,2,128,128]{3,2,1,0:T(8,128)(2,1)S(1)}, bf16[4,2,128,128]{3,2,1,0:T(8,128)(2,1)S(1)}, u32[]{:S(2)}, u32[]{:S(2)}) collective-permute-start(bf16[4,2,128,128]{3,2,1,0:T(8,128)(2,1)S(1)} %bitcast.52), channel_id=1, source_target_pairs={{0,18},{16,0},{2,16},{18,2},{1,19},{17,1},{3,17},{19,3},{4,22},{20... | collective-permute-start | bytes 786440 | tf_op jit(solution)/shard_map/ppermute | solution.py:22
  38.1 10.7 %collective-permute-start.5 = (bf16[4,2,128,128]{3,2,1,0:T(8,128)(2,1)S(1)}, bf16[4,2,128,128]{3,2,1,0:T(8,128)(2,1)S(1)}, u32[]{:S(2)}, u32[]{:S(2)}) collective-permute-start(bf16[4,2,128,128]{3,2,1,0:T(8,128)(2,1)S(1)} %bitcast.53), channel_id=1, source_target_pairs={{0,2},{16,18},{2,0},{18,16},{1,3},{17,19},{3,1},{19,17},{4,6},{20,... | collective-permute-start | bytes 786440 | tf_op jit(solution)/shard_map/ppermute | solution.py:22
  38.4 14.5 %collective-permute-start.4 = (bf16[4,2,128,128]{3,2,1,0:T(8,128)(2,1)S(1)}, bf16[4,2,128,128]{3,2,1,0:T(8,128)(2,1)S(1)}, u32[]{:S(2)}, u32[]{:S(2)}) collective-permute-start(bf16[4,2,128,128]{3,2,1,0:T(8,128)(2,1)S(1)} %bitcast.54), channel_id=1, source_target_pairs={{0,16},{16,2},{2,18},{18,0},{1,17},{17,3},{3,19},{19,1},{4,20},{20... | collective-permute-start | bytes 786440 | tf_op jit(solution)/shard_map/ppermute | solution.py:22

commit v9 on v8

--- a/solution.py
+++ b/solution.py
@@ -39,16 +39,29 @@
 def prepare(z_ref, w_ref, lows, wt, lower):
     for k in range(8):
         wt[k * 128 : (k + 1) * 128, :] = w_ref[k].T
-    for shift in range(4):
-        z = (z_ref[0] + 4 - shift) % 4
+
+    def place(ref, row, col):
         for j in range(4):
-            row = pl.multiple_of(((z % 2) * 4 + j) * 128, 128)
             for e in range(2):
-                block = lows[shift][j, e]
-                lower[z // 2, pl.ds(row, 128), e * 128 : (e + 1) * 128] = block
-
-
-def products(uw_ref, acc_ref, out_ref, wt, lower):
+                rows = slice(row + j * 128, row + (j + 1) * 128)
+                lower[rows, col + e * 128 : col + (e + 1) * 128] = ref[j, e]
+
+    here, before, across, after = lows
+    place(here, 0, 0)
+    place(across, 0, 256)
+
+    @pl.when(z_ref[0] == 0)
+    def _():
+        place(after, 512, 0)
+        place(before, 512, 256)
+
+    @pl.when(z_ref[0] != 0)
+    def _():
+        place(before, 512, 0)
+        place(after, 512, 256)
+
+
+def products(zh, uw_ref, acc_ref, out_ref, wt, lower):
     count = uw_ref.shape[0] // 2
     for at in range(0, count, QB):
         u = jnp.concatenate([uw_ref[at + q] for q in range(QB)], axis=1)
@@ -66,38 +79,39 @@
             ],
             axis=0,
         )
-        paired = [mm(left, lower[zh]).astype(BF16) for zh in range(2)]
+        paired = mm(left, lower[...]).astype(BF16)
         rows = jnp.concatenate(
             [
                 jnp.concatenate(
                     [
-                        paired[zh][q * 128 : (q + 1) * 128, e * 128 : (e + 1) * 128]
+                        paired[q * 128 : (q + 1) * 128, d * 128 : (d + 1) * 128]
                         for q in range(QB)
                     ],
                     axis=1,
                 )
-                for zh in range(2)
-                for e in range(2)
+                for d in range(4)
             ],
             axis=0,
         )
         slabs = uw_ref[count + at : count + at + QB].reshape(QB * 128, 128)
         part = mm(rows, slabs).reshape(2, 2, 128, 128)
-        if at > 0:
-            out_ref[...] += part
-        elif acc_ref is None:
-            out_ref[...] = part
-        else:
-            out_ref[...] = acc_ref[...] + part
+        for zd in range(2):
+            to = zh if zd == 0 else 1 - zh
+            if at > 0:
+                out_ref[to] += part[zd]
+            elif acc_ref is None:
+                out_ref[to] = part[zd]
+            else:
+                out_ref[to] = acc_ref[to] + part[zd]
 
 
 def first_kernel(z_ref, w_ref, uw_ref, l0, l1, l2, l3, out_ref, wt, lower):
     prepare(z_ref, w_ref, (l0, l1, l2, l3), wt, lower)
-    products(uw_ref, None, out_ref, wt, lower)
+    products(z_ref[1], uw_ref, None, out_ref, wt, lower)
 
 
 def second_kernel(z_ref, wt, uw_ref, lower, acc_ref, out_ref):
-    products(uw_ref, acc_ref, out_ref, wt, lower)
+    products(z_ref[1], uw_ref, acc_ref, out_ref, wt, lower)
 
 
 def contract(body, args, outs):
@@ -161,6 +175,7 @@
     column = jnp.where(zh == 0, column, jnp.roll(column, 2, axis=0))
     column = lax.optimization_barrier(column).reshape(4, 4, 2, 4, 4, 128)
     ks = column.transpose(1, 3, 2, 4, 0, 5)
+    ks = jnp.where(zl == 0, ks, ks[:, :, ::-1])
 
     lowers = (lower, along_z(lower, 1), along_z(lower, 2), along_z(lower, 3))
 
@@ -178,14 +193,16 @@
     got = lax.all_to_all(send, ("x", "y"), 0, 0, tiled=True)
     w = got[:, 128:160].reshape(16, 8, 4, 128).transpose(1, 0, 2, 3)
     u = got[:, :128].reshape(16, 16, 8, 128).transpose(1, 0, 2, 3).reshape(16, 128, 128)
-    w = ordered(c, w, swapped(w, "c"))
-    w = w.transpose(1, 2, 0, 3, 4).reshape(8, 128, 128)
+    other = swapped(w, "c")
+    w = jnp.concatenate(
+        [jnp.where(c == 0, w, other), jnp.where(c == 0, other, w)], axis=2
+    ).reshape(8, 128, 128)
     uw = jnp.concatenate([u, got[:, 160:]])
     uw_other = swapped(uw, "c")
 
-    at = (2 * zh + zl).astype(jnp.int32)[None]
+    at = jnp.stack([zl, zh]).astype(jnp.int32)
     total = ((2, 2, 128, 128), F32)
-    kept = ((1024, 128), BF16), ((2, 1024, 256), BF16)
+    kept = ((1024, 128), BF16), ((1024, 512), BF16)
     acc, wt, low = contract(
         first_kernel, (at, w, uw, *lowers), (total, *kept)
     )

time: 78.2 us -> 78.8 us (level)
    another operation x2 -> x1, other arithmetic: 1.1 us -> 0.01 us  [ordered(): both = jnp.stack([own, other])]
    select_n x0 -> x2, other arithmetic: none -> 0.98 us  [the longest x1 0.93 us: on_device(): jnp.where(c == 0, w, other)]
where the time goes in v9:
time: 78.8 us; the launch traced here: 78.6 us
  blocking collectives  39 us (49%)
  waiting for transfers between devices  15.9 us (20%)
  Pallas kernels  10.8 us (14%)
  starting transfers between devices  9.69 us (12%)
  other arithmetic  1.55 us (2%)
  local copies, waits for them, and re-layouts  1.27 us (2%)
    all_to_all x1, blocking collectives, on_device(): got = lax.all_to_all(send, ('x', 'y'), 0, 0, tiled=True)  23.8 us
    ppermute x6, waiting for transfers between devices, along_z(): lax.ppermute(value, ('zl', 'zh'), [(at(z), at((z + shift) % 4)) for z in...  15.9 us
    all_to_all x1, blocking collectives, on_device(): parts = lax.all_to_all(parts, ('x', 'zl', 'y', 'zh'), 0, 0, tiled=True)  15.1 us
    pallas_call x2, Pallas kernels, contract(): pl.pallas_call(body, in_specs=[pl.BlockSpec(memory_space=pltpu.SMEM)] + [...  9.69 us
    ppermute x6, starting transfers between devices, along_z(): lax.ppermute(value, ('zl', 'zh'), [(at(z), at((z + shift) % 4)) for z in...  9.03 us
  transfers between devices with their start and end apart: 8, of which 5 were waited for; matrix products, arithmetic and copies ran while one was open for 2% of the time, Pallas kernels for 6%

profile of v9, /device:TPU:0, one launch (start us, length us, event | category | flops | bytes accessed | tf_op | source)
XLA Modules:
  0.0 78.6 jit_solution(809428757545882725)
XLA Ops:
  0.0 1.1 %fetch.1 = (bf16[128,128]{1,0:T(8,128)(2,1)S(1)}, bf16[128,4,128]{2,1,0:T(4,128)(2,1)S(1)}, bf16[128,4,2,128]{3,2,1,0:T(2,128)(2,1)S(1)}) custom-call(bf16[128,128]{1,0:T(8,128)(2,1)} %refs_0_.1, bf16[128,4,128]{2,1,0:T(4,128)(2,1)} %refs_1_.1, bf16[128,4,2,128]{3,2,1,0:T(2,128)(2,1)} %refs_2_.1), custom_call_target="tpu_custom_call" | custom-call | tf_op jit(solution)/shard_map/fetch/pallas_call | solution.py:145
  1.1 0.2 fusion
  1.3 2.1 %collective-permute-start.1 = (bf16[192,128]{1,0:T(8,128)(2,1)S(1)}, bf16[192,128]{1,0:T(8,128)(2,1)S(1)}, u32[]{:S(2)}, u32[]{:S(2)}) collective-permute-start(bf16[192,128]{1,0:T(8,128)(2,1)S(1)} %pad_maximum_fusion.3), channel_id=1, source_target_pairs={{0,16},{16,2},{2,18},{18,0},{1,17},{17,3},{3,19},{19,1},{4,20},{20... | collective-permute-start | bytes 147464 | tf_op jit(solution)/shard_map/ppermute | solution.py:22
  3.4 2.2 %collective-permute-start = (bf16[192,128]{1,0:T(8,128)(2,1)S(1)}, bf16[192,128]{1,0:T(8,128)(2,1)S(1)}, u32[]{:S(2)}, u32[]{:S(2)}) collective-permute-start(bf16[192,128]{1,0:T(8,128)(2,1)S(1)} %pad_maximum_fusion.3), channel_id=1, source_target_pairs={{0,18},{16,0},{2,16},{18,2},{1,19},{17,1},{3,17},{19,3},{4,22},{20... | collective-permute-start | bytes 147464 | tf_op jit(solution)/shard_map/ppermute | solution.py:22
  5.6 1.8 %collective-permute-start.2 = (bf16[128,128]{1,0:T(8,128)(2,1)S(1)}, bf16[128,128]{1,0:T(8,128)(2,1)S(1)}, u32[]{:S(2)}, u32[]{:S(2)}) collective-permute-start(bf16[128,128]{1,0:T(8,128)(2,1)S(1)} %get-tuple-element.12), channel_id=1, source_target_pairs={{0,2},{16,18},{2,0},{18,16},{1,3},{17,19},{3,1},{19,17},{4,6},{20,... | collective-permute-start | bytes 98312 | tf_op jit(solution)/shard_map/ppermute | solution.py:22
  7.4 0.2 collective-permute-done.1
  7.7 3.3 %collective-permute-done.2 = bf16[128,128]{1,0:T(8,128)(2,1)S(1)} collective-permute-done((bf16[128,128]{1,0:T(8,128)(2,1)S(1)}, bf16[128,128]{1,0:T(8,128)(2,1)S(1)}, u32[]{:S(2)}, u32[]{:S(2)}) %collective-permute-start.2) | collective-permute-done | bytes 32800 | tf_op jit(solution)/shard_map/ppermute | solution.py:22
  11.1 0.1 copy.30
  11.2 0.1 reverse_select_fusion
  11.3 0.1 broadcast_in_dim.26
  11.4 0.1 broadcast_in_dim.27
  11.5 0.1 pad_maximum_fusion
  11.6 23.8 %all_to_all.10 = bf16[16,288,128]{2,1,0:T(8,128)(2,1)S(1)} all-to-all(bf16[16,288,128]{2,1,0:T(8,128)(2,1)S(1)} %pad_maximum_fusion), channel_id=1, replica_groups=mesh['x'=4,'zl'=2,'y'=4,'zh'=2,'c'=2] {'x','y'}, dimensions={0} | all-to-all | bytes 2359296 | tf_op jit(solution)/shard_map/all_to_all | solution.py:193
  35.4 0.1 slice_bitcast_fusion
  35.5 0.1 copy.28
  35.6 0.1 pad_maximum_fusion.1.uw_ref
  35.7 0.1 collective-permute-start.7
  35.8 0.6 collective-permute-start.3
  36.5 1.7 %collective-permute-start.6 = (bf16[4,2,128,128]{3,2,1,0:T(8,128)(2,1)S(1)}, bf16[4,2,128,128]{3,2,1,0:T(8,128)(2,1)S(1)}, u32[]{:S(2)}, u32[]{:S(2)}) collective-permute-start(bf16[4,2,128,128]{3,2,1,0:T(8,128)(2,1)S(1)} %bitcast.54), channel_id=1, source_target_pairs={{0,18},{16,0},{2,16},{18,2},{1,19},{17,1},{3,17},{19,3},{4,22},{20... | collective-permute-start | bytes 786440 | tf_op jit(solution)/shard_map/ppermute | solution.py:22
  38.1 0.4 collective-permute-start.5
  38.5 0.9 %collective-permute-start.4 = (bf16[4,2,128,128]{3,2,1,0:T(8,128)(2,1)S(1)}, bf16[4,2,128,128]{3,2,1,0:T(8,128)(2,1)S(1)}, u32[]{:S(2)}, u32[]{:S(2)}) collective-permute-start(bf16[4,2,128,128]{3,2,1,0:T(8,128)(2,1)S(1)} %bitcast.56), channel_id=1, source_target_pairs={{0,16},{16,2},{2,18},{18,0},{1,17},{17,3},{3,19},{19,1},{4,20},{20... | collective-permute-start | bytes 786440 | tf_op jit(solution)/shard_map/ppermute | solution.py:22
  39.4 0.1 pad_add_fusion.z_ref
  39.5 0.9 %broadcast_select_fusion.1 = (bf16[4,16,8,128]{3,2,0,1:T(8,128)(2,1)S(1)}, bf16[4,16,8,128]{3,2,0,1:T(8,128)(2,1)S(1)}) fusion(bf16[4,16,8,128]{3,2,0,1:T(8,128)(2,1)S(1)} %bitcast.62, bf16[4,16,8,128]{3,2,0,1:T(8,128)(2,1)} %bitcast.49, pred[]{:T(512)S(6)} %eq.15), kind=kLoop, calls=%fused_computation.15 | loop fusion | flops 131072 | bytes 524289 | tf_op jit(solution)/shard_map/jit(_where)/select_n | solution.py:198
  40.4 0.1 copy_bitcast_fusion.2.w_ref
  40.6 5.1 %collective-permute-done.6.l3 = bf16[4,2,128,128]{3,2,1,0:T(8,128)(2,1)S(1)} collective-permute-done((bf16[4,2,128,128]{3,2,1,0:T(8,128)(2,1)S(1)}, bf16[4,2,128,128]{3,2,1,0:T(8,128)(2,1)S(1)}, u32[]{:S(2)}, u32[]{:S(2)}) %collective-permute-start.6) | collective-permute-done | bytes 262176 | tf_op jit(solution)/shard_map/ppermute | solution.py:22
  45.7 3.1 %collective-permute-done.5.l2 = bf16[4,2,128,128]{3,2,1,0:T(8,128)(2,1)S(1)} collective-permute-done((bf16[4,2,128,128]{3,2,1,0:T(8,128)(2,1)S(1)}, bf16[4,2,128,128]{3,2,1,0:T(8,128)(2,1)S(1)}, u32[]{:S(2)}, u32[]{:S(2)}) %collective-permute-start.5) | collective-permute-done | bytes 262176 | tf_op jit(solution)/shard_map/ppermute | solution.py:22
  48.8 4.2 %collective-permute-done.4.l1 = bf16[4,2,128,128]{3,2,1,0:T(8,128)(2,1)S(1)} collective-permute-done((bf16[4,2,128,128]{3,2,1,0:T(8,128)(2,1)S(1)}, bf16[4,2,128,128]{3,2,1,0:T(8,128)(2,1)S(1)}, u32[]{:S(2)}, u32[]{:S(2)}) %collective-permute-start.4) | collective-permute-done | bytes 262176 | tf_op jit(solution)/shard_map/ppermute | solution.py:22
  53.0 5.0 %contract.2 = (f32[2,2,128,128]{3,2,1,0:T(8,128)S(1)}, bf16[1024,128]{1,0:T(8,128)(2,1)S(1)}, bf16[1024,512]{1,0:T(8,128)(2,1)S(1)}) custom-call(s32[2]{0:T(128)S(1)} %pad_add_fusion.z_ref, bf16[8,128,128]{2,1,0:T(8,128)(2,1)S(1)} %copy_bitcast_fusion.2.w_ref, bf16[32,128,128]{2,1,0:T(8,128)(2,1)S(1)} %pad_maximum_fusion.1.uw_ref, ...), custom_call_target="tpu_custom_call" | custom-call | flops 4000000000 | bytes 4194304 | tf_op jit(solution)/shard_map/contract/pallas_call | solution.py:119
  58.1 4.6 %contract.3 = f32[2,2,128,128]{3,2,1,0:T(8,128)S(1)} custom-call(s32[2]{0:T(128)S(1)} %pad_add_fusion.z_ref, bf16[1024,128]{1,0:T(8,128)(2,1)S(1)} %get-tuple-element.14.wt, bf16[32,128,128]{2,1,0:T(8,128)(2,1)S(1)} %collective-permute-done.7.uw_ref, bf16[1024,512]{1,0:T(8,128)(2,1)S(1)} %get-tuple-element.15.lower, ...), custom_call_target="tpu_custom_call" | custom-call | flops 4000000000 | bytes 4194304 | tf_op jit(solution)/shard_map/contract/pallas_call | solution.py:119
  62.8 15.1 %all_to_all.11 = f32[64,8,128]{2,1,0:T(8,128)S(1)} all-to-all(f32[64,8,128]{2,1,0:T(8,128)S(1)} %bitcast.60), channel_id=1, replica_groups=mesh['x'=4,'zl'=2,'y'=4,'zh'=2,'c'=2] {'x','zl','y','zh'}, dimensions={0} | all-to-all | bytes 524288 | tf_op jit(solution)/shard_map/all_to_all | solution.py:212
  77.9 0.1 reduce_sum.9
  78.0 0.6 copy.21
  (20 shorter events, 0.3 us)
Async XLA Ops:
  1.3 6.3 %collective-permute-start.1 = (bf16[192,128]{1,0:T(8,128)(2,1)S(1)}, bf16[192,128]{1,0:T(8,128)(2,1)S(1)}, u32[]{:S(2)}, u32[]{:S(2)}) collective-permute-start(bf16[192,128]{1,0:T(8,128)(2,1)S(1)} %pad_maximum_fusion.3), channel_id=1, source_target_pairs={{0,16},{16,2},{2,18},{18,0},{1,17},{17,3},{3,19},{19,1},{4,20},{20... | collective-permute-start | bytes 147464 | tf_op jit(solution)/shard_map/ppermute | solution.py:22
  3.4 4.2 %collective-permute-start = (bf16[192,128]{1,0:T(8,128)(2,1)S(1)}, bf16[192,128]{1,0:T(8,128)(2,1)S(1)}, u32[]{:S(2)}, u32[]{:S(2)}) collective-permute-start(bf16[192,128]{1,0:T(8,128)(2,1)S(1)} %pad_maximum_fusion.3), channel_id=1, source_target_pairs={{0,18},{16,0},{2,16},{18,2},{1,19},{17,1},{3,17},{19,3},{4,22},{20... | collective-permute-start | bytes 147464 | tf_op jit(solution)/shard_map/ppermute | solution.py:22
  5.6 5.4 %collective-permute-start.2 = (bf16[128,128]{1,0:T(8,128)(2,1)S(1)}, bf16[128,128]{1,0:T(8,128)(2,1)S(1)}, u32[]{:S(2)}, u32[]{:S(2)}) collective-permute-start(bf16[128,128]{1,0:T(8,128)(2,1)S(1)} %get-tuple-element.12), channel_id=1, source_target_pairs={{0,2},{16,18},{2,0},{18,16},{1,3},{17,19},{3,1},{19,17},{4,6},{20,... | collective-permute-start | bytes 98312 | tf_op jit(solution)/shard_map/ppermute | solution.py:22
  35.7 22.3 %collective-permute-start.7 = (bf16[32,128,128]{2,1,0:T(8,128)(2,1)S(1)}, bf16[32,128,128]{2,1,0:T(8,128)(2,1)S(1)}, u32[]{:S(2)}, u32[]{:S(2)}) collective-permute-start(bf16[32,128,128]{2,1,0:T(8,128)(2,1)S(1)} %pad_maximum_fusion.1.uw_ref), channel_id=1, source_target_pairs={{0,1},{1,0},{2,3},{3,2},{4,5},{5,4},{6,7},{7,6},{8,9},{9,8},{10,11... | collective-permute-start | bytes 3145736 | tf_op jit(solution)/shard_map/ppermute | solution.py:15
  35.8 3.6 %collective-permute-start.3 = (bf16[8,16,4,128]{3,2,0,1:T(4,128)(2,1)S(1)}, bf16[8,16,4,128]{3,2,0,1:T(4,128)(2,1)}, u32[]{:S(2)}, u32[]{:S(2)}) collective-permute-start(bf16[8,16,4,128]{3,2,0,1:T(4,128)(2,1)S(1)} %bitcast.61), channel_id=1, source_target_pairs={{0,1},{1,0},{2,3},{3,2},{4,5},{5,4},{6,7},{7,6},{8,9},{9,8},{10,11... | collective-permute-start | bytes 393224 | tf_op jit(solution)/shard_map/ppermute | solution.py:15
  36.5 9.2 %collective-permute-start.6 = (bf16[4,2,128,128]{3,2,1,0:T(8,128)(2,1)S(1)}, bf16[4,2,128,128]{3,2,1,0:T(8,128)(2,1)S(1)}, u32[]{:S(2)}, u32[]{:S(2)}) collective-permute-start(bf16[4,2,128,128]{3,2,1,0:T(8,128)(2,1)S(1)} %bitcast.54), channel_id=1, source_target_pairs={{0,18},{16,0},{2,16},{18,2},{1,19},{17,1},{3,17},{19,3},{4,22},{20... | collective-permute-start | bytes 786440 | tf_op jit(solution)/shard_map/ppermute | solution.py:22
  38.1 10.7 %collective-permute-start.5 = (bf16[4,2,128,128]{3,2,1,0:T(8,128)(2,1)S(1)}, bf16[4,2,128,128]{3,2,1,0:T(8,128)(2,1)S(1)}, u32[]{:S(2)}, u32[]{:S(2)}) collective-permute-start(bf16[4,2,128,128]{3,2,1,0:T(8,128)(2,1)S(1)} %bitcast.55), channel_id=1, source_target_pairs={{0,2},{16,18},{2,0},{18,16},{1,3},{17,19},{3,1},{19,17},{4,6},{20,... | collective-permute-start | bytes 786440 | tf_op jit(solution)/shard_map/ppermute | solution.py:22
  38.5 14.5 %collective-permute-start.4 = (bf16[4,2,128,128]{3,2,1,0:T(8,128)(2,1)S(1)}, bf16[4,2,128,128]{3,2,1,0:T(8,128)(2,1)S(1)}, u32[]{:S(2)}, u32[]{:S(2)}) collective-permute-start(bf16[4,2,128,128]{3,2,1,0:T(8,128)(2,1)S(1)} %bitcast.56), channel_id=1, source_target_pairs={{0,16},{16,2},{2,18},{18,0},{1,17},{17,3},{3,19},{19,1},{4,20},{20... | collective-permute-start | bytes 786440 | tf_op jit(solution)/shard_map/ppermute | solution.py:22

commit v10 on v9

--- a/solution.py
+++ b/solution.py
@@ -36,7 +36,7 @@
 QB = 4
 
 
-def prepare(z_ref, w_ref, lows, wt, lower):
+def prepare(zl, w_ref, lows, wt, lower):
     for k in range(8):
         wt[k * 128 : (k + 1) * 128, :] = w_ref[k].T
 
@@ -50,12 +50,12 @@
     place(here, 0, 0)
     place(across, 0, 256)
 
-    @pl.when(z_ref[0] == 0)
+    @pl.when(zl == 0)
     def _():
         place(after, 512, 0)
         place(before, 512, 256)
 
-    @pl.when(z_ref[0] != 0)
+    @pl.when(zl != 0)
     def _():
         place(before, 512, 0)
         place(after, 512, 256)
@@ -105,20 +105,20 @@
                 out_ref[to] = acc_ref[to] + part[zd]
 
 
-def first_kernel(z_ref, w_ref, uw_ref, l0, l1, l2, l3, out_ref, wt, lower):
-    prepare(z_ref, w_ref, (l0, l1, l2, l3), wt, lower)
-    products(z_ref[1], uw_ref, None, out_ref, wt, lower)
-
-
-def second_kernel(z_ref, wt, uw_ref, lower, acc_ref, out_ref):
-    products(z_ref[1], uw_ref, acc_ref, out_ref, wt, lower)
-
-
-def contract(body, args, outs):
+def first_kernel(zl_ref, zh_ref, w_ref, uw_ref, l0, l1, l2, l3, out_ref, wt, lower):
+    prepare(zl_ref[0], w_ref, (l0, l1, l2, l3), wt, lower)
+    products(zh_ref[0], uw_ref, None, out_ref, wt, lower)
+
+
+def second_kernel(zh_ref, wt, uw_ref, lower, acc_ref, out_ref):
+    products(zh_ref[0], uw_ref, acc_ref, out_ref, wt, lower)
+
+
+def contract(body, scalars, args, outs):
     vmem = pl.BlockSpec(memory_space=pltpu.VMEM)
     return pl.pallas_call(
         body,
-        in_specs=[pl.BlockSpec(memory_space=pltpu.SMEM)] + [vmem] * (len(args) - 1),
+        in_specs=[pl.BlockSpec(memory_space=pltpu.SMEM)] * len(scalars) + [vmem] * len(args),
         out_specs=[vmem] * len(outs),
         out_shape=[jax.ShapeDtypeStruct(*out) for out in outs],
         compiler_params=pltpu.CompilerParams(vmem_limit_bytes=40 * 1024 * 1024),
@@ -126,7 +126,7 @@
             flops=4 * 10**9, bytes_accessed=4 * 2**20, transcendentals=0
         ),
         name="contract",
-    )(*args)
+    )(*scalars, *args)
 
 
 def fetch_kernel(*refs):
@@ -200,13 +200,13 @@
     uw = jnp.concatenate([u, got[:, 160:]])
     uw_other = swapped(uw, "c")
 
-    at = jnp.stack([zl, zh]).astype(jnp.int32)
+    here, there = zl.astype(jnp.int32)[None], zh.astype(jnp.int32)[None]
     total = ((2, 2, 128, 128), F32)
     kept = ((1024, 128), BF16), ((1024, 512), BF16)
     acc, wt, low = contract(
-        first_kernel, (at, w, uw, *lowers), (total, *kept)
-    )
-    (acc,) = contract(second_kernel, (at, wt, uw_other, low, acc), (total,))
+        first_kernel, (here, there), (w, uw, *lowers), (total, *kept)
+    )
+    (acc,) = contract(second_kernel, (there,), (wt, uw_other, low, acc), (total,))
 
     parts = acc.reshape(2, 2, 32, 4, 128).transpose(2, 0, 1, 3, 4).reshape(64, 8, 128)
     parts = lax.all_to_all(parts, ("x", "zl", "y", "zh"), 0, 0, tiled=True)

time: 78.8 us -> 77.7 us (0.986)
  Pallas kernels: 10.8 us -> 9.67 us
    pallas_call x2, Pallas kernels: 9.69 us -> 8.61 us  [contract(): pl.pallas_call(body, in_specs=[pl.BlockSpec(memory_space=pltpu.SMEM)] * l...]
where the time goes in v10:
time: 77.7 us; the launch traced here: 77.5 us
  blocking collectives  39 us (50%)
  waiting for transfers between devices  16 us (21%)
  starting transfers between devices  9.69 us (12%)
  Pallas kernels  9.67 us (12%)
  other arithmetic  1.47 us (2%)
  local copies, waits for them, and re-layouts  1.27 us (2%)
    all_to_all x1, blocking collectives, on_device(): got = lax.all_to_all(send, ('x', 'y'), 0, 0, tiled=True)  23.8 us
    ppermute x6, waiting for transfers between devices, along_z(): lax.ppermute(value, ('zl', 'zh'), [(at(z), at((z + shift) % 4)) for z in...  16 us
    all_to_all x1, blocking collectives, on_device(): parts = lax.all_to_all(parts, ('x', 'zl', 'y', 'zh'), 0, 0, tiled=True)  15.1 us
    ppermute x6, starting transfers between devices, along_z(): lax.ppermute(value, ('zl', 'zh'), [(at(z), at((z + shift) % 4)) for z in...  9.03 us
    pallas_call x2, Pallas kernels, contract(): pl.pallas_call(body, in_specs=[pl.BlockSpec(memory_space=pltpu.SMEM)] * l...  8.61 us
  transfers between devices with their start and end apart: 8, of which 5 were waited for; matrix products, arithmetic and copies ran while one was open for 2% of the time, Pallas kernels for 6%

profile of v10, /device:TPU:0, one launch (start us, length us, event | category | flops | bytes accessed | tf_op | source)
XLA Modules:
  0.0 77.5 jit_solution(1284380978631991135)
XLA Ops:
  0.0 1.1 %fetch.1 = (bf16[128,128]{1,0:T(8,128)(2,1)S(1)}, bf16[128,4,128]{2,1,0:T(4,128)(2,1)S(1)}, bf16[128,4,2,128]{3,2,1,0:T(2,128)(2,1)S(1)}) custom-call(bf16[128,128]{1,0:T(8,128)(2,1)} %refs_0_.1, bf16[128,4,128]{2,1,0:T(4,128)(2,1)} %refs_1_.1, bf16[128,4,2,128]{3,2,1,0:T(2,128)(2,1)} %refs_2_.1), custom_call_target="tpu_custom_call" | custom-call | tf_op jit(solution)/shard_map/fetch/pallas_call | solution.py:145
  1.1 0.2 fusion
  1.3 2.1 %collective-permute-start.1 = (bf16[192,128]{1,0:T(8,128)(2,1)S(1)}, bf16[192,128]{1,0:T(8,128)(2,1)S(1)}, u32[]{:S(2)}, u32[]{:S(2)}) collective-permute-start(bf16[192,128]{1,0:T(8,128)(2,1)S(1)} %pad_maximum_fusion.3), channel_id=1, source_target_pairs={{0,16},{16,2},{2,18},{18,0},{1,17},{17,3},{3,19},{19,1},{4,20},{20... | collective-permute-start | bytes 147464 | tf_op jit(solution)/shard_map/ppermute | solution.py:22
  3.4 2.2 %collective-permute-start = (bf16[192,128]{1,0:T(8,128)(2,1)S(1)}, bf16[192,128]{1,0:T(8,128)(2,1)S(1)}, u32[]{:S(2)}, u32[]{:S(2)}) collective-permute-start(bf16[192,128]{1,0:T(8,128)(2,1)S(1)} %pad_maximum_fusion.3), channel_id=1, source_target_pairs={{0,18},{16,0},{2,16},{18,2},{1,19},{17,1},{3,17},{19,3},{4,22},{20... | collective-permute-start | bytes 147464 | tf_op jit(solution)/shard_map/ppermute | solution.py:22
  5.6 1.8 %collective-permute-start.2 = (bf16[128,128]{1,0:T(8,128)(2,1)S(1)}, bf16[128,128]{1,0:T(8,128)(2,1)S(1)}, u32[]{:S(2)}, u32[]{:S(2)}) collective-permute-start(bf16[128,128]{1,0:T(8,128)(2,1)S(1)} %get-tuple-element.12), channel_id=1, source_target_pairs={{0,2},{16,18},{2,0},{18,16},{1,3},{17,19},{3,1},{19,17},{4,6},{20,... | collective-permute-start | bytes 98312 | tf_op jit(solution)/shard_map/ppermute | solution.py:22
  7.4 0.2 collective-permute-done.1
  7.6 0.0 collective-permute-done
  7.7 3.3 %collective-permute-done.2 = bf16[128,128]{1,0:T(8,128)(2,1)S(1)} collective-permute-done((bf16[128,128]{1,0:T(8,128)(2,1)S(1)}, bf16[128,128]{1,0:T(8,128)(2,1)S(1)}, u32[]{:S(2)}, u32[]{:S(2)}) %collective-permute-start.2) | collective-permute-done | bytes 32800 | tf_op jit(solution)/shard_map/ppermute | solution.py:22
  11.1 0.1 copy.30
  11.2 0.1 reverse_select_fusion
  11.3 0.1 broadcast_in_dim.34
  11.4 0.1 broadcast_in_dim.35
  11.5 0.1 pad_maximum_fusion
  11.6 23.8 %all_to_all.10 = bf16[16,288,128]{2,1,0:T(8,128)(2,1)S(1)} all-to-all(bf16[16,288,128]{2,1,0:T(8,128)(2,1)S(1)} %pad_maximum_fusion), channel_id=1, replica_groups=mesh['x'=4,'zl'=2,'y'=4,'zh'=2,'c'=2] {'x','y'}, dimensions={0} | all-to-all | bytes 2359296 | tf_op jit(solution)/shard_map/all_to_all | solution.py:193
  35.4 0.1 slice_bitcast_fusion
  35.5 0.1 copy.28
  35.6 0.1 pad_maximum_fusion.1.uw_ref
  35.7 0.1 collective-permute-start.7
  35.8 0.6 collective-permute-start.3
  36.5 1.7 %collective-permute-start.6 = (bf16[4,2,128,128]{3,2,1,0:T(8,128)(2,1)S(1)}, bf16[4,2,128,128]{3,2,1,0:T(8,128)(2,1)S(1)}, u32[]{:S(2)}, u32[]{:S(2)}) collective-permute-start(bf16[4,2,128,128]{3,2,1,0:T(8,128)(2,1)S(1)} %bitcast.54), channel_id=1, source_target_pairs={{0,18},{16,0},{2,16},{18,2},{1,19},{17,1},{3,17},{19,3},{4,22},{20... | collective-permute-start | bytes 786440 | tf_op jit(solution)/shard_map/ppermute | solution.py:22
  38.1 0.4 collective-permute-start.5
  38.5 0.9 %collective-permute-start.4 = (bf16[4,2,128,128]{3,2,1,0:T(8,128)(2,1)S(1)}, bf16[4,2,128,128]{3,2,1,0:T(8,128)(2,1)S(1)}, u32[]{:S(2)}, u32[]{:S(2)}) collective-permute-start(bf16[4,2,128,128]{3,2,1,0:T(8,128)(2,1)S(1)} %bitcast.56), channel_id=1, source_target_pairs={{0,16},{16,2},{2,18},{18,0},{1,17},{17,3},{3,19},{19,1},{4,20},{20... | collective-permute-start | bytes 786440 | tf_op jit(solution)/shard_map/ppermute | solution.py:22
  39.4 0.9 %broadcast_select_fusion.1 = (bf16[4,16,8,128]{3,2,0,1:T(8,128)(2,1)S(1)}, bf16[4,16,8,128]{3,2,0,1:T(8,128)(2,1)S(1)}) fusion(bf16[4,16,8,128]{3,2,0,1:T(8,128)(2,1)S(1)} %bitcast.62, bf16[4,16,8,128]{3,2,0,1:T(8,128)(2,1)} %bitcast.49, pred[]{:T(512)S(6)} %eq.15), kind=kLoop, calls=%fused_computation.15 | loop fusion | flops 131072 | bytes 524289 | tf_op jit(solution)/shard_map/jit(_where)/select_n | solution.py:198
  40.3 0.1 copy_bitcast_fusion.2.w_ref
  40.5 5.2 %collective-permute-done.6.l3 = bf16[4,2,128,128]{3,2,1,0:T(8,128)(2,1)S(1)} collective-permute-done((bf16[4,2,128,128]{3,2,1,0:T(8,128)(2,1)S(1)}, bf16[4,2,128,128]{3,2,1,0:T(8,128)(2,1)S(1)}, u32[]{:S(2)}, u32[]{:S(2)}) %collective-permute-start.6) | collective-permute-done | bytes 262176 | tf_op jit(solution)/shard_map/ppermute | solution.py:22
  45.7 3.1 %collective-permute-done.5.l2 = bf16[4,2,128,128]{3,2,1,0:T(8,128)(2,1)S(1)} collective-permute-done((bf16[4,2,128,128]{3,2,1,0:T(8,128)(2,1)S(1)}, bf16[4,2,128,128]{3,2,1,0:T(8,128)(2,1)S(1)}, u32[]{:S(2)}, u32[]{:S(2)}) %collective-permute-start.5) | collective-permute-done | bytes 262176 | tf_op jit(solution)/shard_map/ppermute | solution.py:22
  48.8 4.2 %collective-permute-done.4.l1 = bf16[4,2,128,128]{3,2,1,0:T(8,128)(2,1)S(1)} collective-permute-done((bf16[4,2,128,128]{3,2,1,0:T(8,128)(2,1)S(1)}, bf16[4,2,128,128]{3,2,1,0:T(8,128)(2,1)S(1)}, u32[]{:S(2)}, u32[]{:S(2)}) %collective-permute-start.4) | collective-permute-done | bytes 262176 | tf_op jit(solution)/shard_map/ppermute | solution.py:22
  53.0 4.5 %contract.2 = (f32[2,2,128,128]{3,2,1,0:T(8,128)S(1)}, bf16[1024,128]{1,0:T(8,128)(2,1)S(1)}, bf16[1024,512]{1,0:T(8,128)(2,1)S(1)}) custom-call(s32[1]{0:T(128)} %bitcast.1.zl_ref, s32[1]{0:T(128)} %bitcast.zh_ref, bf16[8,128,128]{2,1,0:T(8,128)(2,1)S(1)} %copy_bitcast_fusion.2.w_ref, bf16[32,128,128]{2,1,0:T(8,128)(2,1)S(1)} %pad_maximum_fusion.1.uw_ref, ...), custom_call_target="tpu_custom_call" | custom-call | flops 4000000000 | bytes 4194304 | tf_op jit(solution)/shard_map/contract/pallas_call | solution.py:119
  57.5 4.1 %contract.3 = f32[2,2,128,128]{3,2,1,0:T(8,128)S(1)} custom-call(s32[1]{0:T(128)} %bitcast.zh_ref, bf16[1024,128]{1,0:T(8,128)(2,1)S(1)} %get-tuple-element.14.wt, bf16[32,128,128]{2,1,0:T(8,128)(2,1)S(1)} %collective-permute-done.7.uw_ref, bf16[1024,512]{1,0:T(8,128)(2,1)S(1)} %get-tuple-element.15.lower, f32[2,2,128,128]{3,2,1,0:T(8,128)S(1)} %get-tuple-element.16.acc_ref), custom_call_target="tpu_custom_call" | custom-call | flops 4000000000 | bytes 4194304 | tf_op jit(solution)/shard_map/contract/pallas_call | solution.py:119
  61.7 15.1 %all_to_all.11 = f32[64,8,128]{2,1,0:T(8,128)S(1)} all-to-all(f32[64,8,128]{2,1,0:T(8,128)S(1)} %bitcast.60), channel_id=1, replica_groups=mesh['x'=4,'zl'=2,'y'=4,'zh'=2,'c'=2] {'x','zl','y','zh'}, dimensions={0} | all-to-all | bytes 524288 | tf_op jit(solution)/shard_map/all_to_all | solution.py:212
  76.8 0.1 reduce_sum.9
  76.9 0.6 copy.21
  (19 shorter events, 0.3 us)
Async XLA Ops:
  1.3 6.3 %collective-permute-start.1 = (bf16[192,128]{1,0:T(8,128)(2,1)S(1)}, bf16[192,128]{1,0:T(8,128)(2,1)S(1)}, u32[]{:S(2)}, u32[]{:S(2)}) collective-permute-start(bf16[192,128]{1,0:T(8,128)(2,1)S(1)} %pad_maximum_fusion.3), channel_id=1, source_target_pairs={{0,16},{16,2},{2,18},{18,0},{1,17},{17,3},{3,19},{19,1},{4,20},{20... | collective-permute-start | bytes 147464 | tf_op jit(solution)/shard_map/ppermute | solution.py:22
  3.4 4.2 %collective-permute-start = (bf16[192,128]{1,0:T(8,128)(2,1)S(1)}, bf16[192,128]{1,0:T(8,128)(2,1)S(1)}, u32[]{:S(2)}, u32[]{:S(2)}) collective-permute-start(bf16[192,128]{1,0:T(8,128)(2,1)S(1)} %pad_maximum_fusion.3), channel_id=1, source_target_pairs={{0,18},{16,0},{2,16},{18,2},{1,19},{17,1},{3,17},{19,3},{4,22},{20... | collective-permute-start | bytes 147464 | tf_op jit(solution)/shard_map/ppermute | solution.py:22
  5.6 5.4 %collective-permute-start.2 = (bf16[128,128]{1,0:T(8,128)(2,1)S(1)}, bf16[128,128]{1,0:T(8,128)(2,1)S(1)}, u32[]{:S(2)}, u32[]{:S(2)}) collective-permute-start(bf16[128,128]{1,0:T(8,128)(2,1)S(1)} %get-tuple-element.12), channel_id=1, source_target_pairs={{0,2},{16,18},{2,0},{18,16},{1,3},{17,19},{3,1},{19,17},{4,6},{20,... | collective-permute-start | bytes 98312 | tf_op jit(solution)/shard_map/ppermute | solution.py:22
  35.7 21.8 %collective-permute-start.7 = (bf16[32,128,128]{2,1,0:T(8,128)(2,1)S(1)}, bf16[32,128,128]{2,1,0:T(8,128)(2,1)S(1)}, u32[]{:S(2)}, u32[]{:S(2)}) collective-permute-start(bf16[32,128,128]{2,1,0:T(8,128)(2,1)S(1)} %pad_maximum_fusion.1.uw_ref), channel_id=1, source_target_pairs={{0,1},{1,0},{2,3},{3,2},{4,5},{5,4},{6,7},{7,6},{8,9},{9,8},{10,11... | collective-permute-start | bytes 3145736 | tf_op jit(solution)/shard_map/ppermute | solution.py:15
  35.8 3.6 %collective-permute-start.3 = (bf16[8,16,4,128]{3,2,0,1:T(4,128)(2,1)S(1)}, bf16[8,16,4,128]{3,2,0,1:T(4,128)(2,1)}, u32[]{:S(2)}, u32[]{:S(2)}) collective-permute-start(bf16[8,16,4,128]{3,2,0,1:T(4,128)(2,1)S(1)} %bitcast.61), channel_id=1, source_target_pairs={{0,1},{1,0},{2,3},{3,2},{4,5},{5,4},{6,7},{7,6},{8,9},{9,8},{10,11... | collective-permute-start | bytes 393224 | tf_op jit(solution)/shard_map/ppermute | solution.py:15
  36.5 9.2 %collective-permute-start.6 = (bf16[4,2,128,128]{3,2,1,0:T(8,128)(2,1)S(1)}, bf16[4,2,128,128]{3,2,1,0:T(8,128)(2,1)S(1)}, u32[]{:S(2)}, u32[]{:S(2)}) collective-permute-start(bf16[4,2,128,128]{3,2,1,0:T(8,128)(2,1)S(1)} %bitcast.54), channel_id=1, source_target_pairs={{0,18},{16,0},{2,16},{18,2},{1,19},{17,1},{3,17},{19,3},{4,22},{20... | collective-permute-start | bytes 786440 | tf_op jit(solution)/shard_map/ppermute | solution.py:22
  38.1 10.7 %collective-permute-start.5 = (bf16[4,2,128,128]{3,2,1,0:T(8,128)(2,1)S(1)}, bf16[4,2,128,128]{3,2,1,0:T(8,128)(2,1)S(1)}, u32[]{:S(2)}, u32[]{:S(2)}) collective-permute-start(bf16[4,2,128,128]{3,2,1,0:T(8,128)(2,1)S(1)} %bitcast.55), channel_id=1, source_target_pairs={{0,2},{16,18},{2,0},{18,16},{1,3},{17,19},{3,1},{19,17},{4,6},{20,... | collective-permute-start | bytes 786440 | tf_op jit(solution)/shard_map/ppermute | solution.py:22
  38.5 14.5 %collective-permute-start.4 = (bf16[4,2,128,128]{3,2,1,0:T(8,128)(2,1)S(1)}, bf16[4,2,128,128]{3,2,1,0:T(8,128)(2,1)S(1)}, u32[]{:S(2)}, u32[]{:S(2)}) collective-permute-start(bf16[4,2,128,128]{3,2,1,0:T(8,128)(2,1)S(1)} %bitcast.56), channel_id=1, source_target_pairs={{0,16},{16,2},{2,18},{18,0},{1,17},{17,3},{3,19},{19,1},{4,20},{20... | collective-permute-start | bytes 786440 | tf_op jit(solution)/shard_map/ppermute | solution.py:22
